TPU v7x, 32 devices: a whole 2x2x4 slice. The times are simulated.
32 devices in a mesh: gz: 16 (over z, y, x), gx: 2 (over core).
Axes of the slice: x: 2, y: 2, z: 4, core: 2. Of those that a mesh axis runs over, the one named last changes fastest.
Arguments:
- b_field: float32 [3, 48, 128, 256], P(None, 'gx', 'gz'), may hold values from -6 to 6
- resist: float32 [48, 128, 256], P('gx', 'gz'), may hold values from 0.05 to 0.8
- ymix: float32 [256, 256], replicated, may hold values from -0.5 to 1.5
- zmix: float32 [128, 128], replicated, may hold values from -0.5 to 1.5
Outputs:
- b_next: float32 [3, 48, 128, 256], P(None, 'gx', 'gz')
- potential: float32 [3, 48, 128, 256], P(None, 'gx', 'gz')
All inputs are finite; a program needn't handle non-finite values.
Results may differ from a plain program's by a relative error of at most 0.000073.
Values sent between devices are 32-bit elements; how exact they have to be, the bound alone decides.
No kernel may reach another device: no remote copies, remote signals or barrier semaphores. Data moves between devices by JAX's collectives and lax.ppermute only.
A program may use at most 64 MiB of HBM per device.

v0:
```python
import jax
import jax.numpy as jnp
from jax import lax
from jax.sharding import PartitionSpec as P

time_step = 0.1
friction = 1.0


def with_halo(block, sides, width):
    for axis, dim in sides:
        count = lax.axis_size(axis)
        forward = [(i, i + 1) for i in range(count - 1)]
        backward = [(target, source) for source, target in forward]
        low = lax.ppermute(
            lax.slice_in_dim(block, block.shape[dim] - width, None, axis=dim), axis, forward
        )
        high = lax.ppermute(lax.slice_in_dim(block, 0, width, axis=dim), axis, backward)
        block = jnp.concatenate([low, block, high], axis=dim)
    return block


def curl_of(padded):
    centre = padded[:, 1:-1, 1:-1, :]
    grad_x = (padded[:, 2:, 1:-1, :] - padded[:, :-2, 1:-1, :]) * 0.5
    grad_z = (padded[:, 1:-1, 2:, :] - padded[:, 1:-1, :-2, :]) * 0.5
    grad_y = (jnp.roll(centre, -1, 3) - jnp.roll(centre, 1, 3)) * 0.5
    return jnp.stack([grad_y[2] - grad_z[1], grad_z[0] - grad_x[2], grad_x[1] - grad_y[0]])


def cross_product(lhs_vec, rhs_vec):
    return jnp.stack(
        [
            lhs_vec[1] * rhs_vec[2] - lhs_vec[2] * rhs_vec[1],
            lhs_vec[2] * rhs_vec[0] - lhs_vec[0] * rhs_vec[2],
            lhs_vec[0] * rhs_vec[1] - lhs_vec[1] * rhs_vec[0],
        ]
    )


def electric(current, field, resist):
    strength = jnp.sum(field * field, axis=0) + 1.0
    velocity = cross_product(current, field) / (friction * strength)
    return resist * current - cross_product(velocity, field)


def on_device(b_field, resist, ymix, zmix):
    cells_z = b_field.shape[2]
    total_z = cells_z * lax.axis_size("gz")
    padded = with_halo(b_field, (("gz", 2), ("gx", 1)), 1)
    current = curl_of(padded)
    efield = electric(current, b_field, resist)
    padded_e = with_halo(efield, (("gz", 2), ("gx", 1)), 1)
    curl_e = curl_of(padded_e)
    stepped = b_field - time_step * curl_e
    along_y = jnp.einsum("cxzi,ij->cxjz", stepped, ymix, precision=lax.Precision.HIGHEST)
    norm_scale = total_z ** (-0.5)
    running = jnp.cumsum(zmix, axis=1)
    slab_ends = running[:, cells_z - 1 :: cells_z][:, :-1]
    lower_flux = jnp.concatenate([jnp.zeros((total_z, 1), jnp.float32), slab_ends], axis=1)
    line_matrix = jnp.concatenate([zmix, lower_flux], axis=1)
    product = jnp.einsum(
        "cxym,mk->cxyk",
        lax.all_to_all(along_y, "gz", split_axis=2, concat_axis=3, tiled=True),
        line_matrix,
        precision=lax.Precision.HIGHEST,
    )
    along_z = product[..., :total_z]
    flux_rows = product[..., total_z:]
    returned, returned_flux = (
        lax.all_to_all(along_z, "gz", split_axis=3, concat_axis=2, tiled=True),
        lax.all_to_all(flux_rows, "gz", split_axis=3, concat_axis=2, tiled=True),
    )
    b_next = jnp.transpose(returned, (0, 1, 3, 2))
    offset = jnp.transpose(returned_flux, (0, 1, 3, 2))
    column = (jnp.cumsum(b_next, axis=2) + offset) * norm_scale
    potential = jnp.stack([column[1], -column[0], column[2]])
    return (b_next, potential)


def solution(mesh):
    in_specs = (P(None, "gx", "gz", None), P("gx", "gz", None), P(), P())
    out_specs = (P(None, "gx", "gz", None), P(None, "gx", "gz", None))
    return jax.shard_map(
        on_device, mesh=mesh, in_specs=in_specs, out_specs=out_specs, check_vma=False
    )
```

profile of v0, /device:TPU:0, one launch (start us, length us, event | category | flops | bytes accessed | tf_op | source)
XLA Modules:
  0.0 133.2 jit_solution(13753559410698514036)
XLA Ops:
  0.7 1.3 copy.57
  2.0 1.3 collective-permute-start
  3.3 5.5 %collective-permute-start.1 = (f32[3,24,1,256]{3,1,2,0:T(8,128)S(1)}, f32[3,24,1,256]{3,1,2,0:T(8,128)S(1)}, u32[]{:S(2)}, u32[]{:S(2)}) collective-permute-start(f32[3,24,1,256]{3,1,2,0:T(8,128)S(1)} %get-tuple-element.33), channel_id=1, source_target_pairs={{0,2},{2,4},{4,6},{6,8},{8,10},{10,12},{12,14},{14,16},{16,18},{18... | collective-permute-start | bytes 221192 | tf_op jit(solution)/shard_map/ppermute | solution.py:15
  8.8 1.1 multiply_reduce_fusion
  10.4 1.5 %collective-permute-done.1 = f32[3,24,1,256]{3,1,2,0:T(8,128)S(1)} collective-permute-done((f32[3,24,1,256]{3,1,2,0:T(8,128)S(1)}, f32[3,24,1,256]{3,1,2,0:T(8,128)S(1)}, u32[]{:S(2)}, u32[]{:S(2)}) %collective-permute-start.1) | collective-permute-done | bytes 73760 | tf_op jit(solution)/shard_map/ppermute | solution.py:15
  12.1 1.3 collective-permute-start.2
  13.4 3.0 %collective-permute-start.3 = (f32[3,1,10,256]{3,1,2,0:T(1,128)S(1)}, f32[3,1,10,256]{3,1,2,0:T(1,128)S(1)}, u32[]{:S(2)}, u32[]{:S(2)}) collective-permute-start(f32[3,1,10,256]{3,1,2,0:T(1,128)S(1)} %get-tuple-element.15), channel_id=1, source_target_pairs={{0,1},{2,3},{4,5},{6,7},{8,9},{10,11},{12,13},{14,15},{16,17},{18,... | collective-permute-start | bytes 92168 | tf_op jit(solution)/shard_map/ppermute | solution.py:15
  18.2 4.4 %collective-permute-start.5 = (f32[3,24,1,256]{3,1,2,0:T(8,128)S(1)}, f32[3,24,1,256]{3,1,2,0:T(8,128)S(1)}, u32[]{:S(2)}, u32[]{:S(2)}) collective-permute-start(f32[3,24,1,256]{3,1,2,0:T(8,128)S(1)} %get-tuple-element.22), channel_id=1, source_target_pairs={{0,2},{2,4},{4,6},{6,8},{8,10},{10,12},{12,14},{14,16},{16,18},{18... | collective-permute-start | bytes 221192 | tf_op jit(solution)/shard_map/ppermute | solution.py:15
  22.6 1.3 collective-permute-start.4
  24.6 5.0 %collective-permute-done.4 = f32[3,24,1,256]{3,1,2,0:T(8,128)S(1)} collective-permute-done((f32[3,24,1,256]{3,1,2,0:T(8,128)S(1)}, f32[3,24,1,256]{3,1,2,0:T(8,128)S(1)}, u32[]{:S(2)}, u32[]{:S(2)}) %collective-permute-start.4) | collective-permute-done | bytes 73760 | tf_op jit(solution)/shard_map/ppermute | solution.py:18
  29.7 1.3 collective-permute-start.6
  31.0 3.0 %collective-permute-start.7 = (f32[3,1,10,256]{3,1,2,0:T(1,128)S(1)}, f32[3,1,10,256]{3,1,2,0:T(1,128)S(1)}, u32[]{:S(2)}, u32[]{:S(2)}) collective-permute-start(f32[3,1,10,256]{3,1,2,0:T(1,128)S(1)} %get-tuple-element.13), channel_id=1, source_target_pairs={{0,1},{2,3},{4,5},{6,7},{8,9},{10,11},{12,13},{14,15},{16,17},{18,... | collective-permute-start | bytes 92168 | tf_op jit(solution)/shard_map/ppermute | solution.py:15
  35.4 1.5 %convolution_bitcast_fusion = f32[3,24,256,8]{2,3,1,0:T(8,128)} fusion(f32[3,24,8,256]{3,1,2,0:T(8,128)S(1)} %fusion.14, f32[256,256]{1,0:T(8,128)S(1)} %copy-done), kind=kOutput, calls=%fused_computation.3 | convolution fusion | flops 452984832 | bytes 1441792 | tf_op jit(solution)/shard_map/cxzi,ij->cxjz/dot_general | solution.py:56
  37.0 2.1 %copy.59 = f32[3,24,256,8]{1,3,0,2:T(8,128)S(1)} copy(f32[3,24,256,8]{2,3,1,0:T(8,128)} %convolution_bitcast_fusion) | data formatting | bytes 1179648 | tf_op jit(solution)/shard_map/cxzi,ij->cxjz/transpose | solution.py:56
  39.1 3.3 %reshape.13 = f32[16,1,9216]{2,1,0:T(1,128)} reshape(f32[256,3,8,24]{3,2,1,0:T(8,128)S(1)} %bitcast.45) | data formatting | bytes 1179648
  42.4 9.8 %all-to-all-start = ((f32[16,1,9216]{2,1,0:T(1,128)}), f32[16,1,9216]{2,1,0:T(1,128)S(1)}, u32[]{:S(2)}, u32[]{:S(2)}) async-start(f32[16,1,9216]{2,1,0:T(1,128)} %reshape.13), calls=%async_computation | async-start | bytes 1179648 | tf_op jit(solution)/shard_map/all_to_all | solution.py:64
  52.5 16.3 %all-to-all-done = f32[16,1,9216]{2,1,0:T(1,128)S(1)} async-done(((f32[16,1,9216]{2,1,0:T(1,128)}), f32[16,1,9216]{2,1,0:T(1,128)S(1)}, u32[]{:S(2)}, u32[]{:S(2)}) %all-to-all-start) | async-done | bytes 589856 | tf_op jit(solution)/shard_map/all_to_all | solution.py:64
  69.3 3.0 %reduce = f32[16,9216]{1,0:T(8,128)} reduce(f32[16,1,9216]{2,1,0:T(1,128)S(1)} %all-to-all-done, f32[]{:T(128)} %broadcast.20), dimensions={1}, to_apply=%all_to_all.37.reduce_sub_computation | reduce | bytes 1179652 | tf_op jit(solution)/shard_map/all_to_all | solution.py:64
  72.3 3.4 %reshape.14 = f32[256,3,8,24]{3,2,1,0:T(8,128)S(1)} reshape(f32[16,9216]{1,0:T(8,128)} %reduce) | data formatting | bytes 1179648
  75.7 5.1 %fusion = f32[3,24,16,144]{3,1,2,0:T(8,128)S(1)} fusion(f32[3,24,16,16,8]{1,4,0,2,3:T(8,128)S(1)} %bitcast.44, f32[128,15]{0,1:T(8,128)S(1)} %bitcast.51, f32[128,128]{0,1:T(8,128)S(1)} %copy.63, f32[144]{0:T(256)S(1)} %pad.4.clone), kind=kOutput, calls=%fused_computation | convolution fusion | flops 254840832 | bytes 1327168 | tf_op jit(solution)/shard_map/cxym,mk->cxyk/dot_general | solution.py:62
  80.8 1.0 copy-done.2
  82.1 0.9 reshape.17
  83.0 4.3 %all-to-all-start.2 = ((f32[16,1,1152]{2,1,0:T(1,128)}), f32[16,1,1152]{2,1,0:T(1,128)S(1)}, u32[]{:S(2)}, u32[]{:S(2)}) async-start(f32[16,1,1152]{2,1,0:T(1,128)} %reshape.17), calls=%async_computation.2 | async-start | bytes 147456 | tf_op jit(solution)/shard_map/all_to_all | solution.py:72
  87.3 1.9 %slice.253 = f32[3,24,16,128]{3,1,2,0:T(8,128)} slice(f32[3,24,16,144]{3,1,2,0:T(8,128)} %copy-done.2), slice={[0:3], [0:24], [0:16], [0:128]} | slice | bytes 1179648 | tf_op jit(solution)/shard_map/slice | solution.py:68
  89.3 2.1 %copy.65 = f32[3,24,16,128]{1,2,0,3:T(8,128)S(1)} copy(f32[3,24,16,128]{3,1,2,0:T(8,128)} %slice.253) | data formatting | bytes 1179648 | tf_op jit(solution)/shard_map/slice | solution.py:68
  91.4 3.3 %reshape.15 = f32[16,1,9216]{2,1,0:T(1,128)} reshape(f32[128,3,16,24]{3,2,1,0:T(8,128)S(1)} %bitcast.46) | data formatting | bytes 1179648
  94.9 6.7 %all-to-all-start.1 = ((f32[16,1,9216]{2,1,0:T(1,128)}), f32[16,1,9216]{2,1,0:T(1,128)S(1)}, u32[]{:S(2)}, u32[]{:S(2)}) async-start(f32[16,1,9216]{2,1,0:T(1,128)} %reshape.15), calls=%async_computation.1 | async-start | bytes 1179648 | tf_op jit(solution)/shard_map/all_to_all | solution.py:71
  103.3 13.4 %all-to-all-done.1 = f32[16,1,9216]{2,1,0:T(1,128)S(1)} async-done(((f32[16,1,9216]{2,1,0:T(1,128)}), f32[16,1,9216]{2,1,0:T(1,128)S(1)}, u32[]{:S(2)}, u32[]{:S(2)}) %all-to-all-start.1) | async-done | bytes 589856 | tf_op jit(solution)/shard_map/all_to_all | solution.py:71
  116.7 3.0 %reduce.1 = f32[16,9216]{1,0:T(8,128)} reduce(f32[16,1,9216]{2,1,0:T(1,128)S(1)} %all-to-all-done.1, f32[]{:T(128)} %broadcast.20), dimensions={1}, to_apply=%all_to_all.41.reduce_sub_computation | reduce | bytes 1179652 | tf_op jit(solution)/shard_map/all_to_all | solution.py:71
  119.6 3.4 %reshape.16 = f32[128,3,16,24]{3,2,1,0:T(8,128)S(1)} reshape(f32[16,9216]{1,0:T(8,128)} %reduce.1) | data formatting | bytes 1179648
  123.0 4.8 %copy.67 = f32[3,24,16,16,8]{3,2,4,1,0:T(8,128)} copy(f32[3,24,16,16,8]{1,3,0,4,2:T(8,128)S(1)} %bitcast.47) | data formatting | bytes 1179648 | tf_op jit(solution)/shard_map/all_to_all | solution.py:71
  127.8 3.9 %all_to_all.44 = f32[3,24,256,8]{2,3,1,0:T(8,128)S(1)} reshape(f32[3,24,16,16,8]{3,2,4,1,0:T(8,128)} %copy.67) | data formatting | bytes 1179648 | tf_op jit(solution)/shard_map/all_to_all | solution.py:71
  (60 shorter events, 8.9 us)
Async XLA Ops:
  0.6 34.8 %copy-start = (f32[256,256]{1,0:T(8,128)S(1)}, f32[256,256]{1,0:T(8,128)}, u32[]{:S(2)}) copy-start(f32[256,256]{1,0:T(8,128)} %param.6) | copy-start | bytes 786436
  0.6 11.2 %copy-start.1 = (f32[3,24,8,256]{3,2,1,0:T(8,128)S(1)}, f32[3,24,8,256]{3,2,1,0:T(8,128)}, u32[]{:S(2)}) copy-start(f32[3,24,8,256]{3,2,1,0:T(8,128)} %param.4) | copy-start | bytes 1769476
  2.0 10.0 %collective-permute-start = (f32[3,24,1,256]{3,1,2,0:T(8,128)S(1)}, f32[3,24,1,256]{3,1,2,0:T(8,128)S(1)}, u32[]{:S(2)}, u32[]{:S(2)}) collective-permute-start(f32[3,24,1,256]{3,1,2,0:T(8,128)S(1)} %get-tuple-element.32), channel_id=1, source_target_pairs={{2,0},{4,2},{6,4},{8,6},{10,8},{12,10},{14,12},{16,14},{18,16},{20... | collective-permute-start | bytes 221192 | tf_op jit(solution)/shard_map/ppermute | solution.py:18
  3.3 8.5 %collective-permute-start.1 = (f32[3,24,1,256]{3,1,2,0:T(8,128)S(1)}, f32[3,24,1,256]{3,1,2,0:T(8,128)S(1)}, u32[]{:S(2)}, u32[]{:S(2)}) collective-permute-start(f32[3,24,1,256]{3,1,2,0:T(8,128)S(1)} %get-tuple-element.33), channel_id=1, source_target_pairs={{0,2},{2,4},{4,6},{6,8},{8,10},{10,12},{12,14},{14,16},{16,18},{18... | collective-permute-start | bytes 221192 | tf_op jit(solution)/shard_map/ppermute | solution.py:15
  10.1 6.7 %copy-start.4 = (f32[24,8,256]{2,1,0:T(8,128)S(1)}, f32[24,8,256]{2,1,0:T(8,128)}, u32[]{:S(2)}) copy-start(f32[24,8,256]{2,1,0:T(8,128)} %param.5) | copy-start | bytes 589828
  12.1 4.8 %collective-permute-start.2 = (f32[3,1,10,256]{3,1,2,0:T(1,128)S(1)}, f32[3,1,10,256]{3,1,2,0:T(1,128)S(1)}, u32[]{:S(2)}, u32[]{:S(2)}) collective-permute-start(f32[3,1,10,256]{3,1,2,0:T(1,128)S(1)} %get-tuple-element.14), channel_id=1, source_target_pairs={{1,0},{3,2},{5,4},{7,6},{9,8},{11,10},{13,12},{15,14},{17,16},{19,... | collective-permute-start | bytes 92168 | tf_op jit(solution)/shard_map/ppermute | solution.py:18
  13.4 3.9 %collective-permute-start.3 = (f32[3,1,10,256]{3,1,2,0:T(1,128)S(1)}, f32[3,1,10,256]{3,1,2,0:T(1,128)S(1)}, u32[]{:S(2)}, u32[]{:S(2)}) collective-permute-start(f32[3,1,10,256]{3,1,2,0:T(1,128)S(1)} %get-tuple-element.15), channel_id=1, source_target_pairs={{0,1},{2,3},{4,5},{6,7},{8,9},{10,11},{12,13},{14,15},{16,17},{18,... | collective-permute-start | bytes 92168 | tf_op jit(solution)/shard_map/ppermute | solution.py:15
  18.2 6.4 %collective-permute-start.5 = (f32[3,24,1,256]{3,1,2,0:T(8,128)S(1)}, f32[3,24,1,256]{3,1,2,0:T(8,128)S(1)}, u32[]{:S(2)}, u32[]{:S(2)}) collective-permute-start(f32[3,24,1,256]{3,1,2,0:T(8,128)S(1)} %get-tuple-element.22), channel_id=1, source_target_pairs={{0,2},{2,4},{4,6},{6,8},{8,10},{10,12},{12,14},{14,16},{16,18},{18... | collective-permute-start | bytes 221192 | tf_op jit(solution)/shard_map/ppermute | solution.py:15
  22.6 7.1 %collective-permute-start.4 = (f32[3,24,1,256]{3,1,2,0:T(8,128)S(1)}, f32[3,24,1,256]{3,1,2,0:T(8,128)S(1)}, u32[]{:S(2)}, u32[]{:S(2)}) collective-permute-start(f32[3,24,1,256]{3,1,2,0:T(8,128)S(1)} %get-tuple-element.23), channel_id=1, source_target_pairs={{2,0},{4,2},{6,4},{8,6},{10,8},{12,10},{14,12},{16,14},{18,16},{20... | collective-permute-start | bytes 221192 | tf_op jit(solution)/shard_map/ppermute | solution.py:18
  29.7 4.6 %collective-permute-start.6 = (f32[3,1,10,256]{3,1,2,0:T(1,128)S(1)}, f32[3,1,10,256]{3,1,2,0:T(1,128)S(1)}, u32[]{:S(2)}, u32[]{:S(2)}) collective-permute-start(f32[3,1,10,256]{3,1,2,0:T(1,128)S(1)} %get-tuple-element.12), channel_id=1, source_target_pairs={{1,0},{3,2},{5,4},{7,6},{9,8},{11,10},{13,12},{15,14},{17,16},{19,... | collective-permute-start | bytes 92168 | tf_op jit(solution)/shard_map/ppermute | solution.py:18
  31.0 3.9 %collective-permute-start.7 = (f32[3,1,10,256]{3,1,2,0:T(1,128)S(1)}, f32[3,1,10,256]{3,1,2,0:T(1,128)S(1)}, u32[]{:S(2)}, u32[]{:S(2)}) collective-permute-start(f32[3,1,10,256]{3,1,2,0:T(1,128)S(1)} %get-tuple-element.13), channel_id=1, source_target_pairs={{0,1},{2,3},{4,5},{6,7},{8,9},{10,11},{12,13},{14,15},{16,17},{18,... | collective-permute-start | bytes 92168 | tf_op jit(solution)/shard_map/ppermute | solution.py:15
  39.0 13.1 %copy-start.5 = (f32[128,128]{1,0:T(8,128)S(1)}, f32[128,128]{1,0:T(8,128)}, u32[]{:S(2)}) copy-start(f32[128,128]{1,0:T(8,128)} %param.7) | copy-start | bytes 196612
  42.4 26.4 %all-to-all-start = ((f32[16,1,9216]{2,1,0:T(1,128)}), f32[16,1,9216]{2,1,0:T(1,128)S(1)}, u32[]{:S(2)}, u32[]{:S(2)}) async-start(f32[16,1,9216]{2,1,0:T(1,128)} %reshape.13), calls=%async_computation | async-start | bytes 1179648 | tf_op jit(solution)/shard_map/all_to_all | solution.py:64
  80.8 1.0 copy-start.2
  83.0 11.9 %all-to-all-start.2 = ((f32[16,1,1152]{2,1,0:T(1,128)}), f32[16,1,1152]{2,1,0:T(1,128)S(1)}, u32[]{:S(2)}, u32[]{:S(2)}) async-start(f32[16,1,1152]{2,1,0:T(1,128)} %reshape.17), calls=%async_computation.2 | async-start | bytes 147456 | tf_op jit(solution)/shard_map/all_to_all | solution.py:72
  94.9 21.8 %all-to-all-start.1 = ((f32[16,1,9216]{2,1,0:T(1,128)}), f32[16,1,9216]{2,1,0:T(1,128)S(1)}, u32[]{:S(2)}, u32[]{:S(2)}) async-start(f32[16,1,9216]{2,1,0:T(1,128)} %reshape.15), calls=%async_computation.1 | async-start | bytes 1179648 | tf_op jit(solution)/shard_map/all_to_all | solution.py:71
  131.7 1.5 %copy-start.3 = (f32[3,24,256,8]{2,3,1,0:T(8,128)}, f32[3,24,256,8]{2,3,1,0:T(8,128)S(1)}, u32[]{:S(2)}) copy-start(f32[3,24,256,8]{2,3,1,0:T(8,128)S(1)} %all_to_all.44) | copy-start | bytes 1769476
where the time goes:
time: 134 us; the launch traced here: 133 us
  starting transfers between devices  41.9 us (31%)
  waiting for transfers between devices  37.9 us (28%)
  local copies, waits for them, and re-layouts  34.3 us (26%)
  other arithmetic  11.3 us (8%)
  matrix products  6.63 us (5%)
    unnamed x23, local copies, waits for them, and re-layouts  17.2 us
    all_to_all x1, waiting for transfers between devices, on_device(): lax.all_to_all(along_y, 'gz', split_axis=2, concat_axis=3, tiled=True)  16.3 us
    ppermute x4, starting transfers between devices, with_halo(): lax.ppermute(lax.slice_in_dim(block, block.shape[dim] - width, None, axis...  16 us
    all_to_all x1, waiting for transfers between devices, on_device(): lax.all_to_all(along_z, 'gz', split_axis=3, concat_axis=2, tiled=True)  13.4 us
    all_to_all x1, starting transfers between devices, on_device(): lax.all_to_all(along_y, 'gz', split_axis=2, concat_axis=3, tiled=True)  9.81 us
    all_to_all x2, local copies, waits for them, and re-layouts, on_device(): lax.all_to_all(along_z, 'gz', split_axis=3, concat_axis=2, tiled=True)  8.66 us
    all_to_all x1, starting transfers between devices, on_device(): lax.all_to_all(along_z, 'gz', split_axis=3, concat_axis=2, tiled=True)  6.68 us
    ppermute x4, starting transfers between devices, with_halo(): lax.ppermute(lax.slice_in_dim(block, 0, width, axis=dim), axis, backward)  5.17 us
  transfers between devices with their start and end apart: 11, of which 8 were waited for; matrix products, arithmetic and copies ran while one was open for 9% of the time, Pallas kernels for 0%

commit v1 on v0

v1 whole, which is shorter than its diff:
```python
import functools
import jax
import jax.numpy as jnp
from jax import lax
from jax.experimental import pallas as pl
from jax.experimental.pallas import tpu as pltpu
from jax.sharding import PartitionSpec as P

time_step = 0.1
friction = 1.0
LANES = 128
SUBLANES = 8
VMEM = pl.BlockSpec(memory_space=pltpu.VMEM)
SMEM = pl.BlockSpec(memory_space=pltpu.SMEM)


def with_halo(block, sides, width):
    for axis, dim in sides:
        count = lax.axis_size(axis)
        forward = [(i, i + 1) for i in range(count - 1)]
        backward = [(target, source) for source, target in forward]
        low = lax.ppermute(
            lax.slice_in_dim(block, block.shape[dim] - width, None, axis=dim), axis, forward
        )
        high = lax.ppermute(lax.slice_in_dim(block, 0, width, axis=dim), axis, backward)
        block = jnp.concatenate([low, block, high], axis=dim)
    return block


def curl_of(padded):
    centre = padded[:, 1:-1, 1:-1, :]
    grad_x = (padded[:, 2:, 1:-1, :] - padded[:, :-2, 1:-1, :]) * 0.5
    grad_z = (padded[:, 1:-1, 2:, :] - padded[:, 1:-1, :-2, :]) * 0.5
    grad_y = (jnp.roll(centre, -1, 3) - jnp.roll(centre, 1, 3)) * 0.5
    return jnp.stack([grad_y[2] - grad_z[1], grad_z[0] - grad_x[2], grad_x[1] - grad_y[0]])


def cross_parts(lhs, rhs):
    return (
        lhs[1] * rhs[2] - lhs[2] * rhs[1],
        lhs[2] * rhs[0] - lhs[0] * rhs[2],
        lhs[0] * rhs[1] - lhs[1] * rhs[0],
    )


def electric_parts(current, field, resist):
    strength = field[0] * field[0] + field[1] * field[1] + field[2] * field[2] + 1.0
    inverse = 1.0 / (friction * strength)
    velocity = [part * inverse for part in cross_parts(current, field)]
    pushed = cross_parts(velocity, field)
    return [resist * current[c] - pushed[c] for c in range(3)]


def plain_form(b_field, resist, ymix, zmix):
    cells_z = b_field.shape[2]
    total_z = cells_z * lax.axis_size("gz")
    padded = with_halo(b_field, (("gz", 2), ("gx", 1)), 1)
    efield = jnp.stack(electric_parts(curl_of(padded), b_field, resist))
    curl_e = curl_of(with_halo(efield, (("gz", 2), ("gx", 1)), 1))
    stepped = b_field - time_step * curl_e
    along_y = jnp.einsum("cxzi,ij->cxjz", stepped, ymix, precision=lax.Precision.HIGHEST)
    running = jnp.cumsum(zmix, axis=1)
    slab_ends = running[:, cells_z - 1 :: cells_z][:, :-1]
    lower_flux = jnp.concatenate([jnp.zeros((total_z, 1), jnp.float32), slab_ends], axis=1)
    line_matrix = jnp.concatenate([zmix, lower_flux], axis=1)
    product = jnp.einsum(
        "cxym,mk->cxyk",
        lax.all_to_all(along_y, "gz", split_axis=2, concat_axis=3, tiled=True),
        line_matrix,
        precision=lax.Precision.HIGHEST,
    )
    returned, returned_flux = (
        lax.all_to_all(part, "gz", split_axis=3, concat_axis=2, tiled=True)
        for part in (product[..., :total_z], product[..., total_z:])
    )
    b_next = jnp.transpose(returned, (0, 1, 3, 2))
    offset = jnp.transpose(returned_flux, (0, 1, 3, 2))
    column = (jnp.cumsum(b_next, axis=2) + offset) * total_z ** (-0.5)
    return b_next, jnp.stack([column[1], -column[0], column[2]])


def pack_rows_kernel(b_ref, r_ref, side_ref, gx_ref, up_ref, down_ref):
    cells_x, cells_z = b_ref.shape[1], b_ref.shape[2]
    near = jnp.where(gx_ref[0] == 0, 0, 1)
    up_ref[...] = jnp.zeros_like(up_ref)
    down_ref[...] = jnp.zeros_like(down_ref)
    for out, edge, inner in ((up_ref, cells_z - 1, cells_z - 2), (down_ref, 0, 1)):
        for x in range(cells_x):
            for c in range(3):
                out[pl.ds(c * cells_x + x, 1), :] = b_ref[c, x, pl.ds(edge, 1), :]
            out[pl.ds(3 * cells_x + x, 1), :] = r_ref[x, pl.ds(edge, 1), :]
            for c in range(2):
                out[pl.ds((4 + c) * cells_x + x, 1), :] = b_ref[c, x, pl.ds(inner, 1), :]
        for c in range(3):
            out[pl.ds(6 * cells_x + c, 1), :] = side_ref[2 * c + near, pl.ds(edge, 1), :]


def granule_transpose(tiles, width):
    count = len(tiles)
    index = lax.broadcasted_iota(jnp.int32, tiles[0].shape, 1) // width
    step = count // 2
    while step:
        keep = (index & step) == 0
        moved = list(tiles)
        for i in range(count):
            if i & step:
                continue
            low, high = tiles[i], tiles[i + step]
            moved[i] = jnp.where(keep, low, pltpu.roll(high, step * width, 1))
            moved[i + step] = jnp.where(keep, pltpu.roll(low, LANES - step * width, 1), high)
        tiles = moved
        step //= 2
    return tiles


def advance_kernel(b_ref, r_ref, side_ref, below_ref, above_ref, ymix_ref, gx_ref, out_ref,
                   field, eta, elec, rows, mixed):
    cells_x, cells_z, cells_y = b_ref.shape[1:]
    tall = 2 * cells_z
    first = gx_ref[0] == 0
    near = jnp.where(first, 0, 1)
    near_at = jnp.where(first, cells_x + 2, 1)
    far_at = jnp.where(first, cells_x + 3, 0)
    empty_at = jnp.where(first, 0, cells_x + 2)
    level = lax.broadcasted_iota(jnp.int32, (cells_z, cells_y), 0)
    zero = jnp.zeros((cells_z, cells_y), jnp.float32)

    def beyond(above, above2, below, below2):
        tile = jnp.where(level == 0, above, zero)
        tile = jnp.where(level == cells_z - 1, below, tile)
        if above2 is not None:
            tile = jnp.where(level == 1, above2, tile)
            tile = jnp.where(level == cells_z - 2, below2, tile)
        return tile

    def row(ref, at):
        return ref[pl.ds(at, 1), :]

    def fill(x, carry):
        for c in range(3):
            field[c, x + 2, :cells_z, :] = b_ref[c, x]
            at = c * cells_x + x
            if c < 2:
                at2 = (4 + c) * cells_x + x
                tile = beyond(row(above_ref, at), row(above_ref, at2), row(below_ref, at), row(below_ref, at2))
            else:
                tile = beyond(row(above_ref, at), None, row(below_ref, at), None)
            field[c, x + 2, cells_z:, :] = tile
        eta[x + 1, :cells_z, :] = r_ref[x]
        at = 3 * cells_x + x
        eta[x + 1, cells_z:, :] = beyond(row(above_ref, at), None, row(below_ref, at), None)
        return carry

    lax.fori_loop(0, cells_x, fill, 0)
    for c in range(3):
        field[c, near_at, :cells_z, :] = side_ref[2 * c + near]
        at = 6 * cells_x + c
        field[c, near_at, cells_z:, :] = beyond(row(above_ref, at), None, row(below_ref, at), None)
        field[c, far_at, :cells_z, :] = side_ref[2 * c + 1 - near]
        field[c, far_at, cells_z:, :] = zero
        field[c, empty_at] = jnp.zeros((tall, cells_y), jnp.float32)
        field[c, empty_at + 1] = jnp.zeros((tall, cells_y), jnp.float32)
    eta[near_at - 1, :cells_z, :] = side_ref[6 + near]
    eta[near_at - 1, cells_z:, :] = zero
    eta[jnp.where(first, 0, cells_x + 1)] = jnp.zeros((tall, cells_y), jnp.float32)

    def slope(after, before):
        return (after - before) * 0.5

    def along_z(value):
        return slope(pltpu.roll(value, tall - 1, 0), pltpu.roll(value, 1, 0))

    def along_row(value):
        return slope(pltpu.roll(value, cells_y - 1, 1), pltpu.roll(value, 1, 1))

    def electric_at(x, carry):
        here = [field[c, x + 1] for c in range(3)]
        dx = [None] + [slope(field[c, x + 2], field[c, x]) for c in (1, 2)]
        current = (
            along_row(here[2]) - along_z(here[1]),
            along_z(here[0]) - dx[2],
            dx[1] - along_row(here[0]),
        )
        made = electric_parts(current, here, eta[x])
        for c in range(3):
            elec[c, x] = made[c]
        return carry

    lax.fori_loop(0, cells_x + 2, electric_at, 0)

    def step_at(x, carry):
        here = [elec[c, x + 1] for c in range(3)]
        dx = [None] + [slope(elec[c, x + 2, :cells_z], elec[c, x, :cells_z]) for c in (1, 2)]
        inner = [value[:cells_z] for value in here]
        curl = (
            along_row(inner[2]) - along_z(here[1])[:cells_z],
            along_z(here[0])[:cells_z] - dx[2],
            dx[1] - along_row(inner[0]),
        )
        for c in range(3):
            rows[pl.ds((c * cells_x + x) * cells_z, cells_z), :] = b_ref[c, x] - time_step * curl[c]
        return carry

    lax.fori_loop(0, cells_x, step_at, 0)
    mixed[...] = jnp.dot(
        rows[...], ymix_ref[...], precision=lax.Precision.HIGHEST, preferred_element_type=jnp.float32
    )
    scatter_blocks(mixed, out_ref, cells_z)


def scatter_blocks(mixed, out_ref, cells_z):
    parts = out_ref.shape[0]
    width = mixed.shape[1] // parts
    count = LANES // width
    for group in range(mixed.shape[0] // (cells_z * count)):
        for half in range(mixed.shape[1] // LANES):
            tiles = [
                mixed[(group * count + i) * cells_z : (group * count + i + 1) * cells_z,
                      half * LANES : (half + 1) * LANES]
                for i in range(count)
            ]
            for i, tile in enumerate(granule_transpose(tiles, width)):
                out_ref[half * count + i, group * cells_z : (group + 1) * cells_z, :] = tile


def line_matrix_kernel(zmix_ref, out_ref):
    total = zmix_ref.shape[0]
    parts = out_ref.shape[0] - total
    turned = jnp.transpose(zmix_ref[...])
    slab = lax.broadcasted_iota(jnp.int32, (parts, total), 0) * (total // parts)
    lower = (lax.broadcasted_iota(jnp.int32, (parts, total), 1) < slab).astype(jnp.float32)
    out_ref[:total] = turned
    out_ref[total:] = jnp.dot(
        lower, turned, precision=lax.Precision.HIGHEST, preferred_element_type=jnp.float32
    )


def lines_kernel(cells_z, in_ref, line_ref, out_ref):
    parts, height, _ = in_ref.shape
    groups = height // cells_z
    total = parts * cells_z
    lines = jnp.concatenate(
        [in_ref[:, g * cells_z : (g + 1) * cells_z, :].reshape(total, LANES) for g in range(groups)], axis=1
    )
    product = jnp.dot(
        line_ref[...], lines, precision=lax.Precision.HIGHEST, preferred_element_type=jnp.float32
    )
    for g in range(groups):
        part = product[:, g * LANES : (g + 1) * LANES]
        out_ref[:, g * cells_z : (g + 1) * cells_z, :] = part[:total].reshape(parts, cells_z, LANES)
        for s in range(parts):
            out_ref[s, height + g : height + g + 1, :] = part[total + s : total + s + 1]


def finish_kernel(scale, in_ref, next_ref, pot_ref):
    cells_x, cells_z, cells_y = next_ref.shape[1:]
    parts = in_ref.shape[0]
    width = cells_y // parts
    count = LANES // width
    groups = 3 * cells_x // count
    level = lax.broadcasted_iota(jnp.int32, (cells_z, LANES), 0)
    for g in range(groups):
        c = g * count // cells_x
        for half in range(cells_y // LANES):
            lanes = slice(half * LANES, (half + 1) * LANES)
            tiles, columns = [], []
            for i in range(count):
                part = half * count + i
                tile = in_ref[part, g * cells_z : (g + 1) * cells_z, :]
                total, step = tile, 1
                while step < cells_z:
                    total = total + jnp.where(level >= step, pltpu.roll(total, step, 0), 0.0)
                    step *= 2
                offset = in_ref[part, groups * cells_z + g : groups * cells_z + g + 1, :]
                factor = -scale if c == 0 else scale
                tiles.append(tile)
                columns.append((total + offset) * factor)
            target = (1, 0, 2)[c]
            for i, tile in enumerate(granule_transpose(tiles, width)):
                next_ref[c, g * count + i - c * cells_x, :, lanes] = tile
            for i, tile in enumerate(granule_transpose(columns, width)):
                pot_ref[target, g * count + i - c * cells_x, :, lanes] = tile


def kernel_form(b_field, resist, ymix, zmix):
    _, cells_x, cells_z, cells_y = b_field.shape
    parts = lax.axis_size("gz")
    total_z = cells_z * parts
    f32 = jnp.float32
    gx = lax.axis_index("gx")
    place = gx.astype(jnp.int32).reshape(1)
    start = jnp.where(gx == 0, cells_x - 2, 0)
    edge = lax.dynamic_slice_in_dim(b_field, start, 2, axis=1).reshape(6, cells_z, cells_y)
    edge_r = lax.dynamic_slice_in_dim(resist, start, 2, axis=0)
    side = lax.ppermute(jnp.concatenate([edge, edge_r]), "gx", [(0, 1), (1, 0)])

    packed = -(-(6 * cells_x + 3) // SUBLANES) * SUBLANES
    slab = jax.ShapeDtypeStruct((packed, cells_y), f32)
    up, down = pl.pallas_call(
        pack_rows_kernel,
        out_shape=(slab, slab),
        in_specs=[VMEM, VMEM, VMEM, SMEM],
        out_specs=(VMEM, VMEM),
    )(b_field, resist, side, place)
    below = lax.ppermute(up, "gz", [(i, i + 1) for i in range(parts - 1)])
    above = lax.ppermute(down, "gz", [(i + 1, i) for i in range(parts - 1)])

    groups = 3 * cells_x * cells_y // parts // LANES
    height = groups * cells_z
    sent = pl.pallas_call(
        advance_kernel,
        out_shape=jax.ShapeDtypeStruct((parts, height, LANES), f32),
        in_specs=[VMEM] * 6 + [SMEM],
        out_specs=VMEM,
        scratch_shapes=[
            pltpu.VMEM((3, cells_x + 4, 2 * cells_z, cells_y), f32),
            pltpu.VMEM((cells_x + 2, 2 * cells_z, cells_y), f32),
            pltpu.VMEM((3, cells_x + 2, 2 * cells_z, cells_y), f32),
            pltpu.VMEM((3 * cells_x * cells_z, cells_y), f32),
            pltpu.VMEM((3 * cells_x * cells_z, cells_y), f32),
        ],
    )(b_field, resist, side, below, above, ymix, place)
    line = pl.pallas_call(
        line_matrix_kernel,
        out_shape=jax.ShapeDtypeStruct((total_z + parts, total_z), f32),
        in_specs=[VMEM],
        out_specs=VMEM,
    )(zmix)
    lines = lax.all_to_all(sent, "gz", split_axis=0, concat_axis=0, tiled=True)
    product = pl.pallas_call(
        functools.partial(lines_kernel, cells_z),
        out_shape=jax.ShapeDtypeStruct((parts, height + groups, LANES), f32),
        in_specs=[VMEM, VMEM],
        out_specs=VMEM,
    )(lines, line)
    returned = lax.all_to_all(product, "gz", split_axis=0, concat_axis=0, tiled=True)
    whole = jax.ShapeDtypeStruct(b_field.shape, f32)
    return pl.pallas_call(
        functools.partial(finish_kernel, total_z ** (-0.5)),
        out_shape=(whole, whole),
        in_specs=[VMEM],
        out_specs=(VMEM, VMEM),
    )(returned)


def on_device(b_field, resist, ymix, zmix):
    _, cells_x, cells_z, cells_y = b_field.shape
    parts = lax.axis_size("gz")
    width = cells_y // parts
    fits = (
        lax.axis_size("gx") == 2
        and parts > 1
        and cells_z == SUBLANES
        and cells_x >= 4
        and cells_y % LANES == 0
        and cells_y % parts == 0
        and LANES % width == 0
        and cells_x % (LANES // width) == 0
    )
    return (kernel_form if fits else plain_form)(b_field, resist, ymix, zmix)


def solution(mesh):
    in_specs = (P(None, "gx", "gz", None), P("gx", "gz", None), P(), P())
    out_specs = (P(None, "gx", "gz", None), P(None, "gx", "gz", None))
    return jax.shard_map(
        on_device, mesh=mesh, in_specs=in_specs, out_specs=out_specs, check_vma=False
    )
```

time: 134 us -> 85.3 us (0.64)
  local copies, waits for them, and re-layouts: 34.3 us -> 3.63 us
  starting transfers between devices: 41.9 us -> 13.1 us
  blocking collectives: 0 us -> 23.6 us
  Pallas kernels: 0 us -> 21.1 us
  waiting for transfers between devices: 37.9 us -> 22.7 us
  other arithmetic: 11.3 us -> 0.01 us
  matrix products: 6.63 us -> 0 us
    all_to_all x0 -> x1, blocking collectives: none -> 23.6 us  [kernel_form(): lax.all_to_all(product, 'gz', split_axis=0, concat_axis=0, tiled=True)]
    pallas_call x0 -> x5, Pallas kernels: none -> 21.1 us  [the longest x1 8.13 us: kernel_form(): pl.pallas_call(advance_kernel, out_shape=jax.ShapeDtypeStruct((parts, hei...]
    all_to_all x3 -> x1, waiting for transfers between devices: 30 us -> 14 us  [kernel_form(): lines = lax.all_to_all(sent, 'gz', split_axis=0, concat_axis=0, tiled=True)]
    unnamed x23 -> x8, local copies, waits for them, and re-layouts: 17.2 us -> 2.11 us
    ppermute x8 -> x3, starting transfers between devices: 21.1 us -> 6.58 us  [the longest x1 4.73 us: kernel_form(): below = lax.ppermute(up, 'gz', [(i, i + 1) for i in range(parts - 1)])]
    all_to_all x3 -> x1, starting transfers between devices: 20.8 us -> 6.49 us  [kernel_form(): lines = lax.all_to_all(sent, 'gz', split_axis=0, concat_axis=0, tiled=True)]
    all_to_all x5 -> x0, local copies, waits for them, and re-layouts: 9.54 us -> none  [the longest x2 8.66 us: on_device(): lax.all_to_all(along_z, 'gz', split_axis=3, concat_axis=2, tiled=True)]
    all_to_all x3 -> x0, other arithmetic: 6.72 us -> none  [the longest x1 2.96 us: on_device(): lax.all_to_all(along_z, 'gz', split_axis=3, concat_axis=2, tiled=True)]
  transfers between devices with their start and end apart: 11 -> 4, of which waited for: 8 -> 4; matrix products, arithmetic and copies ran while one was open for 9% -> 0% of each run, Pallas kernels for 0% -> 2%
where the time goes in v1:
time: 85.3 us; the launch traced here: 84.7 us
  blocking collectives  23.6 us (28%)
  waiting for transfers between devices  22.7 us (27%)
  Pallas kernels  21.1 us (25%)
  starting transfers between devices  13.1 us (15%)
  local copies, waits for them, and re-layouts  3.63 us (4%)
    all_to_all x1, blocking collectives, kernel_form(): lax.all_to_all(product, 'gz', split_axis=0, concat_axis=0, tiled=True)  23.6 us
    all_to_all x1, waiting for transfers between devices, kernel_form(): lines = lax.all_to_all(sent, 'gz', split_axis=0, concat_axis=0, tiled=True)  14 us
    pallas_call x1, Pallas kernels, kernel_form(): pl.pallas_call(advance_kernel, out_shape=jax.ShapeDtypeStruct((parts, hei...  8.13 us
    pallas_call x1, Pallas kernels, kernel_form(): pl.pallas_call(functools.partial(finish_kernel, total_z ** (-0.5)), out_s...  6.54 us
    all_to_all x1, starting transfers between devices, kernel_form(): lines = lax.all_to_all(sent, 'gz', split_axis=0, concat_axis=0, tiled=True)  6.49 us
    ppermute x1, waiting for transfers between devices, kernel_form(): above = lax.ppermute(down, 'gz', [(i + 1, i) for i in range(parts - 1)])  5.17 us
    ppermute x1, starting transfers between devices, kernel_form(): below = lax.ppermute(up, 'gz', [(i, i + 1) for i in range(parts - 1)])  4.73 us
    pallas_call x1, Pallas kernels, kernel_form(): pl.pallas_call(functools.partial(lines_kernel, cells_z), out_shape=jax.Sh...  2.63 us
  transfers between devices with their start and end apart: 4, of which 4 were waited for; matrix products, arithmetic and copies ran while one was open for 0% of the time, Pallas kernels for 2%

profile of v1, /device:TPU:0, one launch (start us, length us, event | category | flops | bytes accessed | tf_op | source)
XLA Modules:
  0.0 84.7 jit_solution(3672401611234909743)
XLA Ops:
  0.6 0.7 constant_dynamic-slice_fusion
  1.4 0.8 constant_dynamic-slice_fusion.1
  2.2 0.6 collective-permute-start
  2.7 0.9 %collective-permute-done.side_ref = f32[8,8,256]{2,1,0:T(8,128)S(1)} collective-permute-done((f32[8,8,256]{2,1,0:T(8,128)S(1)}, f32[8,8,256]{2,1,0:T(8,128)S(1)}, u32[]{:S(2)}, u32[]{:S(2)}) %collective-permute-start) | collective-permute-done | bytes 65568 | tf_op jit(solution)/shard_map/ppermute | solution.py:295
  3.6 0.0 copy-start.1
  3.6 0.6 copy-done.1
  4.3 2.1 %shard_map.59 = (f32[152,256]{1,0:T(8,128)}, f32[152,256]{1,0:T(8,128)}) custom-call(f32[3,24,8,256]{3,2,1,0:T(8,128)} %b_ref.3, f32[24,8,256]{2,1,0:T(8,128)} %r_ref.3, f32[8,8,256]{2,1,0:T(8,128)} %copy-done.1, s32[1]{0:T(128)} %bitcast.1.gx_ref), custom_call_target="tpu_custom_call" | custom-call | tf_op jit(solution)/shard_map/pallas_call | solution.py:299
  6.3 4.7 %collective-permute-start.1 = (f32[152,256]{1,0:T(8,128)}, f32[152,256]{1,0:T(8,128)S(1)}, u32[]{:S(2)}, u32[]{:S(2)}) collective-permute-start(f32[152,256]{1,0:T(8,128)} %get-tuple-element.4), channel_id=1, source_target_pairs={{0,2},{2,4},{4,6},{6,8},{8,10},{10,12},{12,14},{14,16},{16,18},{18... | collective-permute-start | bytes 466952 | tf_op jit(solution)/shard_map/ppermute | solution.py:305
  11.1 1.3 %collective-permute-start.2 = (f32[152,256]{1,0:T(8,128)}, f32[152,256]{1,0:T(8,128)S(1)}, u32[]{:S(2)}, u32[]{:S(2)}) collective-permute-start(f32[152,256]{1,0:T(8,128)} %get-tuple-element.5), channel_id=1, source_target_pairs={{2,0},{4,2},{6,4},{8,6},{10,8},{12,10},{14,12},{16,14},{18,16},{20... | collective-permute-start | bytes 466952 | tf_op jit(solution)/shard_map/ppermute | solution.py:306
  12.3 2.6 %collective-permute-done.1.below_ref = f32[152,256]{1,0:T(8,128)S(1)} collective-permute-done((f32[152,256]{1,0:T(8,128)}, f32[152,256]{1,0:T(8,128)S(1)}, u32[]{:S(2)}, u32[]{:S(2)}) %collective-permute-start.1) | collective-permute-done | bytes 155680 | tf_op jit(solution)/shard_map/ppermute | solution.py:305
  14.9 0.0 copy-start.2
  14.9 5.2 %collective-permute-done.2.above_ref = f32[152,256]{1,0:T(8,128)S(1)} collective-permute-done((f32[152,256]{1,0:T(8,128)}, f32[152,256]{1,0:T(8,128)S(1)}, u32[]{:S(2)}, u32[]{:S(2)}) %collective-permute-start.2) | collective-permute-done | bytes 155680 | tf_op jit(solution)/shard_map/ppermute | solution.py:306
  20.1 0.0 copy-done.2
  20.1 0.0 copy-start.3
  20.1 0.7 copy-done.3
  20.8 8.1 %shard_map.60 = f32[16,72,128]{2,1,0:T(8,128)} custom-call(f32[3,24,8,256]{3,2,1,0:T(8,128)} %b_ref.3, f32[24,8,256]{2,1,0:T(8,128)} %r_ref.3, f32[8,8,256]{2,1,0:T(8,128)} %copy-done.1, f32[152,256]{1,0:T(8,128)} %copy-done.2, f32[152,256]{1,0:T(8,128)} %copy-done.3, f32[256,256]{1,0:T(8,128)} %ymix_ref.1, s32[1]{0:T(128)} %bitcast.1.gx_ref), custom_call_target="tpu_custom_call" | custom-call | tf_op jit(solution)/shard_map/pallas_call | solution.py:310
  28.9 6.5 %all-to-all-start = ((f32[16,72,128]{2,1,0:T(8,128)}), f32[16,72,128]{2,1,0:T(8,128)S(1)}, u32[]{:S(2)}, u32[]{:S(2)}) async-start(f32[16,72,128]{2,1,0:T(8,128)} %shard_map.60), calls=%async_computation | async-start | bytes 1179648 | tf_op jit(solution)/shard_map/all_to_all | solution.py:329
  35.4 1.7 %shard_map.61.line_ref = f32[144,128]{1,0:T(8,128)} custom-call(f32[128,128]{1,0:T(8,128)} %zmix_ref.1), custom_call_target="tpu_custom_call" | custom-call | tf_op jit(solution)/shard_map/pallas_call | solution.py:323
  37.1 14.0 %all-to-all-done.in_ref = f32[16,72,128]{2,1,0:T(8,128)S(1)} async-done(((f32[16,72,128]{2,1,0:T(8,128)}), f32[16,72,128]{2,1,0:T(8,128)S(1)}, u32[]{:S(2)}, u32[]{:S(2)}) %all-to-all-start) | async-done | bytes 589856 | tf_op jit(solution)/shard_map/all_to_all | solution.py:329
  51.1 0.0 copy-start
  51.2 0.8 copy-done
  52.0 2.6 %shard_map.62 = f32[16,81,128]{2,1,0:T(8,128)} custom-call(f32[16,72,128]{2,1,0:T(8,128)} %copy-done, f32[144,128]{1,0:T(8,128)} %shard_map.61.line_ref), custom_call_target="tpu_custom_call" | custom-call | tf_op jit(solution)/shard_map/pallas_call | solution.py:330
  54.6 23.6 %all_to_all.10.in_ref = f32[16,81,128]{2,1,0:T(8,128)} all-to-all(f32[16,81,128]{2,1,0:T(8,128)} %shard_map.62), channel_id=1, replica_groups=mesh['gz'=16,'gx'=2] {'gz'}, dimensions={0} | all-to-all | bytes 1327104 | tf_op jit(solution)/shard_map/all_to_all | solution.py:336
  78.2 6.5 %shard_map.63 = (f32[3,24,8,256]{3,2,1,0:T(8,128)}, f32[3,24,8,256]{3,2,1,0:T(8,128)}) custom-call(f32[16,81,128]{2,1,0:T(8,128)} %all_to_all.10.in_ref), custom_call_target="tpu_custom_call" | custom-call | tf_op jit(solution)/shard_map/pallas_call | solution.py:338
  (1 shorter events, 0.0 us)
Async XLA Ops:
  2.2 1.5 %collective-permute-start = (f32[8,8,256]{2,1,0:T(8,128)S(1)}, f32[8,8,256]{2,1,0:T(8,128)S(1)}, u32[]{:S(2)}, u32[]{:S(2)}) collective-permute-start(f32[8,8,256]{2,1,0:T(8,128)S(1)} %pad_maximum_fusion), channel_id=1, source_target_pairs={{0,1},{1,0},{2,3},{3,2},{4,5},{5,4},{6,7},{7,6},{8,9},{9,8},{10,11... | collective-permute-start | bytes 196616 | tf_op jit(solution)/shard_map/ppermute | solution.py:295
  3.6 0.6 copy-start.1
  6.3 8.6 %collective-permute-start.1 = (f32[152,256]{1,0:T(8,128)}, f32[152,256]{1,0:T(8,128)S(1)}, u32[]{:S(2)}, u32[]{:S(2)}) collective-permute-start(f32[152,256]{1,0:T(8,128)} %get-tuple-element.4), channel_id=1, source_target_pairs={{0,2},{2,4},{4,6},{6,8},{8,10},{10,12},{12,14},{14,16},{16,18},{18... | collective-permute-start | bytes 466952 | tf_op jit(solution)/shard_map/ppermute | solution.py:305
  11.1 9.1 %collective-permute-start.2 = (f32[152,256]{1,0:T(8,128)}, f32[152,256]{1,0:T(8,128)S(1)}, u32[]{:S(2)}, u32[]{:S(2)}) collective-permute-start(f32[152,256]{1,0:T(8,128)} %get-tuple-element.5), channel_id=1, source_target_pairs={{2,0},{4,2},{6,4},{8,6},{10,8},{12,10},{14,12},{16,14},{18,16},{20... | collective-permute-start | bytes 466952 | tf_op jit(solution)/shard_map/ppermute | solution.py:306
  14.9 5.2 %copy-start.2 = (f32[152,256]{1,0:T(8,128)}, f32[152,256]{1,0:T(8,128)S(1)}, u32[]{:S(2)}) copy-start(f32[152,256]{1,0:T(8,128)S(1)} %collective-permute-done.1.below_ref) | copy-start | bytes 466948
  20.1 0.7 copy-start.3
  28.9 22.2 %all-to-all-start = ((f32[16,72,128]{2,1,0:T(8,128)}), f32[16,72,128]{2,1,0:T(8,128)S(1)}, u32[]{:S(2)}, u32[]{:S(2)}) async-start(f32[16,72,128]{2,1,0:T(8,128)} %shard_map.60), calls=%async_computation | async-start | bytes 1179648 | tf_op jit(solution)/shard_map/all_to_all | solution.py:329
  51.1 0.8 copy-start

commit v2 on v1

--- a/solution.py
+++ b/solution.py
@@ -10,6 +10,7 @@
 friction = 1.0
 LANES = 128
 SUBLANES = 8
+CHUNKS = 2
 VMEM = pl.BlockSpec(memory_space=pltpu.VMEM)
 SMEM = pl.BlockSpec(memory_space=pltpu.SMEM)
 
@@ -113,8 +114,7 @@
     return tiles
 
 
-def advance_kernel(b_ref, r_ref, side_ref, below_ref, above_ref, ymix_ref, gx_ref, out_ref,
-                   field, eta, elec, rows, mixed):
+def advance_kernel(b_ref, r_ref, side_ref, below_ref, above_ref, gx_ref, rows, field, eta, elec):
     cells_x, cells_z, cells_y = b_ref.shape[1:]
     tall = 2 * cells_z
     first = gx_ref[0] == 0
@@ -202,21 +202,26 @@
         return carry
 
     lax.fori_loop(0, cells_x, step_at, 0)
-    mixed[...] = jnp.dot(
-        rows[...], ymix_ref[...], precision=lax.Precision.HIGHEST, preferred_element_type=jnp.float32
-    )
-    scatter_blocks(mixed, out_ref, cells_z)
-
-
-def scatter_blocks(mixed, out_ref, cells_z):
-    parts = out_ref.shape[0]
-    width = mixed.shape[1] // parts
+
+
+def mix_kernel(cells_z, first, rows_ref, ymix_ref, out_ref):
+    parts, height, _ = out_ref.shape
+    groups = height // cells_z
+    cells_y = rows_ref.shape[1]
+    width = cells_y // parts
     count = LANES // width
-    for group in range(mixed.shape[0] // (cells_z * count)):
-        for half in range(mixed.shape[1] // LANES):
+    each = count * cells_z
+    mixed = jnp.dot(
+        rows_ref[first * each : (first + groups) * each, :],
+        ymix_ref[...],
+        precision=lax.Precision.HIGHEST,
+        preferred_element_type=jnp.float32,
+    )
+    for group in range(groups):
+        for half in range(cells_y // LANES):
+            lanes = slice(half * LANES, (half + 1) * LANES)
             tiles = [
-                mixed[(group * count + i) * cells_z : (group * count + i + 1) * cells_z,
-                      half * LANES : (half + 1) * LANES]
+                mixed[group * each + i * cells_z : group * each + (i + 1) * cells_z, lanes]
                 for i in range(count)
             ]
             for i, tile in enumerate(granule_transpose(tiles, width)):
@@ -252,15 +257,18 @@
             out_ref[s, height + g : height + g + 1, :] = part[total + s : total + s + 1]
 
 
-def finish_kernel(scale, in_ref, next_ref, pot_ref):
-    cells_x, cells_z, cells_y = next_ref.shape[1:]
-    parts = in_ref.shape[0]
+def finish_kernel(scale, cells_z, first, kept, *refs):
+    in_ref = refs[0]
+    next_ref, pot_ref, buffer, sems = refs[1 + kept :]
+    _, cells_x, _, cells_y = next_ref.shape
+    parts, rows, _ = in_ref.shape
+    groups = rows // (cells_z + 1)
     width = cells_y // parts
     count = LANES // width
-    groups = 3 * cells_x // count
     level = lax.broadcasted_iota(jnp.int32, (cells_z, LANES), 0)
+    copies = []
     for g in range(groups):
-        c = g * count // cells_x
+        c, x = divmod((first + g) * count, cells_x)
         for half in range(cells_y // LANES):
             lanes = slice(half * LANES, (half + 1) * LANES)
             tiles, columns = [], []
@@ -275,11 +283,21 @@
                 factor = -scale if c == 0 else scale
                 tiles.append(tile)
                 columns.append((total + offset) * factor)
-            target = (1, 0, 2)[c]
-            for i, tile in enumerate(granule_transpose(tiles, width)):
-                next_ref[c, g * count + i - c * cells_x, :, lanes] = tile
-            for i, tile in enumerate(granule_transpose(columns, width)):
-                pot_ref[target, g * count + i - c * cells_x, :, lanes] = tile
+            for k, made in enumerate((tiles, columns)):
+                for i, tile in enumerate(granule_transpose(made, width)):
+                    buffer[k, g, i, :, lanes] = tile
+        for k, (target, ref) in enumerate(((c, next_ref), ((1, 0, 2)[c], pot_ref))):
+            copy = pltpu.make_async_copy(
+                buffer.at[k, g], ref.at[target, pl.ds(x, count)], sems.at[k, g]
+            )
+            copy.start()
+            copies.append(copy)
+    for copy in copies:
+        copy.wait()
+
+
+def limit(mib):
+    return pltpu.CompilerParams(vmem_limit_bytes=mib * 2**20)
 
 
 def kernel_form(b_field, resist, ymix, zmix):
@@ -301,46 +319,85 @@
         out_shape=(slab, slab),
         in_specs=[VMEM, VMEM, VMEM, SMEM],
         out_specs=(VMEM, VMEM),
+        compiler_params=limit(6),
     )(b_field, resist, side, place)
     below = lax.ppermute(up, "gz", [(i, i + 1) for i in range(parts - 1)])
     above = lax.ppermute(down, "gz", [(i + 1, i) for i in range(parts - 1)])
 
-    groups = 3 * cells_x * cells_y // parts // LANES
-    height = groups * cells_z
-    sent = pl.pallas_call(
+    rows = pl.pallas_call(
         advance_kernel,
-        out_shape=jax.ShapeDtypeStruct((parts, height, LANES), f32),
-        in_specs=[VMEM] * 6 + [SMEM],
+        out_shape=jax.ShapeDtypeStruct((3 * cells_x * cells_z, cells_y), f32),
+        in_specs=[VMEM] * 5 + [SMEM],
         out_specs=VMEM,
         scratch_shapes=[
             pltpu.VMEM((3, cells_x + 4, 2 * cells_z, cells_y), f32),
             pltpu.VMEM((cells_x + 2, 2 * cells_z, cells_y), f32),
             pltpu.VMEM((3, cells_x + 2, 2 * cells_z, cells_y), f32),
-            pltpu.VMEM((3 * cells_x * cells_z, cells_y), f32),
-            pltpu.VMEM((3 * cells_x * cells_z, cells_y), f32),
         ],
-    )(b_field, resist, side, below, above, ymix, place)
+        compiler_params=limit(10),
+        cost_estimate=estimate(200.0 * 3 * cells_x * cells_z * cells_y),
+    )(b_field, resist, side, below, above, place)
     line = pl.pallas_call(
         line_matrix_kernel,
         out_shape=jax.ShapeDtypeStruct((total_z + parts, total_z), f32),
         in_specs=[VMEM],
         out_specs=VMEM,
+        compiler_params=limit(4),
     )(zmix)
-    lines = lax.all_to_all(sent, "gz", split_axis=0, concat_axis=0, tiled=True)
-    product = pl.pallas_call(
-        functools.partial(lines_kernel, cells_z),
-        out_shape=jax.ShapeDtypeStruct((parts, height + groups, LANES), f32),
-        in_specs=[VMEM, VMEM],
-        out_specs=VMEM,
-    )(lines, line)
-    returned = lax.all_to_all(product, "gz", split_axis=0, concat_axis=0, tiled=True)
+
+    count = LANES // (cells_y // parts)
+    groups = 3 * cells_x // count
+    chunks = split_groups(groups)
+    lines = []
+    for first, size in chunks:
+        sent = pl.pallas_call(
+            functools.partial(mix_kernel, cells_z, first),
+            out_shape=jax.ShapeDtypeStruct((parts, size * cells_z, LANES), f32),
+            in_specs=[VMEM, VMEM],
+            out_specs=VMEM,
+            compiler_params=limit(6),
+            cost_estimate=estimate(2.0 * size * count * cells_z * cells_y * cells_y),
+        )(rows, ymix)
+        lines.append(lax.all_to_all(sent, "gz", split_axis=0, concat_axis=0, tiled=True))
+    returned = []
+    for (first, size), part in zip(chunks, lines):
+        product = pl.pallas_call(
+            functools.partial(lines_kernel, cells_z),
+            out_shape=jax.ShapeDtypeStruct((parts, size * (cells_z + 1), LANES), f32),
+            in_specs=[VMEM, VMEM],
+            out_specs=VMEM,
+            compiler_params=limit(6),
+            cost_estimate=estimate(2.0 * size * LANES * total_z * (total_z + parts)),
+        )(part, line)
+        returned.append(lax.all_to_all(product, "gz", split_axis=0, concat_axis=0, tiled=True))
     whole = jax.ShapeDtypeStruct(b_field.shape, f32)
-    return pl.pallas_call(
-        functools.partial(finish_kernel, total_z ** (-0.5)),
-        out_shape=(whole, whole),
-        in_specs=[VMEM],
-        out_specs=(VMEM, VMEM),
-    )(returned)
+    hbm = pl.BlockSpec(memory_space=pl.ANY)
+    outs = ()
+    for (first, size), part in zip(chunks, returned):
+        outs = pl.pallas_call(
+            functools.partial(finish_kernel, total_z ** (-0.5), cells_z, first, len(outs)),
+            out_shape=(whole, whole),
+            in_specs=[VMEM] + [hbm] * len(outs),
+            out_specs=(hbm, hbm),
+            scratch_shapes=[
+                pltpu.VMEM((2, size, count, cells_z, cells_y), f32),
+                pltpu.SemaphoreType.DMA((2, size)),
+            ],
+            input_output_aliases={1: 0, 2: 1} if outs else {},
+            compiler_params=limit(6),
+            cost_estimate=estimate(200.0 * size * count * cells_z * cells_y),
+        )(part, *outs)
+    return outs
+
+
+def estimate(flops):
+    return pl.CostEstimate(flops=int(flops), bytes_accessed=0, transcendentals=0)
+
+
+def split_groups(groups):
+    head = groups - groups // CHUNKS * (CHUNKS - 1)
+    sizes = [head] + [groups // CHUNKS] * (CHUNKS - 1)
+    return [(sum(sizes[:i]), size) for i, size in enumerate(sizes)]
 
 
 def on_device(b_field, resist, ymix, zmix):

time: 85.3 us -> 86.7 us (1.016)
  blocking collectives: 23.6 us -> 0 us
  waiting for transfers between devices: 22.7 us -> 43.3 us
  starting transfers between devices: 13.1 us -> 24.1 us
  Pallas kernels: 21.1 us -> 15.4 us
  local copies, waits for them, and re-layouts: 3.63 us -> 2.66 us
    all_to_all x1 -> x0, blocking collectives: 23.6 us -> none  [kernel_form(): lax.all_to_all(product, 'gz', split_axis=0, concat_axis=0, tiled=True)]
    all_to_all x1 -> x4, waiting for transfers between devices: 14 us -> 34.9 us  [the longest x2 18.1 us: kernel_form(): lax.all_to_all(product, 'gz', split_axis=0, concat_axis=0, tiled=True)]
    all_to_all x1 -> x4, starting transfers between devices: 6.49 us -> 17.3 us  [the longest x2 10.2 us: kernel_form(): lax.all_to_all(sent, 'gz', split_axis=0, concat_axis=0, tiled=True)]
    pallas_call x2 -> x5, Pallas kernels: 14.7 us -> 12.6 us  [the longest x1 4.96 us: kernel_form(): pl.pallas_call(advance_kernel, out_shape=jax.ShapeDtypeStruct((3 * cells_...]
    pallas_call x1, Pallas kernels: 2.05 us -> 0.17 us  [kernel_form(): pl.pallas_call(pack_rows_kernel, out_shape=(slab, slab), in_specs=[VMEM,...]
    pallas_call x1, Pallas kernels: 1.73 us -> 0.24 us  [kernel_form(): pl.pallas_call(line_matrix_kernel, out_shape=jax.ShapeDtypeStruct((total_...]
    unnamed x8 -> x10, local copies, waits for them, and re-layouts: 2.11 us -> 1.08 us
    pallas_call x1 -> x2, Pallas kernels: 2.63 us -> 2.35 us  [kernel_form(): pl.pallas_call(functools.partial(lines_kernel, cells_z), out_shape=jax.Sh...]
  transfers between devices with their start and end apart: 4 -> 7, of which waited for: 4 -> 7; matrix products, arithmetic and copies ran while one was open for 0% -> 0% of each run, Pallas kernels for 2% -> 8%
where the time goes in v2:
time: 86.7 us; the launch traced here: 86.1 us
  waiting for transfers between devices  43.3 us (50%)
  starting transfers between devices  24.1 us (28%)
  Pallas kernels  15.4 us (18%)
  local copies, waits for them, and re-layouts  2.66 us (3%)
    all_to_all x2, waiting for transfers between devices, kernel_form(): lax.all_to_all(product, 'gz', split_axis=0, concat_axis=0, tiled=True)  18.1 us
    all_to_all x2, waiting for transfers between devices, kernel_form(): lax.all_to_all(sent, 'gz', split_axis=0, concat_axis=0, tiled=True)  16.8 us
    all_to_all x2, starting transfers between devices, kernel_form(): lax.all_to_all(sent, 'gz', split_axis=0, concat_axis=0, tiled=True)  10.2 us
    all_to_all x2, starting transfers between devices, kernel_form(): lax.all_to_all(product, 'gz', split_axis=0, concat_axis=0, tiled=True)  7.19 us
    ppermute x1, waiting for transfers between devices, kernel_form(): above = lax.ppermute(down, 'gz', [(i + 1, i) for i in range(parts - 1)])  5.28 us
    pallas_call x1, Pallas kernels, kernel_form(): pl.pallas_call(advance_kernel, out_shape=jax.ShapeDtypeStruct((3 * cells_...  4.96 us
    pallas_call x2, Pallas kernels, kernel_form(): pl.pallas_call(functools.partial(finish_kernel, total_z ** (-0.5), cells_...  4.92 us
    ppermute x1, starting transfers between devices, kernel_form(): below = lax.ppermute(up, 'gz', [(i, i + 1) for i in range(parts - 1)])  4.74 us
  transfers between devices with their start and end apart: 7, of which 7 were waited for; matrix products, arithmetic and copies ran while one was open for 0% of the time, Pallas kernels for 8%

profile of v2, /device:TPU:0, one launch (start us, length us, event | category | flops | bytes accessed | tf_op | source)
XLA Modules:
  0.0 86.1 jit_solution(1447723988623008665)
XLA Ops:
  0.6 0.0 copy-start.3
  0.6 0.8 constant_dynamic-slice_fusion
  1.4 0.8 constant_dynamic-slice_fusion.1
  2.2 0.6 collective-permute-start
  2.8 0.9 %collective-permute-done.side_ref = f32[8,8,256]{2,1,0:T(8,128)S(1)} collective-permute-done((f32[8,8,256]{2,1,0:T(8,128)S(1)}, f32[8,8,256]{2,1,0:T(8,128)S(1)}, u32[]{:S(2)}, u32[]{:S(2)}) %collective-permute-start) | collective-permute-done | bytes 65568 | tf_op jit(solution)/shard_map/ppermute | solution.py:313
  3.7 0.0 copy-done.3
  3.7 1.1 %copy-done = f32[3,24,8,256]{3,2,1,0:T(8,128)S(1)} copy-done((f32[3,24,8,256]{3,2,1,0:T(8,128)S(1)}, f32[3,24,8,256]{3,2,1,0:T(8,128)}, u32[]{:S(2)}) %copy-start) | copy-done | bytes 589848
  4.8 0.2 shard_map.59
  4.9 4.7 %collective-permute-start.1 = (f32[152,256]{1,0:T(8,128)S(1)}, f32[152,256]{1,0:T(8,128)S(1)}, u32[]{:S(2)}, u32[]{:S(2)}) collective-permute-start(f32[152,256]{1,0:T(8,128)S(1)} %get-tuple-element.6), channel_id=1, source_target_pairs={{0,2},{2,4},{4,6},{6,8},{8,10},{10,12},{12,14},{14,16},{16,18},{18... | collective-permute-start | bytes 466952 | tf_op jit(solution)/shard_map/ppermute | solution.py:324
  9.7 0.0 copy-start.2
  9.7 1.4 %collective-permute-start.2 = (f32[152,256]{1,0:T(8,128)S(1)}, f32[152,256]{1,0:T(8,128)S(1)}, u32[]{:S(2)}, u32[]{:S(2)}) collective-permute-start(f32[152,256]{1,0:T(8,128)S(1)} %get-tuple-element.7), channel_id=1, source_target_pairs={{2,0},{4,2},{6,4},{8,6},{10,8},{12,10},{14,12},{16,14},{18,16},{20... | collective-permute-start | bytes 466952 | tf_op jit(solution)/shard_map/ppermute | solution.py:325
  11.1 2.1 %collective-permute-done.1.below_ref = f32[152,256]{1,0:T(8,128)S(1)} collective-permute-done((f32[152,256]{1,0:T(8,128)S(1)}, f32[152,256]{1,0:T(8,128)S(1)}, u32[]{:S(2)}, u32[]{:S(2)}) %collective-permute-start.1) | collective-permute-done | bytes 155680 | tf_op jit(solution)/shard_map/ppermute | solution.py:324
  13.3 5.3 %collective-permute-done.2.above_ref = f32[152,256]{1,0:T(8,128)S(1)} collective-permute-done((f32[152,256]{1,0:T(8,128)S(1)}, f32[152,256]{1,0:T(8,128)S(1)}, u32[]{:S(2)}, u32[]{:S(2)}) %collective-permute-start.2) | collective-permute-done | bytes 155680 | tf_op jit(solution)/shard_map/ppermute | solution.py:325
  18.5 0.0 copy-done.1
  18.5 5.0 %shard_map.60.rows_ref = f32[576,256]{1,0:T(8,128)S(1)} custom-call(f32[3,24,8,256]{3,2,1,0:T(8,128)S(1)} %copy-done.1, f32[24,8,256]{2,1,0:T(8,128)S(1)} %copy-done.3, f32[8,8,256]{2,1,0:T(8,128)S(1)} %collective-permute-done.side_ref, f32[152,256]{1,0:T(8,128)S(1)} %collective-permute-done.1.below_ref, f32[152,256]{1,0:T(8,128)S(1)} %collective-permute-done.2.above_ref, ...), custom_call_target="tpu_custom_call" | custom-call | flops 29491200 | tf_op jit(solution)/shard_map/pallas_call | solution.py:327
  23.5 0.0 copy-done.2
  23.5 1.4 %shard_map.64 = f32[16,40,128]{2,1,0:T(8,128)} custom-call(f32[576,256]{1,0:T(8,128)S(1)} %shard_map.60.rows_ref, f32[256,256]{1,0:T(8,128)S(1)} %copy-done.2), custom_call_target="tpu_custom_call" | custom-call | flops 41943040 | tf_op jit(solution)/shard_map/pallas_call | solution.py:353
  24.9 6.6 %all-to-all-start.2 = ((f32[16,40,128]{2,1,0:T(8,128)}), f32[16,40,128]{2,1,0:T(8,128)S(1)}, u32[]{:S(2)}, u32[]{:S(2)}) async-start(f32[16,40,128]{2,1,0:T(8,128)} %shard_map.64), calls=%async_computation.2 | async-start | bytes 655360 | tf_op jit(solution)/shard_map/all_to_all | solution.py:361
  31.6 1.3 %shard_map.61 = f32[16,32,128]{2,1,0:T(8,128)} custom-call(f32[576,256]{1,0:T(8,128)S(1)} %shard_map.60.rows_ref, f32[256,256]{1,0:T(8,128)S(1)} %copy-done.2), custom_call_target="tpu_custom_call" | custom-call | flops 33554432 | tf_op jit(solution)/shard_map/pallas_call | solution.py:353
  32.9 9.3 %all-to-all-done.2.in_ref = f32[16,40,128]{2,1,0:T(8,128)S(1)} async-done(((f32[16,40,128]{2,1,0:T(8,128)}), f32[16,40,128]{2,1,0:T(8,128)S(1)}, u32[]{:S(2)}, u32[]{:S(2)}) %all-to-all-start.2) | async-done | bytes 327712 | tf_op jit(solution)/shard_map/all_to_all | solution.py:361
  42.2 3.5 %all-to-all-start = ((f32[16,32,128]{2,1,0:T(8,128)}), f32[16,32,128]{2,1,0:T(8,128)S(1)}, u32[]{:S(2)}, u32[]{:S(2)}) async-start(f32[16,32,128]{2,1,0:T(8,128)} %shard_map.61), calls=%async_computation | async-start | bytes 524288 | tf_op jit(solution)/shard_map/all_to_all | solution.py:361
  45.7 0.0 copy-done.4
  45.7 0.2 shard_map.62.line_ref
  46.0 1.2 %shard_map.65 = f32[16,45,128]{2,1,0:T(8,128)} custom-call(f32[16,40,128]{2,1,0:T(8,128)S(1)} %all-to-all-done.2.in_ref, f32[144,128]{1,0:T(8,128)S(1)} %shard_map.62.line_ref), custom_call_target="tpu_custom_call" | custom-call | flops 23592960 | tf_op jit(solution)/shard_map/pallas_call | solution.py:364
  47.2 7.5 %all-to-all-done.in_ref = f32[16,32,128]{2,1,0:T(8,128)S(1)} async-done(((f32[16,32,128]{2,1,0:T(8,128)}), f32[16,32,128]{2,1,0:T(8,128)S(1)}, u32[]{:S(2)}, u32[]{:S(2)}) %all-to-all-start) | async-done | bytes 262176 | tf_op jit(solution)/shard_map/all_to_all | solution.py:361
  54.7 3.6 %all-to-all-start.3 = ((f32[16,45,128]{2,1,0:T(8,128)}), f32[16,45,128]{2,1,0:T(8,128)S(1)}, u32[]{:S(2)}, u32[]{:S(2)}) async-start(f32[16,45,128]{2,1,0:T(8,128)} %shard_map.65), calls=%async_computation.3 | async-start | bytes 786432 | tf_op jit(solution)/shard_map/all_to_all | solution.py:372
  58.3 1.1 %shard_map.63 = f32[16,36,128]{2,1,0:T(8,128)} custom-call(f32[16,32,128]{2,1,0:T(8,128)S(1)} %all-to-all-done.in_ref, f32[144,128]{1,0:T(8,128)S(1)} %shard_map.62.line_ref), custom_call_target="tpu_custom_call" | custom-call | flops 18874368 | tf_op jit(solution)/shard_map/pallas_call | solution.py:364
  59.4 10.7 %all-to-all-done.3.refs_0_ = f32[16,45,128]{2,1,0:T(8,128)S(1)} async-done(((f32[16,45,128]{2,1,0:T(8,128)}), f32[16,45,128]{2,1,0:T(8,128)S(1)}, u32[]{:S(2)}, u32[]{:S(2)}) %all-to-all-start.3) | async-done | bytes 368672 | tf_op jit(solution)/shard_map/all_to_all | solution.py:372
  70.1 3.6 %all-to-all-start.1 = ((f32[16,36,128]{2,1,0:T(8,128)}), f32[16,36,128]{2,1,0:T(8,128)S(1)}, u32[]{:S(2)}, u32[]{:S(2)}) async-start(f32[16,36,128]{2,1,0:T(8,128)} %shard_map.63), calls=%async_computation.1 | async-start | bytes 655360 | tf_op jit(solution)/shard_map/all_to_all | solution.py:372
  73.7 2.8 %shard_map.66 = (f32[3,24,8,256]{3,2,1,0:T(8,128)}, f32[3,24,8,256]{3,2,1,0:T(8,128)}) custom-call(f32[16,45,128]{2,1,0:T(8,128)S(1)} %all-to-all-done.3.refs_0_), custom_call_target="tpu_custom_call" | custom-call | flops 16384000 | tf_op jit(solution)/shard_map/pallas_call | solution.py:377
  76.5 7.4 %all-to-all-done.1.refs_0_ = f32[16,36,128]{2,1,0:T(8,128)S(1)} async-done(((f32[16,36,128]{2,1,0:T(8,128)}), f32[16,36,128]{2,1,0:T(8,128)S(1)}, u32[]{:S(2)}, u32[]{:S(2)}) %all-to-all-start.1) | async-done | bytes 294944 | tf_op jit(solution)/shard_map/all_to_all | solution.py:372
  83.9 2.1 %shard_map.67 = (f32[3,24,8,256]{3,2,1,0:T(8,128)}, f32[3,24,8,256]{3,2,1,0:T(8,128)}) custom-call(f32[16,36,128]{2,1,0:T(8,128)S(1)} %all-to-all-done.1.refs_0_, f32[3,24,8,256]{3,2,1,0:T(8,128)} %get-tuple-element.8.refs_1_, f32[3,24,8,256]{3,2,1,0:T(8,128)} %get-tuple-element.9.refs_2_), custom_call_target="tpu_custom_call", output_to_operand_aliasing={{0}: (1, {}), {1}: (2, {})} | custom-call | flops 13107200 | tf_op jit(solution)/shard_map/pallas_call | solution.py:377
  (4 shorter events, 0.0 us)
Async XLA Ops:
  0.6 3.1 %copy-start.3 = (f32[24,8,256]{2,1,0:T(8,128)S(1)}, f32[24,8,256]{2,1,0:T(8,128)}, u32[]{:S(2)}) copy-start(f32[24,8,256]{2,1,0:T(8,128)} %r_ref.3) | copy-start | bytes 589828
  2.2 1.5 %collective-permute-start = (f32[8,8,256]{2,1,0:T(8,128)S(1)}, f32[8,8,256]{2,1,0:T(8,128)S(1)}, u32[]{:S(2)}, u32[]{:S(2)}) collective-permute-start(f32[8,8,256]{2,1,0:T(8,128)S(1)} %pad_maximum_fusion), channel_id=1, source_target_pairs={{0,1},{1,0},{2,3},{3,2},{4,5},{5,4},{6,7},{7,6},{8,9},{9,8},{10,11... | collective-permute-start | bytes 196616 | tf_op jit(solution)/shard_map/ppermute | solution.py:313
  3.7 1.1 %copy-start = (f32[3,24,8,256]{3,2,1,0:T(8,128)S(1)}, f32[3,24,8,256]{3,2,1,0:T(8,128)}, u32[]{:S(2)}) copy-start(f32[3,24,8,256]{3,2,1,0:T(8,128)} %b_ref.3) | copy-start | bytes 1769476
  4.8 13.8 %copy-start.1 = (f32[3,24,8,256]{3,2,1,0:T(8,128)S(1)}, f32[3,24,8,256]{3,2,1,0:T(8,128)}, u32[]{:S(2)}) copy-start(f32[3,24,8,256]{3,2,1,0:T(8,128)} %b_ref.3) | copy-start | bytes 1769476
  4.9 8.3 %collective-permute-start.1 = (f32[152,256]{1,0:T(8,128)S(1)}, f32[152,256]{1,0:T(8,128)S(1)}, u32[]{:S(2)}, u32[]{:S(2)}) collective-permute-start(f32[152,256]{1,0:T(8,128)S(1)} %get-tuple-element.6), channel_id=1, source_target_pairs={{0,2},{2,4},{4,6},{6,8},{8,10},{10,12},{12,14},{14,16},{16,18},{18... | collective-permute-start | bytes 466952 | tf_op jit(solution)/shard_map/ppermute | solution.py:324
  9.7 13.8 %copy-start.2 = (f32[256,256]{1,0:T(8,128)S(1)}, f32[256,256]{1,0:T(8,128)}, u32[]{:S(2)}) copy-start(f32[256,256]{1,0:T(8,128)} %ymix_ref.3) | copy-start | bytes 786436
  9.7 8.8 %collective-permute-start.2 = (f32[152,256]{1,0:T(8,128)S(1)}, f32[152,256]{1,0:T(8,128)S(1)}, u32[]{:S(2)}, u32[]{:S(2)}) collective-permute-start(f32[152,256]{1,0:T(8,128)S(1)} %get-tuple-element.7), channel_id=1, source_target_pairs={{2,0},{4,2},{6,4},{8,6},{10,8},{12,10},{14,12},{16,14},{18,16},{20... | collective-permute-start | bytes 466952 | tf_op jit(solution)/shard_map/ppermute | solution.py:325
  24.9 17.2 %all-to-all-start.2 = ((f32[16,40,128]{2,1,0:T(8,128)}), f32[16,40,128]{2,1,0:T(8,128)S(1)}, u32[]{:S(2)}, u32[]{:S(2)}) async-start(f32[16,40,128]{2,1,0:T(8,128)} %shard_map.64), calls=%async_computation.2 | async-start | bytes 655360 | tf_op jit(solution)/shard_map/all_to_all | solution.py:361
  32.9 12.8 %copy-start.4 = (f32[128,128]{1,0:T(8,128)S(1)}, f32[128,128]{1,0:T(8,128)}, u32[]{:S(2)}) copy-start(f32[128,128]{1,0:T(8,128)} %zmix_ref.1) | copy-start | bytes 196612
  42.2 12.6 %all-to-all-start = ((f32[16,32,128]{2,1,0:T(8,128)}), f32[16,32,128]{2,1,0:T(8,128)S(1)}, u32[]{:S(2)}, u32[]{:S(2)}) async-start(f32[16,32,128]{2,1,0:T(8,128)} %shard_map.61), calls=%async_computation | async-start | bytes 524288 | tf_op jit(solution)/shard_map/all_to_all | solution.py:361
  54.7 15.4 %all-to-all-start.3 = ((f32[16,45,128]{2,1,0:T(8,128)}), f32[16,45,128]{2,1,0:T(8,128)S(1)}, u32[]{:S(2)}, u32[]{:S(2)}) async-start(f32[16,45,128]{2,1,0:T(8,128)} %shard_map.65), calls=%async_computation.3 | async-start | bytes 786432 | tf_op jit(solution)/shard_map/all_to_all | solution.py:372
  70.1 13.8 %all-to-all-start.1 = ((f32[16,36,128]{2,1,0:T(8,128)}), f32[16,36,128]{2,1,0:T(8,128)S(1)}, u32[]{:S(2)}, u32[]{:S(2)}) async-start(f32[16,36,128]{2,1,0:T(8,128)} %shard_map.63), calls=%async_computation.1 | async-start | bytes 655360 | tf_op jit(solution)/shard_map/all_to_all | solution.py:372

commit v3 on v2

--- a/solution.py
+++ b/solution.py
@@ -10,7 +10,7 @@
 friction = 1.0
 LANES = 128
 SUBLANES = 8
-CHUNKS = 2
+CHUNKS = 1
 VMEM = pl.BlockSpec(memory_space=pltpu.VMEM)
 SMEM = pl.BlockSpec(memory_space=pltpu.SMEM)
 

time: 86.7 us -> 77.2 us (0.89)
  blocking collectives: 0 us -> 23.2 us
  waiting for transfers between devices: 43.3 us -> 23.6 us
  starting transfers between devices: 24.1 us -> 13.5 us
  Pallas kernels: 15.4 us -> 13.1 us
    all_to_all x0 -> x1, blocking collectives: none -> 23.2 us  [kernel_form(): lax.all_to_all(product, 'gz', split_axis=0, concat_axis=0, tiled=True)]
    all_to_all x2 -> x0, waiting for transfers between devices: 18.1 us -> none  [kernel_form(): lax.all_to_all(product, 'gz', split_axis=0, concat_axis=0, tiled=True)]
    all_to_all x2 -> x0, starting transfers between devices: 7.19 us -> none  [kernel_form(): lax.all_to_all(product, 'gz', split_axis=0, concat_axis=0, tiled=True)]
    all_to_all x2 -> x1, starting transfers between devices: 10.2 us -> 6.77 us  [kernel_form(): lax.all_to_all(sent, 'gz', split_axis=0, concat_axis=0, tiled=True)]
    pallas_call x2 -> x1, Pallas kernels: 2.35 us -> 0.69 us  [kernel_form(): pl.pallas_call(functools.partial(lines_kernel, cells_z), out_shape=jax.Sh...]
    all_to_all x2 -> x1, waiting for transfers between devices: 16.8 us -> 15.3 us  [kernel_form(): lax.all_to_all(sent, 'gz', split_axis=0, concat_axis=0, tiled=True)]
    pallas_call x2 -> x1, Pallas kernels: 2.72 us -> 1.83 us  [kernel_form(): pl.pallas_call(functools.partial(mix_kernel, cells_z, first), out_shape=j...]
    pallas_call x2 -> x1, Pallas kernels: 4.92 us -> 5.25 us  [kernel_form(): pl.pallas_call(functools.partial(finish_kernel, total_z ** (-0.5), cells_...]
  transfers between devices with their start and end apart: 7 -> 4, of which waited for: 7 -> 4; matrix products, arithmetic and copies ran while one was open for 0% -> 0% of each run, Pallas kernels for 8% -> 0%
where the time goes in v3:
time: 77.2 us; the launch traced here: 76.8 us
  waiting for transfers between devices  23.6 us (31%)
  blocking collectives  23.2 us (30%)
  starting transfers between devices  13.5 us (17%)
  Pallas kernels  13.1 us (17%)
  local copies, waits for them, and re-layouts  2.66 us (3%)
    all_to_all x1, blocking collectives, kernel_form(): lax.all_to_all(product, 'gz', split_axis=0, concat_axis=0, tiled=True)  23.2 us
    all_to_all x1, waiting for transfers between devices, kernel_form(): lax.all_to_all(sent, 'gz', split_axis=0, concat_axis=0, tiled=True)  15.3 us
    all_to_all x1, starting transfers between devices, kernel_form(): lax.all_to_all(sent, 'gz', split_axis=0, concat_axis=0, tiled=True)  6.77 us
    ppermute x1, waiting for transfers between devices, kernel_form(): above = lax.ppermute(down, 'gz', [(i + 1, i) for i in range(parts - 1)])  5.28 us
    pallas_call x1, Pallas kernels, kernel_form(): pl.pallas_call(functools.partial(finish_kernel, total_z ** (-0.5), cells_...  5.25 us
    pallas_call x1, Pallas kernels, kernel_form(): pl.pallas_call(advance_kernel, out_shape=jax.ShapeDtypeStruct((3 * cells_...  4.96 us
    ppermute x1, starting transfers between devices, kernel_form(): below = lax.ppermute(up, 'gz', [(i, i + 1) for i in range(parts - 1)])  4.74 us
    ppermute x1, waiting for transfers between devices, kernel_form(): below = lax.ppermute(up, 'gz', [(i, i + 1) for i in range(parts - 1)])  2.13 us
  transfers between devices with their start and end apart: 4, of which 4 were waited for; matrix products, arithmetic and copies ran while one was open for 0% of the time, Pallas kernels for 0%

profile of v3, /device:TPU:0, one launch (start us, length us, event | category | flops | bytes accessed | tf_op | source)
XLA Modules:
  0.0 76.8 jit_solution(4246592130274525096)
XLA Ops:
  0.6 0.0 copy-start.2
  0.6 0.8 %constant_dynamic-slice_fusion = f32[2,8,256]{2,1,0:T(8,128)S(1)} fusion(f32[24,8,256]{2,1,0:T(8,128)} %r_ref.3, s32[]{:T(128)S(6)} %select_n.6), kind=kLoop, calls=%fused_computation.1 | loop fusion | bytes 32772 | tf_op jit(solution)/shard_map/dynamic_slice | solution.py:312
  1.4 0.8 %constant_dynamic-slice_fusion.1 = f32[3,2,8,256]{3,2,1,0:T(8,128)S(1)} fusion(f32[3,24,8,256]{3,2,1,0:T(8,128)} %b_ref.3, s32[]{:T(128)S(6)} %select_n.6), kind=kLoop, calls=%fused_computation.2 | loop fusion | bytes 98308 | tf_op jit(solution)/shard_map/dynamic_slice | solution.py:311
  2.2 0.6 collective-permute-start
  2.8 0.9 %collective-permute-done.side_ref = f32[8,8,256]{2,1,0:T(8,128)S(1)} collective-permute-done((f32[8,8,256]{2,1,0:T(8,128)S(1)}, f32[8,8,256]{2,1,0:T(8,128)S(1)}, u32[]{:S(2)}, u32[]{:S(2)}) %collective-permute-start) | collective-permute-done | bytes 65568 | tf_op jit(solution)/shard_map/ppermute | solution.py:313
  3.7 0.0 copy-done.2
  3.7 0.0 copy-start
  3.7 1.1 %copy-done = f32[3,24,8,256]{3,2,1,0:T(8,128)S(1)} copy-done((f32[3,24,8,256]{3,2,1,0:T(8,128)S(1)}, f32[3,24,8,256]{3,2,1,0:T(8,128)}, u32[]{:S(2)}) %copy-start) | copy-done | bytes 589848
  4.8 0.0 copy-start.1
  4.8 0.2 shard_map.59
  4.9 4.7 %collective-permute-start.1 = (f32[152,256]{1,0:T(8,128)S(1)}, f32[152,256]{1,0:T(8,128)S(1)}, u32[]{:S(2)}, u32[]{:S(2)}) collective-permute-start(f32[152,256]{1,0:T(8,128)S(1)} %get-tuple-element.4), channel_id=1, source_target_pairs={{0,2},{2,4},{4,6},{6,8},{8,10},{10,12},{12,14},{14,16},{16,18},{18... | collective-permute-start | bytes 466952 | tf_op jit(solution)/shard_map/ppermute | solution.py:324
  9.7 0.0 copy-start.3
  9.7 1.4 %collective-permute-start.2 = (f32[152,256]{1,0:T(8,128)S(1)}, f32[152,256]{1,0:T(8,128)S(1)}, u32[]{:S(2)}, u32[]{:S(2)}) collective-permute-start(f32[152,256]{1,0:T(8,128)S(1)} %get-tuple-element.5), channel_id=1, source_target_pairs={{2,0},{4,2},{6,4},{8,6},{10,8},{12,10},{14,12},{16,14},{18,16},{20... | collective-permute-start | bytes 466952 | tf_op jit(solution)/shard_map/ppermute | solution.py:325
  11.1 2.1 %collective-permute-done.1.below_ref = f32[152,256]{1,0:T(8,128)S(1)} collective-permute-done((f32[152,256]{1,0:T(8,128)S(1)}, f32[152,256]{1,0:T(8,128)S(1)}, u32[]{:S(2)}, u32[]{:S(2)}) %collective-permute-start.1) | collective-permute-done | bytes 155680 | tf_op jit(solution)/shard_map/ppermute | solution.py:324
  13.3 5.3 %collective-permute-done.2.above_ref = f32[152,256]{1,0:T(8,128)S(1)} collective-permute-done((f32[152,256]{1,0:T(8,128)S(1)}, f32[152,256]{1,0:T(8,128)S(1)}, u32[]{:S(2)}, u32[]{:S(2)}) %collective-permute-start.2) | collective-permute-done | bytes 155680 | tf_op jit(solution)/shard_map/ppermute | solution.py:325
  18.5 0.0 copy-done.1
  18.5 5.0 %shard_map.60.rows_ref = f32[576,256]{1,0:T(8,128)S(1)} custom-call(f32[3,24,8,256]{3,2,1,0:T(8,128)S(1)} %copy-done.1, f32[24,8,256]{2,1,0:T(8,128)S(1)} %copy-done.2, f32[8,8,256]{2,1,0:T(8,128)S(1)} %collective-permute-done.side_ref, f32[152,256]{1,0:T(8,128)S(1)} %collective-permute-done.1.below_ref, f32[152,256]{1,0:T(8,128)S(1)} %collective-permute-done.2.above_ref, ...), custom_call_target="tpu_custom_call" | custom-call | flops 29491200 | tf_op jit(solution)/shard_map/pallas_call | solution.py:327
  23.5 0.0 copy-done.3
  23.5 1.8 %shard_map.61 = f32[16,72,128]{2,1,0:T(8,128)} custom-call(f32[576,256]{1,0:T(8,128)S(1)} %shard_map.60.rows_ref, f32[256,256]{1,0:T(8,128)S(1)} %copy-done.3), custom_call_target="tpu_custom_call" | custom-call | flops 75497472 | tf_op jit(solution)/shard_map/pallas_call | solution.py:353
  25.4 0.0 copy-start.4
  25.4 6.8 %all-to-all-start = ((f32[16,72,128]{2,1,0:T(8,128)}), f32[16,72,128]{2,1,0:T(8,128)S(1)}, u32[]{:S(2)}, u32[]{:S(2)}) async-start(f32[16,72,128]{2,1,0:T(8,128)} %shard_map.61), calls=%async_computation | async-start | bytes 1179648 | tf_op jit(solution)/shard_map/all_to_all | solution.py:361
  32.1 0.0 copy-done.4
  32.1 0.2 shard_map.62.line_ref
  32.4 15.3 %all-to-all-done.in_ref = f32[16,72,128]{2,1,0:T(8,128)S(1)} async-done(((f32[16,72,128]{2,1,0:T(8,128)}), f32[16,72,128]{2,1,0:T(8,128)S(1)}, u32[]{:S(2)}, u32[]{:S(2)}) %all-to-all-start) | async-done | bytes 589856 | tf_op jit(solution)/shard_map/all_to_all | solution.py:361
  47.6 0.7 shard_map.63
  48.3 23.2 %all_to_all.10.refs_0_ = f32[16,81,128]{2,1,0:T(8,128)S(1)} all-to-all(f32[16,81,128]{2,1,0:T(8,128)S(1)} %shard_map.63), channel_id=1, replica_groups=mesh['gz'=16,'gx'=2] {'gz'}, dimensions={0} | all-to-all | bytes 1327104 | tf_op jit(solution)/shard_map/all_to_all | solution.py:372
  71.5 5.2 %shard_map.64 = (f32[3,24,8,256]{3,2,1,0:T(8,128)}, f32[3,24,8,256]{3,2,1,0:T(8,128)}) custom-call(f32[16,81,128]{2,1,0:T(8,128)S(1)} %all_to_all.10.refs_0_), custom_call_target="tpu_custom_call" | custom-call | flops 29491200 | tf_op jit(solution)/shard_map/pallas_call | solution.py:377
  (1 shorter events, 0.0 us)
Async XLA Ops:
  0.6 3.1 %copy-start.2 = (f32[24,8,256]{2,1,0:T(8,128)S(1)}, f32[24,8,256]{2,1,0:T(8,128)}, u32[]{:S(2)}) copy-start(f32[24,8,256]{2,1,0:T(8,128)} %r_ref.3) | copy-start | bytes 589828
  2.2 1.5 %collective-permute-start = (f32[8,8,256]{2,1,0:T(8,128)S(1)}, f32[8,8,256]{2,1,0:T(8,128)S(1)}, u32[]{:S(2)}, u32[]{:S(2)}) collective-permute-start(f32[8,8,256]{2,1,0:T(8,128)S(1)} %pad_maximum_fusion), channel_id=1, source_target_pairs={{0,1},{1,0},{2,3},{3,2},{4,5},{5,4},{6,7},{7,6},{8,9},{9,8},{10,11... | collective-permute-start | bytes 196616 | tf_op jit(solution)/shard_map/ppermute | solution.py:313
  3.7 1.1 %copy-start = (f32[3,24,8,256]{3,2,1,0:T(8,128)S(1)}, f32[3,24,8,256]{3,2,1,0:T(8,128)}, u32[]{:S(2)}) copy-start(f32[3,24,8,256]{3,2,1,0:T(8,128)} %b_ref.3) | copy-start | bytes 1769476
  4.8 13.8 %copy-start.1 = (f32[3,24,8,256]{3,2,1,0:T(8,128)S(1)}, f32[3,24,8,256]{3,2,1,0:T(8,128)}, u32[]{:S(2)}) copy-start(f32[3,24,8,256]{3,2,1,0:T(8,128)} %b_ref.3) | copy-start | bytes 1769476
  4.9 8.3 %collective-permute-start.1 = (f32[152,256]{1,0:T(8,128)S(1)}, f32[152,256]{1,0:T(8,128)S(1)}, u32[]{:S(2)}, u32[]{:S(2)}) collective-permute-start(f32[152,256]{1,0:T(8,128)S(1)} %get-tuple-element.4), channel_id=1, source_target_pairs={{0,2},{2,4},{4,6},{6,8},{8,10},{10,12},{12,14},{14,16},{16,18},{18... | collective-permute-start | bytes 466952 | tf_op jit(solution)/shard_map/ppermute | solution.py:324
  9.7 13.8 %copy-start.3 = (f32[256,256]{1,0:T(8,128)S(1)}, f32[256,256]{1,0:T(8,128)}, u32[]{:S(2)}) copy-start(f32[256,256]{1,0:T(8,128)} %ymix_ref.1) | copy-start | bytes 786436
  9.7 8.8 %collective-permute-start.2 = (f32[152,256]{1,0:T(8,128)S(1)}, f32[152,256]{1,0:T(8,128)S(1)}, u32[]{:S(2)}, u32[]{:S(2)}) collective-permute-start(f32[152,256]{1,0:T(8,128)S(1)} %get-tuple-element.5), channel_id=1, source_target_pairs={{2,0},{4,2},{6,4},{8,6},{10,8},{12,10},{14,12},{16,14},{18,16},{20... | collective-permute-start | bytes 466952 | tf_op jit(solution)/shard_map/ppermute | solution.py:325
  25.4 6.8 %copy-start.4 = (f32[128,128]{1,0:T(8,128)S(1)}, f32[128,128]{1,0:T(8,128)}, u32[]{:S(2)}) copy-start(f32[128,128]{1,0:T(8,128)} %zmix_ref.1) | copy-start | bytes 196612
  25.4 22.3 %all-to-all-start = ((f32[16,72,128]{2,1,0:T(8,128)}), f32[16,72,128]{2,1,0:T(8,128)S(1)}, u32[]{:S(2)}, u32[]{:S(2)}) async-start(f32[16,72,128]{2,1,0:T(8,128)} %shard_map.61), calls=%async_computation | async-start | bytes 1179648 | tf_op jit(solution)/shard_map/all_to_all | solution.py:361

commit v4 on v1

--- a/solution.py
+++ b/solution.py
@@ -10,6 +10,7 @@
 friction = 1.0
 LANES = 128
 SUBLANES = 8
+PIECES = 3
 VMEM = pl.BlockSpec(memory_space=pltpu.VMEM)
 SMEM = pl.BlockSpec(memory_space=pltpu.SMEM)
 
@@ -95,26 +96,7 @@
             out[pl.ds(6 * cells_x + c, 1), :] = side_ref[2 * c + near, pl.ds(edge, 1), :]
 
 
-def granule_transpose(tiles, width):
-    count = len(tiles)
-    index = lax.broadcasted_iota(jnp.int32, tiles[0].shape, 1) // width
-    step = count // 2
-    while step:
-        keep = (index & step) == 0
-        moved = list(tiles)
-        for i in range(count):
-            if i & step:
-                continue
-            low, high = tiles[i], tiles[i + step]
-            moved[i] = jnp.where(keep, low, pltpu.roll(high, step * width, 1))
-            moved[i + step] = jnp.where(keep, pltpu.roll(low, LANES - step * width, 1), high)
-        tiles = moved
-        step //= 2
-    return tiles
-
-
-def advance_kernel(b_ref, r_ref, side_ref, below_ref, above_ref, ymix_ref, gx_ref, out_ref,
-                   field, eta, elec, rows, mixed):
+def advance_kernel(b_ref, r_ref, side_ref, below_ref, above_ref, gx_ref, rows, field, eta, elec):
     cells_x, cells_z, cells_y = b_ref.shape[1:]
     tall = 2 * cells_z
     first = gx_ref[0] == 0
@@ -202,25 +184,23 @@
         return carry
 
     lax.fori_loop(0, cells_x, step_at, 0)
-    mixed[...] = jnp.dot(
-        rows[...], ymix_ref[...], precision=lax.Precision.HIGHEST, preferred_element_type=jnp.float32
-    )
-    scatter_blocks(mixed, out_ref, cells_z)
-
-
-def scatter_blocks(mixed, out_ref, cells_z):
-    parts = out_ref.shape[0]
-    width = mixed.shape[1] // parts
-    count = LANES // width
-    for group in range(mixed.shape[0] // (cells_z * count)):
-        for half in range(mixed.shape[1] // LANES):
-            tiles = [
-                mixed[(group * count + i) * cells_z : (group * count + i + 1) * cells_z,
-                      half * LANES : (half + 1) * LANES]
-                for i in range(count)
-            ]
-            for i, tile in enumerate(granule_transpose(tiles, width)):
-                out_ref[half * count + i, group * cells_z : (group + 1) * cells_z, :] = tile
+
+
+def mix_kernel(cells_z, rows_ref, ymix_ref, out_ref):
+    parts, height, _ = out_ref.shape
+    each = height // cells_z
+    halves = rows_ref.shape[1] // LANES
+    mixed = jnp.dot(
+        rows_ref[...],
+        ymix_ref[...],
+        precision=lax.Precision.HIGHEST,
+        preferred_element_type=jnp.float32,
+    )
+    for tile in range(parts * each):
+        (part, at), (line, half) = divmod(tile, each), divmod(tile, halves)
+        out_ref[part, at * cells_z : (at + 1) * cells_z, :] = mixed[
+            line * cells_z : (line + 1) * cells_z, half * LANES : (half + 1) * LANES
+        ]
 
 
 def line_matrix_kernel(zmix_ref, out_ref):
@@ -252,34 +232,40 @@
             out_ref[s, height + g : height + g + 1, :] = part[total + s : total + s + 1]
 
 
-def finish_kernel(scale, in_ref, next_ref, pot_ref):
-    cells_x, cells_z, cells_y = next_ref.shape[1:]
-    parts = in_ref.shape[0]
-    width = cells_y // parts
-    count = LANES // width
-    groups = 3 * cells_x // count
+def finish_kernel(scale, cells_z, in_ref, next_ref, pot_ref, buffer, sems):
+    _, cells_x, _, cells_y = next_ref.shape
+    each = in_ref.shape[1] // (cells_z + 1)
+    halves = cells_y // LANES
+    batch = cells_x // PIECES
     level = lax.broadcasted_iota(jnp.int32, (cells_z, LANES), 0)
-    for g in range(groups):
-        c = g * count // cells_x
-        for half in range(cells_y // LANES):
-            lanes = slice(half * LANES, (half + 1) * LANES)
-            tiles, columns = [], []
-            for i in range(count):
-                part = half * count + i
-                tile = in_ref[part, g * cells_z : (g + 1) * cells_z, :]
+    copies = []
+    for piece in range(3 * PIECES):
+        c, x = divmod(piece * batch, cells_x)
+        factor = -scale if c == 0 else scale
+        for i in range(batch):
+            for half in range(halves):
+                part, at = divmod((piece * batch + i) * halves + half, each)
+                tile = in_ref[part, at * cells_z : (at + 1) * cells_z, :]
                 total, step = tile, 1
                 while step < cells_z:
                     total = total + jnp.where(level >= step, pltpu.roll(total, step, 0), 0.0)
                     step *= 2
-                offset = in_ref[part, groups * cells_z + g : groups * cells_z + g + 1, :]
-                factor = -scale if c == 0 else scale
-                tiles.append(tile)
-                columns.append((total + offset) * factor)
-            target = (1, 0, 2)[c]
-            for i, tile in enumerate(granule_transpose(tiles, width)):
-                next_ref[c, g * count + i - c * cells_x, :, lanes] = tile
-            for i, tile in enumerate(granule_transpose(columns, width)):
-                pot_ref[target, g * count + i - c * cells_x, :, lanes] = tile
+                offset = in_ref[part, each * cells_z + at : each * cells_z + at + 1, :]
+                lanes = slice(half * LANES, (half + 1) * LANES)
+                buffer[0, piece, i, :, lanes] = tile
+                buffer[1, piece, i, :, lanes] = (total + offset) * factor
+        for k, (target, ref) in enumerate(((c, next_ref), ((1, 0, 2)[c], pot_ref))):
+            copy = pltpu.make_async_copy(
+                buffer.at[k, piece], ref.at[target, pl.ds(x, batch)], sems.at[k, piece]
+            )
+            copy.start()
+            copies.append(copy)
+    for copy in copies:
+        copy.wait()
+
+
+def limit(mib):
+    return pltpu.CompilerParams(vmem_limit_bytes=mib * 2**20)
 
 
 def kernel_form(b_field, resist, ymix, zmix):
@@ -301,61 +287,78 @@
         out_shape=(slab, slab),
         in_specs=[VMEM, VMEM, VMEM, SMEM],
         out_specs=(VMEM, VMEM),
+        compiler_params=limit(6),
     )(b_field, resist, side, place)
     below = lax.ppermute(up, "gz", [(i, i + 1) for i in range(parts - 1)])
     above = lax.ppermute(down, "gz", [(i + 1, i) for i in range(parts - 1)])
 
-    groups = 3 * cells_x * cells_y // parts // LANES
-    height = groups * cells_z
-    sent = pl.pallas_call(
+    rows = pl.pallas_call(
         advance_kernel,
-        out_shape=jax.ShapeDtypeStruct((parts, height, LANES), f32),
-        in_specs=[VMEM] * 6 + [SMEM],
+        out_shape=jax.ShapeDtypeStruct((3 * cells_x * cells_z, cells_y), f32),
+        in_specs=[VMEM] * 5 + [SMEM],
         out_specs=VMEM,
         scratch_shapes=[
             pltpu.VMEM((3, cells_x + 4, 2 * cells_z, cells_y), f32),
             pltpu.VMEM((cells_x + 2, 2 * cells_z, cells_y), f32),
             pltpu.VMEM((3, cells_x + 2, 2 * cells_z, cells_y), f32),
-            pltpu.VMEM((3 * cells_x * cells_z, cells_y), f32),
-            pltpu.VMEM((3 * cells_x * cells_z, cells_y), f32),
         ],
-    )(b_field, resist, side, below, above, ymix, place)
+        compiler_params=limit(10),
+        cost_estimate=estimate(200.0 * 3 * cells_x * cells_z * cells_y),
+    )(b_field, resist, side, below, above, place)
     line = pl.pallas_call(
         line_matrix_kernel,
         out_shape=jax.ShapeDtypeStruct((total_z + parts, total_z), f32),
         in_specs=[VMEM],
         out_specs=VMEM,
+        compiler_params=limit(4),
     )(zmix)
+
+    each = 3 * cells_x * (cells_y // LANES) // parts
+    sent = pl.pallas_call(
+        functools.partial(mix_kernel, cells_z),
+        out_shape=jax.ShapeDtypeStruct((parts, each * cells_z, LANES), f32),
+        in_specs=[VMEM, VMEM],
+        out_specs=VMEM,
+        compiler_params=limit(6),
+    )(rows, ymix)
     lines = lax.all_to_all(sent, "gz", split_axis=0, concat_axis=0, tiled=True)
     product = pl.pallas_call(
         functools.partial(lines_kernel, cells_z),
-        out_shape=jax.ShapeDtypeStruct((parts, height + groups, LANES), f32),
+        out_shape=jax.ShapeDtypeStruct((parts, each * (cells_z + 1), LANES), f32),
         in_specs=[VMEM, VMEM],
         out_specs=VMEM,
+        compiler_params=limit(6),
     )(lines, line)
     returned = lax.all_to_all(product, "gz", split_axis=0, concat_axis=0, tiled=True)
     whole = jax.ShapeDtypeStruct(b_field.shape, f32)
+    hbm = pl.BlockSpec(memory_space=pl.ANY)
     return pl.pallas_call(
-        functools.partial(finish_kernel, total_z ** (-0.5)),
+        functools.partial(finish_kernel, total_z ** (-0.5), cells_z),
         out_shape=(whole, whole),
         in_specs=[VMEM],
-        out_specs=(VMEM, VMEM),
+        out_specs=(hbm, hbm),
+        scratch_shapes=[
+            pltpu.VMEM((2, 3 * PIECES, cells_x // PIECES, cells_z, cells_y), f32),
+            pltpu.SemaphoreType.DMA((2, 3 * PIECES)),
+        ],
+        compiler_params=limit(6),
     )(returned)
+
+
+def estimate(flops):
+    return pl.CostEstimate(flops=int(flops), bytes_accessed=0, transcendentals=0)
 
 
 def on_device(b_field, resist, ymix, zmix):
     _, cells_x, cells_z, cells_y = b_field.shape
     parts = lax.axis_size("gz")
-    width = cells_y // parts
     fits = (
         lax.axis_size("gx") == 2
         and parts > 1
         and cells_z == SUBLANES
-        and cells_x >= 4
+        and cells_x % PIECES == 0
         and cells_y % LANES == 0
-        and cells_y % parts == 0
-        and LANES % width == 0
-        and cells_x % (LANES // width) == 0
+        and 3 * cells_x * (cells_y // LANES) % parts == 0
     )
     return (kernel_form if fits else plain_form)(b_field, resist, ymix, zmix)
 

time: 85.3 us -> 72.8 us (0.85)
  Pallas kernels: 21.1 us -> 8.69 us
  local copies, waits for them, and re-layouts: 3.63 us -> 2.66 us
  waiting for transfers between devices: 22.7 us -> 23.6 us
    pallas_call x2 -> x3, Pallas kernels: 14.7 us -> 7.59 us  [the longest x1 4.96 us: kernel_form(): pl.pallas_call(advance_kernel, out_shape=jax.ShapeDtypeStruct((3 * cells_...]
    pallas_call x1, Pallas kernels: 2.63 us -> 0.69 us  [kernel_form(): pl.pallas_call(functools.partial(lines_kernel, cells_z), out_shape=jax.Sh...]
    pallas_call x1, Pallas kernels: 2.05 us -> 0.17 us  [kernel_form(): pl.pallas_call(pack_rows_kernel, out_shape=(slab, slab), in_specs=[VMEM,...]
    pallas_call x1, Pallas kernels: 1.73 us -> 0.24 us  [kernel_form(): pl.pallas_call(line_matrix_kernel, out_shape=jax.ShapeDtypeStruct((total_...]
    all_to_all x1, waiting for transfers between devices: 14 us -> 15.3 us  [kernel_form(): lines = lax.all_to_all(sent, 'gz', split_axis=0, concat_axis=0, tiled=True)]
    unnamed x8 -> x10, local copies, waits for them, and re-layouts: 2.11 us -> 1.08 us
  transfers between devices with their start and end apart: 4 -> 4, of which waited for: 4 -> 4; matrix products, arithmetic and copies ran while one was open for 0% -> 0% of each run, Pallas kernels for 2% -> 0%
where the time goes in v4:
time: 72.8 us; the launch traced here: 72.3 us
  waiting for transfers between devices  23.6 us (32%)
  blocking collectives  23.2 us (32%)
  starting transfers between devices  13.5 us (19%)
  Pallas kernels  8.69 us (12%)
  local copies, waits for them, and re-layouts  2.66 us (4%)
    all_to_all x1, blocking collectives, kernel_form(): lax.all_to_all(product, 'gz', split_axis=0, concat_axis=0, tiled=True)  23.2 us
    all_to_all x1, waiting for transfers between devices, kernel_form(): lines = lax.all_to_all(sent, 'gz', split_axis=0, concat_axis=0, tiled=True)  15.3 us
    all_to_all x1, starting transfers between devices, kernel_form(): lines = lax.all_to_all(sent, 'gz', split_axis=0, concat_axis=0, tiled=True)  6.77 us
    ppermute x1, waiting for transfers between devices, kernel_form(): above = lax.ppermute(down, 'gz', [(i + 1, i) for i in range(parts - 1)])  5.28 us
    pallas_call x1, Pallas kernels, kernel_form(): pl.pallas_call(advance_kernel, out_shape=jax.ShapeDtypeStruct((3 * cells_...  4.96 us
    ppermute x1, starting transfers between devices, kernel_form(): below = lax.ppermute(up, 'gz', [(i, i + 1) for i in range(parts - 1)])  4.74 us
    ppermute x1, waiting for transfers between devices, kernel_form(): below = lax.ppermute(up, 'gz', [(i, i + 1) for i in range(parts - 1)])  2.13 us
  transfers between devices with their start and end apart: 4, of which 4 were waited for; matrix products, arithmetic and copies ran while one was open for 0% of the time, Pallas kernels for 0%

profile of v4, /device:TPU:0, one launch (start us, length us, event | category | flops | bytes accessed | tf_op | source)
XLA Modules:
  0.0 72.3 jit_solution(6659329148123482657)
XLA Ops:
  0.6 0.0 copy-start.2
  0.6 0.8 %constant_dynamic-slice_fusion = f32[2,8,256]{2,1,0:T(8,128)S(1)} fusion(f32[24,8,256]{2,1,0:T(8,128)} %r_ref.3, s32[]{:T(128)S(6)} %select_n.6), kind=kLoop, calls=%fused_computation.1 | loop fusion | bytes 32772 | tf_op jit(solution)/shard_map/dynamic_slice | solution.py:280
  1.4 0.8 %constant_dynamic-slice_fusion.1 = f32[3,2,8,256]{3,2,1,0:T(8,128)S(1)} fusion(f32[3,24,8,256]{3,2,1,0:T(8,128)} %b_ref.3, s32[]{:T(128)S(6)} %select_n.6), kind=kLoop, calls=%fused_computation.2 | loop fusion | bytes 98308 | tf_op jit(solution)/shard_map/dynamic_slice | solution.py:279
  2.2 0.6 collective-permute-start
  2.8 0.9 %collective-permute-done.side_ref = f32[8,8,256]{2,1,0:T(8,128)S(1)} collective-permute-done((f32[8,8,256]{2,1,0:T(8,128)S(1)}, f32[8,8,256]{2,1,0:T(8,128)S(1)}, u32[]{:S(2)}, u32[]{:S(2)}) %collective-permute-start) | collective-permute-done | bytes 65568 | tf_op jit(solution)/shard_map/ppermute | solution.py:281
  3.7 0.0 copy-done.2
  3.7 0.0 copy-start
  3.7 1.1 %copy-done = f32[3,24,8,256]{3,2,1,0:T(8,128)S(1)} copy-done((f32[3,24,8,256]{3,2,1,0:T(8,128)S(1)}, f32[3,24,8,256]{3,2,1,0:T(8,128)}, u32[]{:S(2)}) %copy-start) | copy-done | bytes 589848
  4.8 0.0 copy-start.1
  4.8 0.2 shard_map.59
  4.9 4.7 %collective-permute-start.1 = (f32[152,256]{1,0:T(8,128)S(1)}, f32[152,256]{1,0:T(8,128)S(1)}, u32[]{:S(2)}, u32[]{:S(2)}) collective-permute-start(f32[152,256]{1,0:T(8,128)S(1)} %get-tuple-element.4), channel_id=1, source_target_pairs={{0,2},{2,4},{4,6},{6,8},{8,10},{10,12},{12,14},{14,16},{16,18},{18... | collective-permute-start | bytes 466952 | tf_op jit(solution)/shard_map/ppermute | solution.py:292
  9.7 0.0 copy-start.3
  9.7 1.4 %collective-permute-start.2 = (f32[152,256]{1,0:T(8,128)S(1)}, f32[152,256]{1,0:T(8,128)S(1)}, u32[]{:S(2)}, u32[]{:S(2)}) collective-permute-start(f32[152,256]{1,0:T(8,128)S(1)} %get-tuple-element.5), channel_id=1, source_target_pairs={{2,0},{4,2},{6,4},{8,6},{10,8},{12,10},{14,12},{16,14},{18,16},{20... | collective-permute-start | bytes 466952 | tf_op jit(solution)/shard_map/ppermute | solution.py:293
  11.1 2.1 %collective-permute-done.1.below_ref = f32[152,256]{1,0:T(8,128)S(1)} collective-permute-done((f32[152,256]{1,0:T(8,128)S(1)}, f32[152,256]{1,0:T(8,128)S(1)}, u32[]{:S(2)}, u32[]{:S(2)}) %collective-permute-start.1) | collective-permute-done | bytes 155680 | tf_op jit(solution)/shard_map/ppermute | solution.py:292
  13.3 5.3 %collective-permute-done.2.above_ref = f32[152,256]{1,0:T(8,128)S(1)} collective-permute-done((f32[152,256]{1,0:T(8,128)S(1)}, f32[152,256]{1,0:T(8,128)S(1)}, u32[]{:S(2)}, u32[]{:S(2)}) %collective-permute-start.2) | collective-permute-done | bytes 155680 | tf_op jit(solution)/shard_map/ppermute | solution.py:293
  18.5 0.0 copy-done.1
  18.5 5.0 %shard_map.60.rows_ref = f32[576,256]{1,0:T(8,128)S(1)} custom-call(f32[3,24,8,256]{3,2,1,0:T(8,128)S(1)} %copy-done.1, f32[24,8,256]{2,1,0:T(8,128)S(1)} %copy-done.2, f32[8,8,256]{2,1,0:T(8,128)S(1)} %collective-permute-done.side_ref, f32[152,256]{1,0:T(8,128)S(1)} %collective-permute-done.1.below_ref, f32[152,256]{1,0:T(8,128)S(1)} %collective-permute-done.2.above_ref, ...), custom_call_target="tpu_custom_call" | custom-call | flops 29491200 | tf_op jit(solution)/shard_map/pallas_call | solution.py:295
  23.5 0.0 copy-done.3
  23.5 1.5 %shard_map.61 = f32[16,72,128]{2,1,0:T(8,128)} custom-call(f32[576,256]{1,0:T(8,128)S(1)} %shard_map.60.rows_ref, f32[256,256]{1,0:T(8,128)S(1)} %copy-done.3), custom_call_target="tpu_custom_call" | custom-call | tf_op jit(solution)/shard_map/pallas_call | solution.py:317
  25.0 0.0 copy-start.4
  25.0 6.8 %all-to-all-start = ((f32[16,72,128]{2,1,0:T(8,128)}), f32[16,72,128]{2,1,0:T(8,128)S(1)}, u32[]{:S(2)}, u32[]{:S(2)}) async-start(f32[16,72,128]{2,1,0:T(8,128)} %shard_map.61), calls=%async_computation | async-start | bytes 1179648 | tf_op jit(solution)/shard_map/all_to_all | solution.py:324
  31.8 0.0 copy-done.4
  31.8 0.2 shard_map.62.line_ref
  32.0 15.3 %all-to-all-done.in_ref = f32[16,72,128]{2,1,0:T(8,128)S(1)} async-done(((f32[16,72,128]{2,1,0:T(8,128)}), f32[16,72,128]{2,1,0:T(8,128)S(1)}, u32[]{:S(2)}, u32[]{:S(2)}) %all-to-all-start) | async-done | bytes 589856 | tf_op jit(solution)/shard_map/all_to_all | solution.py:324
  47.3 0.7 shard_map.63
  47.9 23.2 %all_to_all.10.in_ref = f32[16,81,128]{2,1,0:T(8,128)S(1)} all-to-all(f32[16,81,128]{2,1,0:T(8,128)S(1)} %shard_map.63), channel_id=1, replica_groups=mesh['gz'=16,'gx'=2] {'gz'}, dimensions={0} | all-to-all | bytes 1327104 | tf_op jit(solution)/shard_map/all_to_all | solution.py:332
  71.2 1.2 %shard_map.64 = (f32[3,24,8,256]{3,2,1,0:T(8,128)}, f32[3,24,8,256]{3,2,1,0:T(8,128)}) custom-call(f32[16,81,128]{2,1,0:T(8,128)S(1)} %all_to_all.10.in_ref), custom_call_target="tpu_custom_call" | custom-call | tf_op jit(solution)/shard_map/pallas_call | solution.py:335
  (1 shorter events, 0.0 us)
Async XLA Ops:
  0.6 3.1 %copy-start.2 = (f32[24,8,256]{2,1,0:T(8,128)S(1)}, f32[24,8,256]{2,1,0:T(8,128)}, u32[]{:S(2)}) copy-start(f32[24,8,256]{2,1,0:T(8,128)} %r_ref.3) | copy-start | bytes 589828
  2.2 1.5 %collective-permute-start = (f32[8,8,256]{2,1,0:T(8,128)S(1)}, f32[8,8,256]{2,1,0:T(8,128)S(1)}, u32[]{:S(2)}, u32[]{:S(2)}) collective-permute-start(f32[8,8,256]{2,1,0:T(8,128)S(1)} %pad_maximum_fusion), channel_id=1, source_target_pairs={{0,1},{1,0},{2,3},{3,2},{4,5},{5,4},{6,7},{7,6},{8,9},{9,8},{10,11... | collective-permute-start | bytes 196616 | tf_op jit(solution)/shard_map/ppermute | solution.py:281
  3.7 1.1 %copy-start = (f32[3,24,8,256]{3,2,1,0:T(8,128)S(1)}, f32[3,24,8,256]{3,2,1,0:T(8,128)}, u32[]{:S(2)}) copy-start(f32[3,24,8,256]{3,2,1,0:T(8,128)} %b_ref.3) | copy-start | bytes 1769476
  4.8 13.8 %copy-start.1 = (f32[3,24,8,256]{3,2,1,0:T(8,128)S(1)}, f32[3,24,8,256]{3,2,1,0:T(8,128)}, u32[]{:S(2)}) copy-start(f32[3,24,8,256]{3,2,1,0:T(8,128)} %b_ref.3) | copy-start | bytes 1769476
  4.9 8.3 %collective-permute-start.1 = (f32[152,256]{1,0:T(8,128)S(1)}, f32[152,256]{1,0:T(8,128)S(1)}, u32[]{:S(2)}, u32[]{:S(2)}) collective-permute-start(f32[152,256]{1,0:T(8,128)S(1)} %get-tuple-element.4), channel_id=1, source_target_pairs={{0,2},{2,4},{4,6},{6,8},{8,10},{10,12},{12,14},{14,16},{16,18},{18... | collective-permute-start | bytes 466952 | tf_op jit(solution)/shard_map/ppermute | solution.py:292
  9.7 13.8 %copy-start.3 = (f32[256,256]{1,0:T(8,128)S(1)}, f32[256,256]{1,0:T(8,128)}, u32[]{:S(2)}) copy-start(f32[256,256]{1,0:T(8,128)} %ymix_ref.1) | copy-start | bytes 786436
  9.7 8.8 %collective-permute-start.2 = (f32[152,256]{1,0:T(8,128)S(1)}, f32[152,256]{1,0:T(8,128)S(1)}, u32[]{:S(2)}, u32[]{:S(2)}) collective-permute-start(f32[152,256]{1,0:T(8,128)S(1)} %get-tuple-element.5), channel_id=1, source_target_pairs={{2,0},{4,2},{6,4},{8,6},{10,8},{12,10},{14,12},{16,14},{18,16},{20... | collective-permute-start | bytes 466952 | tf_op jit(solution)/shard_map/ppermute | solution.py:293
  25.0 6.8 %copy-start.4 = (f32[128,128]{1,0:T(8,128)S(1)}, f32[128,128]{1,0:T(8,128)}, u32[]{:S(2)}) copy-start(f32[128,128]{1,0:T(8,128)} %zmix_ref.1) | copy-start | bytes 196612
  25.0 22.3 %all-to-all-start = ((f32[16,72,128]{2,1,0:T(8,128)}), f32[16,72,128]{2,1,0:T(8,128)S(1)}, u32[]{:S(2)}, u32[]{:S(2)}) async-start(f32[16,72,128]{2,1,0:T(8,128)} %shard_map.61), calls=%async_computation | async-start | bytes 1179648 | tf_op jit(solution)/shard_map/all_to_all | solution.py:324

commit v5 on v0

v5 whole, which is shorter than its diff:
```python
import functools
import jax
import jax.numpy as jnp
from jax import lax
from jax.experimental import pallas as pl
from jax.experimental.pallas import tpu as pltpu
from jax.sharding import PartitionSpec as P

time_step = 0.1
friction = 1.0
LANES = 128
SUBLANES = 8
PIECES = 3
BATCH = 6
VMEM = pl.BlockSpec(memory_space=pltpu.VMEM)
SMEM = pl.BlockSpec(memory_space=pltpu.SMEM)


def with_halo(block, sides, width):
    for axis, dim in sides:
        count = lax.axis_size(axis)
        forward = [(i, i + 1) for i in range(count - 1)]
        backward = [(target, source) for source, target in forward]
        low = lax.ppermute(
            lax.slice_in_dim(block, block.shape[dim] - width, None, axis=dim), axis, forward
        )
        high = lax.ppermute(lax.slice_in_dim(block, 0, width, axis=dim), axis, backward)
        block = jnp.concatenate([low, block, high], axis=dim)
    return block


def curl_of(padded):
    centre = padded[:, 1:-1, 1:-1, :]
    grad_x = (padded[:, 2:, 1:-1, :] - padded[:, :-2, 1:-1, :]) * 0.5
    grad_z = (padded[:, 1:-1, 2:, :] - padded[:, 1:-1, :-2, :]) * 0.5
    grad_y = (jnp.roll(centre, -1, 3) - jnp.roll(centre, 1, 3)) * 0.5
    return jnp.stack([grad_y[2] - grad_z[1], grad_z[0] - grad_x[2], grad_x[1] - grad_y[0]])


def cross_parts(lhs, rhs):
    return (
        lhs[1] * rhs[2] - lhs[2] * rhs[1],
        lhs[2] * rhs[0] - lhs[0] * rhs[2],
        lhs[0] * rhs[1] - lhs[1] * rhs[0],
    )


def electric_parts(current, field, resist):
    strength = field[0] * field[0] + field[1] * field[1] + field[2] * field[2] + 1.0
    inverse = 1.0 / (friction * strength)
    velocity = [part * inverse for part in cross_parts(current, field)]
    pushed = cross_parts(velocity, field)
    return [resist * current[c] - pushed[c] for c in range(3)]


def plain_form(b_field, resist, ymix, zmix):
    cells_z = b_field.shape[2]
    total_z = cells_z * lax.axis_size("gz")
    padded = with_halo(b_field, (("gz", 2), ("gx", 1)), 1)
    efield = jnp.stack(electric_parts(curl_of(padded), b_field, resist))
    curl_e = curl_of(with_halo(efield, (("gz", 2), ("gx", 1)), 1))
    stepped = b_field - time_step * curl_e
    along_y = jnp.einsum("cxzi,ij->cxjz", stepped, ymix, precision=lax.Precision.HIGHEST)
    running = jnp.cumsum(zmix, axis=1)
    slab_ends = running[:, cells_z - 1 :: cells_z][:, :-1]
    lower_flux = jnp.concatenate([jnp.zeros((total_z, 1), jnp.float32), slab_ends], axis=1)
    line_matrix = jnp.concatenate([zmix, lower_flux], axis=1)
    product = jnp.einsum(
        "cxym,mk->cxyk",
        lax.all_to_all(along_y, "gz", split_axis=2, concat_axis=3, tiled=True),
        line_matrix,
        precision=lax.Precision.HIGHEST,
    )
    returned, returned_flux = (
        lax.all_to_all(part, "gz", split_axis=3, concat_axis=2, tiled=True)
        for part in (product[..., :total_z], product[..., total_z:])
    )
    b_next = jnp.transpose(returned, (0, 1, 3, 2))
    offset = jnp.transpose(returned_flux, (0, 1, 3, 2))
    column = (jnp.cumsum(b_next, axis=2) + offset) * total_z ** (-0.5)
    return b_next, jnp.stack([column[1], -column[0], column[2]])


def slope(after, before):
    return (after - before) * 0.5


def along_row(value):
    cells_y = value.shape[1]
    return slope(pltpu.roll(value, cells_y - 1, 1), pltpu.roll(value, 1, 1))


def along_z(value, above, below):
    cells_z = value.shape[0]
    level = lax.broadcasted_iota(jnp.int32, value.shape, 0)
    after = jnp.where(level == cells_z - 1, above, pltpu.roll(value, cells_z - 1, 0))
    before = jnp.where(level == 0, below, pltpu.roll(value, 1, 0))
    return slope(after, before)


def over_x(cells_x, body):
    def trip(i, carry):
        for j in range(BATCH):
            body(i * BATCH + j)
        return carry

    lax.fori_loop(0, cells_x // BATCH, trip, 0)


def pack_kernel(b_ref, gx_ref, up_ref, down_ref, side_ref):
    cells_x, cells_z = b_ref.shape[1], b_ref.shape[2]
    edge = jnp.where(gx_ref[0] == 0, cells_x - 1, 0)
    for c in range(2):
        side_ref[c] = b_ref[c + 1, edge]
        for x in range(cells_x):
            at = pl.ds(c * cells_x + x, 1)
            up_ref[at, :] = b_ref[c, x, cells_z - 1 :, :]
            down_ref[at, :] = b_ref[c, x, :1, :]


def x_neighbours(ref, side_ref, first, c, x):
    cells_x = ref.shape[1]
    after = ref[c, jnp.minimum(x + 1, cells_x - 1)]
    before = ref[c, jnp.maximum(x - 1, 0)]
    zero = jnp.zeros_like(after)
    if side_ref is None:
        past_end, past_start = zero, zero
    else:
        side = side_ref[c - 1]
        past_end, past_start = jnp.where(first, side, zero), jnp.where(first, zero, side)
    return (
        jnp.where(x == cells_x - 1, past_end, after),
        jnp.where(x == 0, past_start, before),
    )


def electric_kernel(b_ref, r_ref, side_ref, below_ref, above_ref, gx_ref, elec_ref, edge_ref):
    cells_x = b_ref.shape[1]
    first = gx_ref[0] == 0

    def at(x):
        here = [b_ref[c, x] for c in range(3)]
        rows = [pl.ds(c * cells_x + x, 1) for c in range(2)]
        dz = [along_z(here[c], above_ref[rows[c], :], below_ref[rows[c], :]) for c in range(2)]
        dx = [None] + [slope(*x_neighbours(b_ref, side_ref, first, c, x)) for c in (1, 2)]
        current = (along_row(here[2]) - dz[1], dz[0] - dx[2], dx[1] - along_row(here[0]))
        for c, value in enumerate(electric_parts(current, here, r_ref[x])):
            elec_ref[c, x] = value

    over_x(cells_x, at)
    edge = jnp.where(first, cells_x - 1, 0)
    for c in range(2):
        edge_ref[c] = elec_ref[c + 1, edge]


def step_kernel(b_ref, elec_ref, rows_ref):
    cells_x, cells_z = b_ref.shape[1], b_ref.shape[2]
    half = 0.5 * time_step

    def at(x):
        here = [elec_ref[c, x] for c in range(3)]
        dz = [along_z(here[c], 0.0, 0.0) for c in range(2)]
        dx = [None] + [slope(*x_neighbours(elec_ref, None, None, c, x)) for c in (1, 2)]
        curl = (along_row(here[2]) - dz[1], dz[0] - dx[2], dx[1] - along_row(here[0]))
        for c in range(3):
            start = pl.multiple_of((c * cells_x + x) * cells_z, cells_z)
            rows_ref[pl.ds(start, cells_z), :] = b_ref[c, x] - time_step * curl[c]
        extra = 3 * cells_x * cells_z + 4 * x
        rows_ref[pl.ds(extra, 1), :] = half * here[1][:1]
        rows_ref[pl.ds(extra + 1, 1), :] = -half * here[1][cells_z - 1 :]
        rows_ref[pl.ds(extra + 2, 1), :] = -half * here[0][:1]
        rows_ref[pl.ds(extra + 3, 1), :] = half * here[0][cells_z - 1 :]

    over_x(cells_x, at)


def full_dot(lhs, rhs):
    return jnp.dot(lhs, rhs, precision=lax.Precision.HIGHEST, preferred_element_type=jnp.float32)


def mix_kernel(cells_x, cells_z, rows_ref, edge_ref, ymix_ref, gx_ref, out_ref, mixed):
    cells_y = rows_ref.shape[1]
    halves = cells_y // LANES
    mixed[...] = full_dot(rows_ref[...], ymix_ref[...])
    first = gx_ref[0] == 0
    factor = jnp.where(first, 0.5 * time_step, -0.5 * time_step)
    added = full_dot(edge_ref[...].reshape(2 * cells_z, cells_y), ymix_ref[...]) * factor
    edge = jnp.where(first, cells_x - 1, 0)
    for c, term in ((1, added[cells_z:]), (2, -added[:cells_z])):
        at = pl.ds(pl.multiple_of((c * cells_x + edge) * cells_z, cells_z), cells_z)
        mixed[at, :] = mixed[at, :] + term
    pairs = cells_x * halves // out_ref.shape[0]
    extra = 3 * cells_x * cells_z
    for x in range(cells_x):
        for half in range(halves):
            part, q = divmod(x * halves + half, pairs)
            lanes = slice(half * LANES, (half + 1) * LANES)
            for c in range(3):
                at = (q * 3 + c) * cells_z
                line = (c * cells_x + x) * cells_z
                out_ref[part, at : at + cells_z, :] = mixed[line : line + cells_z, lanes]
            at = pairs * 3 * cells_z + q * 4
            out_ref[part, at : at + 4, :] = mixed[extra + 4 * x : extra + 4 * x + 4, lanes]


def line_matrix_kernel(zmix_ref, out_ref):
    total = zmix_ref.shape[0]
    parts = out_ref.shape[0] - total
    turned = jnp.transpose(zmix_ref[...])
    slab = lax.broadcasted_iota(jnp.int32, (parts, total), 0) * (total // parts)
    lower = (lax.broadcasted_iota(jnp.int32, (parts, total), 1) < slab).astype(jnp.float32)
    out_ref[:total] = turned
    out_ref[total:] = jnp.dot(
        lower, turned, precision=lax.Precision.HIGHEST, preferred_element_type=jnp.float32
    )


def lines_kernel(cells_z, pairs, in_ref, line_ref, out_ref):
    parts = in_ref.shape[0]
    total = parts * cells_z
    height = pairs * 3 * cells_z
    level = lax.broadcasted_iota(jnp.int32, (cells_z, LANES), 0)
    columns = []
    for q in range(pairs):
        for c in range(3):
            at = (q * 3 + c) * cells_z
            tiles = [in_ref[s, at : at + cells_z, :] for s in range(parts)]
            if c < 2:
                low = height + q * 4 + c * 2
                for s in range(parts):
                    if s < parts - 1:
                        tiles[s] = tiles[s] + jnp.where(
                            level == cells_z - 1, in_ref[s + 1, low : low + 1, :], 0.0
                        )
                    if s > 0:
                        tiles[s] = tiles[s] + jnp.where(
                            level == 0, in_ref[s - 1, low + 1 : low + 2, :], 0.0
                        )
            columns.append(jnp.concatenate(tiles, axis=0))
    product = full_dot(line_ref[...], jnp.concatenate(columns, axis=1))
    for g in range(3 * pairs):
        part = product[:, g * LANES : (g + 1) * LANES]
        out_ref[:, g * cells_z : (g + 1) * cells_z, :] = part[:total].reshape(parts, cells_z, LANES)
        for s in range(parts):
            out_ref[s, height + g : height + g + 1, :] = part[total + s : total + s + 1]


def finish_kernel(scale, cells_z, in_ref, next_ref, pot_ref, buffer, sems):
    _, cells_x, _, cells_y = next_ref.shape
    each = in_ref.shape[1] // (cells_z + 1)
    halves = cells_y // LANES
    batch = cells_x // PIECES
    level = lax.broadcasted_iota(jnp.int32, (cells_z, LANES), 0)
    copies = []
    for piece in range(3 * PIECES):
        c, x = divmod(piece * batch, cells_x)
        factor = -scale if c == 0 else scale
        for i in range(batch):
            for half in range(halves):
                part, q = divmod((x + i) * halves + half, each // 3)
                at = q * 3 + c
                tile = in_ref[part, at * cells_z : (at + 1) * cells_z, :]
                total, step = tile, 1
                while step < cells_z:
                    total = total + jnp.where(level >= step, pltpu.roll(total, step, 0), 0.0)
                    step *= 2
                offset = in_ref[part, each * cells_z + at : each * cells_z + at + 1, :]
                lanes = slice(half * LANES, (half + 1) * LANES)
                buffer[0, piece, i, :, lanes] = tile
                buffer[1, piece, i, :, lanes] = (total + offset) * factor
        for k, (target, ref) in enumerate(((c, next_ref), ((1, 0, 2)[c], pot_ref))):
            copy = pltpu.make_async_copy(
                buffer.at[k, piece], ref.at[target, pl.ds(x, batch)], sems.at[k, piece]
            )
            copy.start()
            copies.append(copy)
    for copy in copies:
        copy.wait()


def limit(mib):
    return pltpu.CompilerParams(vmem_limit_bytes=mib * 2**20)


def kernel_form(b_field, resist, ymix, zmix):
    _, cells_x, cells_z, cells_y = b_field.shape
    parts = lax.axis_size("gz")
    total_z = cells_z * parts
    f32 = jnp.float32
    shape = lambda *sizes: jax.ShapeDtypeStruct(sizes, f32)
    place = lax.axis_index("gx").astype(jnp.int32).reshape(1)
    swap = lambda value: lax.ppermute(value, "gx", [(0, 1), (1, 0)])

    up, down, side = pl.pallas_call(
        pack_kernel,
        out_shape=(shape(2 * cells_x, cells_y), shape(2 * cells_x, cells_y), shape(2, cells_z, cells_y)),
        in_specs=[VMEM, SMEM],
        out_specs=(VMEM, VMEM, VMEM),
        compiler_params=limit(6),
    )(b_field, place)
    below = lax.ppermute(up, "gz", [(i, i + 1) for i in range(parts - 1)])
    above = lax.ppermute(down, "gz", [(i + 1, i) for i in range(parts - 1)])
    elec, edge = pl.pallas_call(
        electric_kernel,
        out_shape=(shape(*b_field.shape), shape(2, cells_z, cells_y)),
        in_specs=[VMEM] * 5 + [SMEM],
        out_specs=(VMEM, VMEM),
        compiler_params=limit(6),
        cost_estimate=estimate(200.0 * b_field.size),
    )(b_field, resist, swap(side), below, above, place)
    rows = pl.pallas_call(
        step_kernel,
        out_shape=shape(3 * cells_x * cells_z + 4 * cells_x, cells_y),
        in_specs=[VMEM] * 2,
        out_specs=VMEM,
        compiler_params=limit(6),
        cost_estimate=estimate(200.0 * b_field.size),
    )(b_field, elec)
    line = pl.pallas_call(
        line_matrix_kernel,
        out_shape=shape(total_z + parts, total_z),
        in_specs=[VMEM],
        out_specs=VMEM,
        compiler_params=limit(4),
    )(zmix)

    pairs = cells_x * (cells_y // LANES) // parts
    sent = pl.pallas_call(
        functools.partial(mix_kernel, cells_x, cells_z),
        out_shape=shape(parts, pairs * (3 * cells_z + 4), LANES),
        in_specs=[VMEM] * 3 + [SMEM],
        out_specs=VMEM,
        scratch_shapes=[pltpu.VMEM(rows.shape, f32)],
        compiler_params=limit(6),
    )(rows, swap(edge), ymix, place)
    lines = lax.all_to_all(sent, "gz", split_axis=0, concat_axis=0, tiled=True)
    product = pl.pallas_call(
        functools.partial(lines_kernel, cells_z, pairs),
        out_shape=shape(parts, pairs * 3 * (cells_z + 1), LANES),
        in_specs=[VMEM, VMEM],
        out_specs=VMEM,
        compiler_params=limit(6),
    )(lines, line)
    returned = lax.all_to_all(product, "gz", split_axis=0, concat_axis=0, tiled=True)
    whole = jax.ShapeDtypeStruct(b_field.shape, f32)
    hbm = pl.BlockSpec(memory_space=pl.ANY)
    return pl.pallas_call(
        functools.partial(finish_kernel, total_z ** (-0.5), cells_z),
        out_shape=(whole, whole),
        in_specs=[VMEM],
        out_specs=(hbm, hbm),
        scratch_shapes=[
            pltpu.VMEM((2, 3 * PIECES, cells_x // PIECES, cells_z, cells_y), f32),
            pltpu.SemaphoreType.DMA((2, 3 * PIECES)),
        ],
        compiler_params=limit(6),
    )(returned)


def estimate(flops):
    return pl.CostEstimate(flops=int(flops), bytes_accessed=0, transcendentals=0)


def on_device(b_field, resist, ymix, zmix):
    _, cells_x, cells_z, cells_y = b_field.shape
    parts = lax.axis_size("gz")
    fits = (
        lax.axis_size("gx") == 2
        and parts > 1
        and cells_z == SUBLANES
        and cells_x % PIECES == 0
        and cells_y % LANES == 0
        and cells_x % BATCH == 0
        and cells_x * (cells_y // LANES) % parts == 0
    )
    return (kernel_form if fits else plain_form)(b_field, resist, ymix, zmix)


def solution(mesh):
    in_specs = (P(None, "gx", "gz", None), P("gx", "gz", None), P(), P())
    out_specs = (P(None, "gx", "gz", None), P(None, "gx", "gz", None))
    return jax.shard_map(
        on_device, mesh=mesh, in_specs=in_specs, out_specs=out_specs, check_vma=False
    )
```

time: 134 us -> 68.9 us (0.51)
  local copies, waits for them, and re-layouts: 34.3 us -> 1.07 us
  starting transfers between devices: 41.9 us -> 14.2 us
  blocking collectives: 0 us -> 23.6 us
  waiting for transfers between devices: 37.9 us -> 23.9 us
  other arithmetic: 11.3 us -> 0 us
  matrix products: 6.63 us -> 0 us
  Pallas kernels: 0 us -> 4.99 us
    all_to_all x0 -> x1, blocking collectives: none -> 23.6 us  [kernel_form(): lax.all_to_all(product, 'gz', split_axis=0, concat_axis=0, tiled=True)]
    unnamed x23 -> x8, local copies, waits for them, and re-layouts: 17.2 us -> 1.07 us
    ppermute x8 -> x4, starting transfers between devices: 21.1 us -> 6.44 us  [the longest x1 5 us: kernel_form(): below = lax.ppermute(up, 'gz', [(i, i + 1) for i in range(parts - 1)])]
    all_to_all x3 -> x1, starting transfers between devices: 20.8 us -> 7.78 us  [kernel_form(): lines = lax.all_to_all(sent, 'gz', split_axis=0, concat_axis=0, tiled=True)]
    all_to_all x3 -> x1, waiting for transfers between devices: 30 us -> 18.7 us  [kernel_form(): lines = lax.all_to_all(sent, 'gz', split_axis=0, concat_axis=0, tiled=True)]
    all_to_all x5 -> x0, local copies, waits for them, and re-layouts: 9.54 us -> none  [the longest x2 8.66 us: on_device(): lax.all_to_all(along_z, 'gz', split_axis=3, concat_axis=2, tiled=True)]
    all_to_all x3 -> x0, other arithmetic: 6.72 us -> none  [the longest x1 2.96 us: on_device(): lax.all_to_all(along_z, 'gz', split_axis=3, concat_axis=2, tiled=True)]
    dot_general x2 -> x0, matrix products: 6.63 us -> none  [the longest x1 5.09 us: on_device(): jnp.einsum('cxym,mk->cxyk', lax.all_to_all(along_y, 'gz', split_axis=2, c...]
  transfers between devices with their start and end apart: 11 -> 5, of which waited for: 8 -> 4; matrix products, arithmetic and copies ran while one was open for 9% -> 0% of each run, Pallas kernels for 0% -> 1%
where the time goes in v5:
time: 68.9 us; the launch traced here: 68.5 us
  waiting for transfers between devices  23.9 us (35%)
  blocking collectives  23.6 us (34%)
  starting transfers between devices  14.2 us (21%)
  Pallas kernels  4.99 us (7%)
  local copies, waits for them, and re-layouts  1.07 us (2%)
  between operations  0.73 us (1%)
    all_to_all x1, blocking collectives, kernel_form(): lax.all_to_all(product, 'gz', split_axis=0, concat_axis=0, tiled=True)  23.6 us
    all_to_all x1, waiting for transfers between devices, kernel_form(): lines = lax.all_to_all(sent, 'gz', split_axis=0, concat_axis=0, tiled=True)  18.7 us
    all_to_all x1, starting transfers between devices, kernel_form(): lines = lax.all_to_all(sent, 'gz', split_axis=0, concat_axis=0, tiled=True)  7.78 us
    ppermute x1, starting transfers between devices, kernel_form(): below = lax.ppermute(up, 'gz', [(i, i + 1) for i in range(parts - 1)])  5 us
    ppermute x1, waiting for transfers between devices, kernel_form(): above = lax.ppermute(down, 'gz', [(i + 1, i) for i in range(parts - 1)])  3.43 us
    ppermute x2, waiting for transfers between devices, kernel_form(): swap = lambda value: lax.ppermute(value, 'gx', [(0, 1), (1, 0)])  1.79 us
    pallas_call x1, Pallas kernels, kernel_form(): pl.pallas_call(functools.partial(mix_kernel, cells_x, cells_z), out_shape...  1.7 us
  transfers between devices with their start and end apart: 5, of which 4 were waited for; matrix products, arithmetic and copies ran while one was open for 0% of the time, Pallas kernels for 1%

profile of v5, /device:TPU:0, one launch (start us, length us, event | category | flops | bytes accessed | tf_op | source)
XLA Modules:
  0.0 68.5 jit_solution(16249522722218714851)
XLA Ops:
  0.6 0.0 copy-start
  0.6 1.1 %copy-done = f32[3,24,8,256]{3,2,1,0:T(8,128)S(1)} copy-done((f32[3,24,8,256]{3,2,1,0:T(8,128)S(1)}, f32[3,24,8,256]{3,2,1,0:T(8,128)}, u32[]{:S(2)}) %copy-start) | copy-done | bytes 589848
  1.7 0.0 copy-start.2
  1.7 0.1 shard_map.59
  1.8 5.0 %collective-permute-start.1 = (f32[48,256]{1,0:T(8,128)S(1)}, f32[48,256]{1,0:T(8,128)S(1)}, u32[]{:S(2)}, u32[]{:S(2)}) collective-permute-start(f32[48,256]{1,0:T(8,128)S(1)} %get-tuple-element.8), channel_id=1, source_target_pairs={{0,2},{2,4},{4,6},{6,8},{8,10},{10,12},{12,14},{14,16},{16,18},{18... | collective-permute-start | bytes 147464 | tf_op jit(solution)/shard_map/ppermute | solution.py:301
  6.8 1.3 %collective-permute-start.2 = (f32[48,256]{1,0:T(8,128)S(1)}, f32[48,256]{1,0:T(8,128)S(1)}, u32[]{:S(2)}, u32[]{:S(2)}) collective-permute-start(f32[48,256]{1,0:T(8,128)S(1)} %get-tuple-element.9), channel_id=1, source_target_pairs={{2,0},{4,2},{6,4},{8,6},{10,8},{12,10},{14,12},{16,14},{18,16},{20... | collective-permute-start | bytes 147464 | tf_op jit(solution)/shard_map/ppermute | solution.py:302
  8.1 0.1 collective-permute-start
  8.1 1.2 %collective-permute-done.side_ref = f32[2,8,256]{2,1,0:T(8,128)S(1)} collective-permute-done((f32[2,8,256]{2,1,0:T(8,128)S(1)}, f32[2,8,256]{2,1,0:T(8,128)S(1)}, u32[]{:S(2)}, u32[]{:S(2)}) %collective-permute-start) | collective-permute-done | bytes 16416 | tf_op jit(solution)/shard_map/ppermute | solution.py:292
  9.3 0.0 collective-permute-done.1.below_ref
  9.3 3.4 %collective-permute-done.2.above_ref = f32[48,256]{1,0:T(8,128)S(1)} collective-permute-done((f32[48,256]{1,0:T(8,128)S(1)}, f32[48,256]{1,0:T(8,128)S(1)}, u32[]{:S(2)}, u32[]{:S(2)}) %collective-permute-start.2) | collective-permute-done | bytes 49184 | tf_op jit(solution)/shard_map/ppermute | solution.py:302
  12.8 0.0 copy-done.2
  12.8 0.6 shard_map.60
  13.3 0.1 collective-permute-start.3
  13.4 0.0 copy-start.1
  13.4 0.5 shard_map.61.rows_ref
  14.0 0.6 collective-permute-done.3.edge_ref
  14.6 0.0 copy-done.1
  14.6 1.7 %shard_map.62 = f32[16,84,128]{2,1,0:T(8,128)} custom-call(f32[672,256]{1,0:T(8,128)S(1)} %shard_map.61.rows_ref, f32[2,8,256]{2,1,0:T(8,128)S(1)} %collective-permute-done.3.edge_ref, f32[256,256]{1,0:T(8,128)S(1)} %copy-done.1, s32[1]{0:T(128)} %bitcast.gx_ref), custom_call_target="tpu_custom_call" | custom-call | tf_op jit(solution)/shard_map/pallas_call | solution.py:328
  16.3 0.0 copy-start.3
  16.3 7.8 %all-to-all-start = ((f32[16,84,128]{2,1,0:T(8,128)}), f32[16,84,128]{2,1,0:T(8,128)S(1)}, u32[]{:S(2)}, u32[]{:S(2)}) async-start(f32[16,84,128]{2,1,0:T(8,128)} %shard_map.62), calls=%async_computation | async-start | bytes 1441792 | tf_op jit(solution)/shard_map/all_to_all | solution.py:336
  24.1 0.0 copy-done.3
  24.1 0.2 shard_map.63.line_ref
  24.3 18.7 %all-to-all-done.in_ref = f32[16,84,128]{2,1,0:T(8,128)S(1)} async-done(((f32[16,84,128]{2,1,0:T(8,128)}), f32[16,84,128]{2,1,0:T(8,128)S(1)}, u32[]{:S(2)}, u32[]{:S(2)}) %all-to-all-start) | async-done | bytes 688160 | tf_op jit(solution)/shard_map/all_to_all | solution.py:336
  43.0 0.7 %shard_map.64 = f32[16,81,128]{2,1,0:T(8,128)S(1)} custom-call(f32[16,84,128]{2,1,0:T(8,128)S(1)} %all-to-all-done.in_ref, f32[144,128]{1,0:T(8,128)S(1)} %shard_map.63.line_ref), custom_call_target="tpu_custom_call" | custom-call | tf_op jit(solution)/shard_map/pallas_call | solution.py:337
  43.7 23.6 %all_to_all.10.in_ref = f32[16,81,128]{2,1,0:T(8,128)S(1)} all-to-all(f32[16,81,128]{2,1,0:T(8,128)S(1)} %shard_map.64), channel_id=1, replica_groups=mesh['gz'=16,'gx'=2] {'gz'}, dimensions={0} | all-to-all | bytes 1327104 | tf_op jit(solution)/shard_map/all_to_all | solution.py:344
  67.4 1.2 %shard_map.65 = (f32[3,24,8,256]{3,2,1,0:T(8,128)}, f32[3,24,8,256]{3,2,1,0:T(8,128)}) custom-call(f32[16,81,128]{2,1,0:T(8,128)S(1)} %all_to_all.10.in_ref), custom_call_target="tpu_custom_call" | custom-call | tf_op jit(solution)/shard_map/pallas_call | solution.py:347
Async XLA Ops:
  0.6 1.1 %copy-start = (f32[3,24,8,256]{3,2,1,0:T(8,128)S(1)}, f32[3,24,8,256]{3,2,1,0:T(8,128)}, u32[]{:S(2)}) copy-start(f32[3,24,8,256]{3,2,1,0:T(8,128)} %b_ref.5) | copy-start | bytes 1769476
  1.7 11.1 %copy-start.2 = (f32[24,8,256]{2,1,0:T(8,128)S(1)}, f32[24,8,256]{2,1,0:T(8,128)}, u32[]{:S(2)}) copy-start(f32[24,8,256]{2,1,0:T(8,128)} %r_ref.1) | copy-start | bytes 589828
  1.8 7.6 %collective-permute-start.1 = (f32[48,256]{1,0:T(8,128)S(1)}, f32[48,256]{1,0:T(8,128)S(1)}, u32[]{:S(2)}, u32[]{:S(2)}) collective-permute-start(f32[48,256]{1,0:T(8,128)S(1)} %get-tuple-element.8), channel_id=1, source_target_pairs={{0,2},{2,4},{4,6},{6,8},{8,10},{10,12},{12,14},{14,16},{16,18},{18... | collective-permute-start | bytes 147464 | tf_op jit(solution)/shard_map/ppermute | solution.py:301
  6.8 6.0 %collective-permute-start.2 = (f32[48,256]{1,0:T(8,128)S(1)}, f32[48,256]{1,0:T(8,128)S(1)}, u32[]{:S(2)}, u32[]{:S(2)}) collective-permute-start(f32[48,256]{1,0:T(8,128)S(1)} %get-tuple-element.9), channel_id=1, source_target_pairs={{2,0},{4,2},{6,4},{8,6},{10,8},{12,10},{14,12},{16,14},{18,16},{20... | collective-permute-start | bytes 147464 | tf_op jit(solution)/shard_map/ppermute | solution.py:302
  8.1 1.2 %collective-permute-start = (f32[2,8,256]{2,1,0:T(8,128)S(1)}, f32[2,8,256]{2,1,0:T(8,128)S(1)}, u32[]{:S(2)}, u32[]{:S(2)}) collective-permute-start(f32[2,8,256]{2,1,0:T(8,128)S(1)} %get-tuple-element.7), channel_id=1, source_target_pairs={{0,1},{1,0},{2,3},{3,2},{4,5},{5,4},{6,7},{7,6},{8,9},{9,8},{10,11... | collective-permute-start | bytes 49160 | tf_op jit(solution)/shard_map/ppermute | solution.py:292
  13.3 1.2 %collective-permute-start.3 = (f32[2,8,256]{2,1,0:T(8,128)S(1)}, f32[2,8,256]{2,1,0:T(8,128)S(1)}, u32[]{:S(2)}, u32[]{:S(2)}) collective-permute-start(f32[2,8,256]{2,1,0:T(8,128)S(1)} %get-tuple-element.11), channel_id=1, source_target_pairs={{0,1},{1,0},{2,3},{3,2},{4,5},{5,4},{6,7},{7,6},{8,9},{9,8},{10,11... | collective-permute-start | bytes 49160 | tf_op jit(solution)/shard_map/ppermute | solution.py:292
  13.4 1.2 %copy-start.1 = (f32[256,256]{1,0:T(8,128)S(1)}, f32[256,256]{1,0:T(8,128)}, u32[]{:S(2)}) copy-start(f32[256,256]{1,0:T(8,128)} %ymix_ref.1) | copy-start | bytes 786436
  16.3 7.8 %copy-start.3 = (f32[128,128]{1,0:T(8,128)S(1)}, f32[128,128]{1,0:T(8,128)}, u32[]{:S(2)}) copy-start(f32[128,128]{1,0:T(8,128)} %zmix_ref.1) | copy-start | bytes 196612
  16.3 26.7 %all-to-all-start = ((f32[16,84,128]{2,1,0:T(8,128)}), f32[16,84,128]{2,1,0:T(8,128)S(1)}, u32[]{:S(2)}, u32[]{:S(2)}) async-start(f32[16,84,128]{2,1,0:T(8,128)} %shard_map.62), calls=%async_computation | async-start | bytes 1441792 | tf_op jit(solution)/shard_map/all_to_all | solution.py:336

commit v6 on v5

--- a/solution.py
+++ b/solution.py
@@ -174,8 +174,15 @@
     over_x(cells_x, at)
 
 
+def split(value):
+    high = value.astype(jnp.bfloat16)
+    return high, (value - high.astype(jnp.float32)).astype(jnp.bfloat16)
+
+
 def full_dot(lhs, rhs):
-    return jnp.dot(lhs, rhs, precision=lax.Precision.HIGHEST, preferred_element_type=jnp.float32)
+    dot = functools.partial(jnp.dot, preferred_element_type=jnp.float32)
+    (lhs_high, lhs_low), (rhs_high, rhs_low) = split(lhs), split(rhs)
+    return dot(lhs_high, rhs_high) + (dot(lhs_high, rhs_low) + dot(lhs_low, rhs_high))
 
 
 def mix_kernel(cells_x, cells_z, rows_ref, edge_ref, ymix_ref, gx_ref, out_ref, mixed):
@@ -300,6 +307,14 @@
     )(b_field, place)
     below = lax.ppermute(up, "gz", [(i, i + 1) for i in range(parts - 1)])
     above = lax.ppermute(down, "gz", [(i + 1, i) for i in range(parts - 1)])
+    line = pl.pallas_call(
+        line_matrix_kernel,
+        out_shape=shape(total_z + parts, total_z),
+        in_specs=[VMEM],
+        out_specs=VMEM,
+        compiler_params=limit(4),
+    )(zmix)
+    line, below = lax.optimization_barrier((line, below))
     elec, edge = pl.pallas_call(
         electric_kernel,
         out_shape=(shape(*b_field.shape), shape(2, cells_z, cells_y)),
@@ -316,14 +331,6 @@
         compiler_params=limit(6),
         cost_estimate=estimate(200.0 * b_field.size),
     )(b_field, elec)
-    line = pl.pallas_call(
-        line_matrix_kernel,
-        out_shape=shape(total_z + parts, total_z),
-        in_specs=[VMEM],
-        out_specs=VMEM,
-        compiler_params=limit(4),
-    )(zmix)
-
     pairs = cells_x * (cells_y // LANES) // parts
     sent = pl.pallas_call(
         functools.partial(mix_kernel, cells_x, cells_z),

time: 68.9 us -> 67.3 us (0.977)
  blocking collectives: 23.6 us -> 50.2 us
  waiting for transfers between devices: 23.9 us -> 4.97 us
  starting transfers between devices: 14.2 us -> 6.44 us
  Pallas kernels: 4.99 us -> 3.57 us
    all_to_all x0 -> x1, blocking collectives: none -> 27.9 us  [kernel_form(): lines = lax.all_to_all(sent, 'gz', split_axis=0, concat_axis=0, tiled=True)]
    all_to_all x1 -> x0, waiting for transfers between devices: 18.7 us -> none  [kernel_form(): lines = lax.all_to_all(sent, 'gz', split_axis=0, concat_axis=0, tiled=True)]
    all_to_all x1 -> x0, starting transfers between devices: 7.78 us -> none  [kernel_form(): lines = lax.all_to_all(sent, 'gz', split_axis=0, concat_axis=0, tiled=True)]
    all_to_all x1, blocking collectives: 23.6 us -> 22.3 us  [kernel_form(): lax.all_to_all(product, 'gz', split_axis=0, concat_axis=0, tiled=True)]
    pallas_call x1, Pallas kernels: 1.7 us -> 0.5 us  [kernel_form(): pl.pallas_call(functools.partial(mix_kernel, cells_x, cells_z), out_shape...]
  transfers between devices with their start and end apart: 5 -> 4, of which waited for: 4 -> 4; matrix products, arithmetic and copies ran while one was open for 0% -> 0% of each run, Pallas kernels for 1% -> 1%
where the time goes in v6:
time: 67.3 us; the launch traced here: 67 us
  blocking collectives  50.2 us (75%)
  starting transfers between devices  6.44 us (10%)
  waiting for transfers between devices  4.97 us (7%)
  Pallas kernels  3.57 us (5%)
  local copies, waits for them, and re-layouts  1.07 us (2%)
  between operations  0.73 us (1%)
    all_to_all x1, blocking collectives, kernel_form(): lines = lax.all_to_all(sent, 'gz', split_axis=0, concat_axis=0, tiled=True)  27.9 us
    all_to_all x1, blocking collectives, kernel_form(): lax.all_to_all(product, 'gz', split_axis=0, concat_axis=0, tiled=True)  22.3 us
    ppermute x1, starting transfers between devices, kernel_form(): below = lax.ppermute(up, 'gz', [(i, i + 1) for i in range(parts - 1)])  5 us
    ppermute x1, waiting for transfers between devices, kernel_form(): above = lax.ppermute(down, 'gz', [(i + 1, i) for i in range(parts - 1)])  3.43 us
    ppermute x2, waiting for transfers between devices, kernel_form(): swap = lambda value: lax.ppermute(value, 'gx', [(0, 1), (1, 0)])  1.43 us
  transfers between devices with their start and end apart: 4, of which 4 were waited for; matrix products, arithmetic and copies ran while one was open for 0% of the time, Pallas kernels for 1%

profile of v6, /device:TPU:0, one launch (start us, length us, event | category | flops | bytes accessed | tf_op | source)
XLA Modules:
  0.0 67.0 jit_solution(18311927136780075926)
XLA Ops:
  0.6 0.0 copy-start
  0.6 1.1 %copy-done = f32[3,24,8,256]{3,2,1,0:T(8,128)S(1)} copy-done((f32[3,24,8,256]{3,2,1,0:T(8,128)S(1)}, f32[3,24,8,256]{3,2,1,0:T(8,128)}, u32[]{:S(2)}) %copy-start) | copy-done | bytes 589848
  1.7 0.0 copy-start.3
  1.7 0.0 copy-start.2
  1.7 0.1 shard_map.59
  1.8 5.0 %collective-permute-start.1 = (f32[48,256]{1,0:T(8,128)S(1)}, f32[48,256]{1,0:T(8,128)S(1)}, u32[]{:S(2)}, u32[]{:S(2)}) collective-permute-start(f32[48,256]{1,0:T(8,128)S(1)} %get-tuple-element.10), channel_id=1, source_target_pairs={{0,2},{2,4},{4,6},{6,8},{8,10},{10,12},{12,14},{14,16},{16,18},{18... | collective-permute-start | bytes 147464 | tf_op jit(solution)/shard_map/ppermute | solution.py:308
  6.8 1.3 %collective-permute-start.2 = (f32[48,256]{1,0:T(8,128)S(1)}, f32[48,256]{1,0:T(8,128)S(1)}, u32[]{:S(2)}, u32[]{:S(2)}) collective-permute-start(f32[48,256]{1,0:T(8,128)S(1)} %get-tuple-element.12), channel_id=1, source_target_pairs={{2,0},{4,2},{6,4},{8,6},{10,8},{12,10},{14,12},{16,14},{18,16},{20... | collective-permute-start | bytes 147464 | tf_op jit(solution)/shard_map/ppermute | solution.py:309
  8.1 0.1 collective-permute-start
  8.2 0.0 copy-done.3
  8.2 0.2 shard_map.60.line_ref
  8.4 0.1 collective-permute-done.1.below_ref
  8.5 0.8 %collective-permute-done.side_ref = f32[2,8,256]{2,1,0:T(8,128)S(1)} collective-permute-done((f32[2,8,256]{2,1,0:T(8,128)S(1)}, f32[2,8,256]{2,1,0:T(8,128)S(1)}, u32[]{:S(2)}, u32[]{:S(2)}) %collective-permute-start) | collective-permute-done | bytes 16416 | tf_op jit(solution)/shard_map/ppermute | solution.py:299
  9.3 3.4 %collective-permute-done.2.above_ref = f32[48,256]{1,0:T(8,128)S(1)} collective-permute-done((f32[48,256]{1,0:T(8,128)S(1)}, f32[48,256]{1,0:T(8,128)S(1)}, u32[]{:S(2)}, u32[]{:S(2)}) %collective-permute-start.2) | collective-permute-done | bytes 49184 | tf_op jit(solution)/shard_map/ppermute | solution.py:309
  12.8 0.0 copy-done.2
  12.8 0.6 shard_map.61
  13.3 0.1 collective-permute-start.3
  13.4 0.0 copy-start.1
  13.4 0.5 shard_map.62.rows_ref
  14.0 0.6 collective-permute-done.3.edge_ref
  14.6 0.0 copy-done.1
  14.6 0.5 shard_map.63
  15.1 27.9 %all_to_all.10.in_ref = f32[16,84,128]{2,1,0:T(8,128)S(1)} all-to-all(f32[16,84,128]{2,1,0:T(8,128)S(1)} %shard_map.63), channel_id=1, replica_groups=mesh['gz'=16,'gx'=2] {'gz'}, dimensions={0} | all-to-all | bytes 1376256 | tf_op jit(solution)/shard_map/all_to_all | solution.py:343
  43.0 0.5 shard_map.64
  43.5 22.3 %all_to_all.11.in_ref = f32[16,81,128]{2,1,0:T(8,128)S(1)} all-to-all(f32[16,81,128]{2,1,0:T(8,128)S(1)} %shard_map.64), channel_id=1, replica_groups=mesh['gz'=16,'gx'=2] {'gz'}, dimensions={0} | all-to-all | bytes 1327104 | tf_op jit(solution)/shard_map/all_to_all | solution.py:351
  65.8 1.2 %shard_map.65 = (f32[3,24,8,256]{3,2,1,0:T(8,128)}, f32[3,24,8,256]{3,2,1,0:T(8,128)}) custom-call(f32[16,81,128]{2,1,0:T(8,128)S(1)} %all_to_all.11.in_ref), custom_call_target="tpu_custom_call" | custom-call | tf_op jit(solution)/shard_map/pallas_call | solution.py:354
Async XLA Ops:
  0.6 1.1 %copy-start = (f32[3,24,8,256]{3,2,1,0:T(8,128)S(1)}, f32[3,24,8,256]{3,2,1,0:T(8,128)}, u32[]{:S(2)}) copy-start(f32[3,24,8,256]{3,2,1,0:T(8,128)} %b_ref.5) | copy-start | bytes 1769476
  1.7 6.5 %copy-start.3 = (f32[128,128]{1,0:T(8,128)S(1)}, f32[128,128]{1,0:T(8,128)}, u32[]{:S(2)}) copy-start(f32[128,128]{1,0:T(8,128)} %zmix_ref.1) | copy-start | bytes 196612
  1.7 11.1 %copy-start.2 = (f32[24,8,256]{2,1,0:T(8,128)S(1)}, f32[24,8,256]{2,1,0:T(8,128)}, u32[]{:S(2)}) copy-start(f32[24,8,256]{2,1,0:T(8,128)} %r_ref.1) | copy-start | bytes 589828
  1.8 6.7 %collective-permute-start.1 = (f32[48,256]{1,0:T(8,128)S(1)}, f32[48,256]{1,0:T(8,128)S(1)}, u32[]{:S(2)}, u32[]{:S(2)}) collective-permute-start(f32[48,256]{1,0:T(8,128)S(1)} %get-tuple-element.10), channel_id=1, source_target_pairs={{0,2},{2,4},{4,6},{6,8},{8,10},{10,12},{12,14},{14,16},{16,18},{18... | collective-permute-start | bytes 147464 | tf_op jit(solution)/shard_map/ppermute | solution.py:308
  6.8 6.0 %collective-permute-start.2 = (f32[48,256]{1,0:T(8,128)S(1)}, f32[48,256]{1,0:T(8,128)S(1)}, u32[]{:S(2)}, u32[]{:S(2)}) collective-permute-start(f32[48,256]{1,0:T(8,128)S(1)} %get-tuple-element.12), channel_id=1, source_target_pairs={{2,0},{4,2},{6,4},{8,6},{10,8},{12,10},{14,12},{16,14},{18,16},{20... | collective-permute-start | bytes 147464 | tf_op jit(solution)/shard_map/ppermute | solution.py:309
  8.1 1.2 %collective-permute-start = (f32[2,8,256]{2,1,0:T(8,128)S(1)}, f32[2,8,256]{2,1,0:T(8,128)S(1)}, u32[]{:S(2)}, u32[]{:S(2)}) collective-permute-start(f32[2,8,256]{2,1,0:T(8,128)S(1)} %get-tuple-element.9), channel_id=1, source_target_pairs={{0,1},{1,0},{2,3},{3,2},{4,5},{5,4},{6,7},{7,6},{8,9},{9,8},{10,11... | collective-permute-start | bytes 49160 | tf_op jit(solution)/shard_map/ppermute | solution.py:299
  13.3 1.2 %collective-permute-start.3 = (f32[2,8,256]{2,1,0:T(8,128)S(1)}, f32[2,8,256]{2,1,0:T(8,128)S(1)}, u32[]{:S(2)}, u32[]{:S(2)}) collective-permute-start(f32[2,8,256]{2,1,0:T(8,128)S(1)} %get-tuple-element.14), channel_id=1, source_target_pairs={{0,1},{1,0},{2,3},{3,2},{4,5},{5,4},{6,7},{7,6},{8,9},{9,8},{10,11... | collective-permute-start | bytes 49160 | tf_op jit(solution)/shard_map/ppermute | solution.py:299
  13.4 1.2 %copy-start.1 = (f32[256,256]{1,0:T(8,128)S(1)}, f32[256,256]{1,0:T(8,128)}, u32[]{:S(2)}) copy-start(f32[256,256]{1,0:T(8,128)} %ymix_ref.1) | copy-start | bytes 786436

commit v7 on v6

--- a/solution.py
+++ b/solution.py
@@ -10,6 +10,7 @@
 friction = 1.0
 LANES = 128
 SUBLANES = 8
+SHORT = 4
 PIECES = 3
 BATCH = 6
 VMEM = pl.BlockSpec(memory_space=pltpu.VMEM)
@@ -79,6 +80,19 @@
     offset = jnp.transpose(returned_flux, (0, 1, 3, 2))
     column = (jnp.cumsum(b_next, axis=2) + offset) * total_z ** (-0.5)
     return b_next, jnp.stack([column[1], -column[0], column[2]])
+
+
+def store_tile(ref, part, at, tile):
+    count = tile.shape[0] // SHORT
+    ref[part, at // SHORT : at // SHORT + count] = tile.reshape(count, SHORT, LANES)
+
+
+def load_tile(ref, part, at, height):
+    return ref[part, at // SHORT : (at + height) // SHORT].reshape(height, LANES)
+
+
+def one_row(ref, part, at):
+    return ref[part, at // SHORT, at % SHORT : at % SHORT + 1, :]
 
 
 def slope(after, before):
@@ -205,9 +219,9 @@
             for c in range(3):
                 at = (q * 3 + c) * cells_z
                 line = (c * cells_x + x) * cells_z
-                out_ref[part, at : at + cells_z, :] = mixed[line : line + cells_z, lanes]
+                store_tile(out_ref, part, at, mixed[line : line + cells_z, lanes])
             at = pairs * 3 * cells_z + q * 4
-            out_ref[part, at : at + 4, :] = mixed[extra + 4 * x : extra + 4 * x + 4, lanes]
+            store_tile(out_ref, part, at, mixed[extra + 4 * x : extra + 4 * x + 4, lanes])
 
 
 def line_matrix_kernel(zmix_ref, out_ref):
@@ -231,30 +245,30 @@
     for q in range(pairs):
         for c in range(3):
             at = (q * 3 + c) * cells_z
-            tiles = [in_ref[s, at : at + cells_z, :] for s in range(parts)]
+            tiles = [load_tile(in_ref, s, at, cells_z) for s in range(parts)]
             if c < 2:
                 low = height + q * 4 + c * 2
                 for s in range(parts):
                     if s < parts - 1:
                         tiles[s] = tiles[s] + jnp.where(
-                            level == cells_z - 1, in_ref[s + 1, low : low + 1, :], 0.0
+                            level == cells_z - 1, one_row(in_ref, s + 1, low), 0.0
                         )
                     if s > 0:
                         tiles[s] = tiles[s] + jnp.where(
-                            level == 0, in_ref[s - 1, low + 1 : low + 2, :], 0.0
+                            level == 0, one_row(in_ref, s - 1, low + 1), 0.0
                         )
             columns.append(jnp.concatenate(tiles, axis=0))
     product = full_dot(line_ref[...], jnp.concatenate(columns, axis=1))
     for g in range(3 * pairs):
         part = product[:, g * LANES : (g + 1) * LANES]
-        out_ref[:, g * cells_z : (g + 1) * cells_z, :] = part[:total].reshape(parts, cells_z, LANES)
+        row = height + g
         for s in range(parts):
-            out_ref[s, height + g : height + g + 1, :] = part[total + s : total + s + 1]
-
-
-def finish_kernel(scale, cells_z, in_ref, next_ref, pot_ref, buffer, sems):
+            store_tile(out_ref, s, g * cells_z, part[s * cells_z : (s + 1) * cells_z])
+            out_ref[s, row // SHORT, row % SHORT : row % SHORT + 1, :] = part[total + s : total + s + 1]
+
+
+def finish_kernel(scale, cells_z, each, in_ref, next_ref, pot_ref, buffer, sems):
     _, cells_x, _, cells_y = next_ref.shape
-    each = in_ref.shape[1] // (cells_z + 1)
     halves = cells_y // LANES
     batch = cells_x // PIECES
     level = lax.broadcasted_iota(jnp.int32, (cells_z, LANES), 0)
@@ -266,12 +280,12 @@
             for half in range(halves):
                 part, q = divmod((x + i) * halves + half, each // 3)
                 at = q * 3 + c
-                tile = in_ref[part, at * cells_z : (at + 1) * cells_z, :]
+                tile = load_tile(in_ref, part, at * cells_z, cells_z)
                 total, step = tile, 1
                 while step < cells_z:
                     total = total + jnp.where(level >= step, pltpu.roll(total, step, 0), 0.0)
                     step *= 2
-                offset = in_ref[part, each * cells_z + at : each * cells_z + at + 1, :]
+                offset = one_row(in_ref, part, each * cells_z + at)
                 lanes = slice(half * LANES, (half + 1) * LANES)
                 buffer[0, piece, i, :, lanes] = tile
                 buffer[1, piece, i, :, lanes] = (total + offset) * factor
@@ -334,7 +348,7 @@
     pairs = cells_x * (cells_y // LANES) // parts
     sent = pl.pallas_call(
         functools.partial(mix_kernel, cells_x, cells_z),
-        out_shape=shape(parts, pairs * (3 * cells_z + 4), LANES),
+        out_shape=shape(parts, pairs * (3 * cells_z + 4) // SHORT, SHORT, LANES),
         in_specs=[VMEM] * 3 + [SMEM],
         out_specs=VMEM,
         scratch_shapes=[pltpu.VMEM(rows.shape, f32)],
@@ -343,7 +357,7 @@
     lines = lax.all_to_all(sent, "gz", split_axis=0, concat_axis=0, tiled=True)
     product = pl.pallas_call(
         functools.partial(lines_kernel, cells_z, pairs),
-        out_shape=shape(parts, pairs * 3 * (cells_z + 1), LANES),
+        out_shape=shape(parts, -(-pairs * 3 * (cells_z + 1) // SHORT), SHORT, LANES),
         in_specs=[VMEM, VMEM],
         out_specs=VMEM,
         compiler_params=limit(6),
@@ -352,7 +366,7 @@
     whole = jax.ShapeDtypeStruct(b_field.shape, f32)
     hbm = pl.BlockSpec(memory_space=pl.ANY)
     return pl.pallas_call(
-        functools.partial(finish_kernel, total_z ** (-0.5), cells_z),
+        functools.partial(finish_kernel, total_z ** (-0.5), cells_z, 3 * pairs),
         out_shape=(whole, whole),
         in_specs=[VMEM],
         out_specs=(hbm, hbm),

time: 67.3 us -> 66.1 us (0.982)
  blocking collectives: 50.2 us -> 48.9 us
where the time goes in v7:
time: 66.1 us; the launch traced here: 65.8 us
  blocking collectives  48.9 us (74%)
  starting transfers between devices  6.44 us (10%)
  waiting for transfers between devices  4.97 us (8%)
  Pallas kernels  3.71 us (6%)
  local copies, waits for them, and re-layouts  1.07 us (2%)
  between operations  0.73 us (1%)
    all_to_all x1, blocking collectives, kernel_form(): lines = lax.all_to_all(sent, 'gz', split_axis=0, concat_axis=0, tiled=True)  27.3 us
    all_to_all x1, blocking collectives, kernel_form(): lax.all_to_all(product, 'gz', split_axis=0, concat_axis=0, tiled=True)  21.7 us
    ppermute x1, starting transfers between devices, kernel_form(): below = lax.ppermute(up, 'gz', [(i, i + 1) for i in range(parts - 1)])  5 us
    ppermute x1, waiting for transfers between devices, kernel_form(): above = lax.ppermute(down, 'gz', [(i + 1, i) for i in range(parts - 1)])  3.43 us
    ppermute x2, waiting for transfers between devices, kernel_form(): swap = lambda value: lax.ppermute(value, 'gx', [(0, 1), (1, 0)])  1.43 us
  transfers between devices with their start and end apart: 4, of which 4 were waited for; matrix products, arithmetic and copies ran while one was open for 0% of the time, Pallas kernels for 1%

profile of v7, /device:TPU:0, one launch (start us, length us, event | category | flops | bytes accessed | tf_op | source)
XLA Modules:
  0.0 65.8 jit_solution(13461424130149708818)
XLA Ops:
  0.6 0.0 copy-start
  0.6 1.1 %copy-done = f32[3,24,8,256]{3,2,1,0:T(8,128)S(1)} copy-done((f32[3,24,8,256]{3,2,1,0:T(8,128)S(1)}, f32[3,24,8,256]{3,2,1,0:T(8,128)}, u32[]{:S(2)}) %copy-start) | copy-done | bytes 589848
  1.7 0.0 copy-start.3
  1.7 0.0 copy-start.2
  1.7 0.1 shard_map.59
  1.8 5.0 %collective-permute-start.1 = (f32[48,256]{1,0:T(8,128)S(1)}, f32[48,256]{1,0:T(8,128)S(1)}, u32[]{:S(2)}, u32[]{:S(2)}) collective-permute-start(f32[48,256]{1,0:T(8,128)S(1)} %get-tuple-element.10), channel_id=1, source_target_pairs={{0,2},{2,4},{4,6},{6,8},{8,10},{10,12},{12,14},{14,16},{16,18},{18... | collective-permute-start | bytes 147464 | tf_op jit(solution)/shard_map/ppermute | solution.py:322
  6.8 1.3 %collective-permute-start.2 = (f32[48,256]{1,0:T(8,128)S(1)}, f32[48,256]{1,0:T(8,128)S(1)}, u32[]{:S(2)}, u32[]{:S(2)}) collective-permute-start(f32[48,256]{1,0:T(8,128)S(1)} %get-tuple-element.12), channel_id=1, source_target_pairs={{2,0},{4,2},{6,4},{8,6},{10,8},{12,10},{14,12},{16,14},{18,16},{20... | collective-permute-start | bytes 147464 | tf_op jit(solution)/shard_map/ppermute | solution.py:323
  8.1 0.1 collective-permute-start
  8.2 0.0 copy-done.3
  8.2 0.2 shard_map.60.line_ref
  8.4 0.1 collective-permute-done.1.below_ref
  8.5 0.8 %collective-permute-done.side_ref = f32[2,8,256]{2,1,0:T(8,128)S(1)} collective-permute-done((f32[2,8,256]{2,1,0:T(8,128)S(1)}, f32[2,8,256]{2,1,0:T(8,128)S(1)}, u32[]{:S(2)}, u32[]{:S(2)}) %collective-permute-start) | collective-permute-done | bytes 16416 | tf_op jit(solution)/shard_map/ppermute | solution.py:313
  9.3 3.4 %collective-permute-done.2.above_ref = f32[48,256]{1,0:T(8,128)S(1)} collective-permute-done((f32[48,256]{1,0:T(8,128)S(1)}, f32[48,256]{1,0:T(8,128)S(1)}, u32[]{:S(2)}, u32[]{:S(2)}) %collective-permute-start.2) | collective-permute-done | bytes 49184 | tf_op jit(solution)/shard_map/ppermute | solution.py:323
  12.8 0.0 copy-done.2
  12.8 0.6 shard_map.61
  13.3 0.1 collective-permute-start.3
  13.4 0.0 copy-start.1
  13.4 0.5 shard_map.62.rows_ref
  14.0 0.6 collective-permute-done.3.edge_ref
  14.6 0.0 copy-done.1
  14.6 0.5 shard_map.63
  15.1 27.3 %all_to_all.10.in_ref = f32[16,21,4,128]{3,2,1,0:T(4,128)S(1)} all-to-all(f32[16,21,4,128]{3,2,1,0:T(4,128)S(1)} %shard_map.63), channel_id=1, replica_groups=mesh['gz'=16,'gx'=2] {'gz'}, dimensions={0} | all-to-all | bytes 1376256 | tf_op jit(solution)/shard_map/all_to_all | solution.py:357
  42.4 0.5 shard_map.64
  42.9 21.7 %all_to_all.11.in_ref = f32[16,21,4,128]{3,2,1,0:T(4,128)S(1)} all-to-all(f32[16,21,4,128]{3,2,1,0:T(4,128)S(1)} %shard_map.64), channel_id=1, replica_groups=mesh['gz'=16,'gx'=2] {'gz'}, dimensions={0} | all-to-all | bytes 1376256 | tf_op jit(solution)/shard_map/all_to_all | solution.py:365
  64.6 1.3 %shard_map.65 = (f32[3,24,8,256]{3,2,1,0:T(8,128)}, f32[3,24,8,256]{3,2,1,0:T(8,128)}) custom-call(f32[16,21,4,128]{3,2,1,0:T(4,128)S(1)} %all_to_all.11.in_ref), custom_call_target="tpu_custom_call" | custom-call | tf_op jit(solution)/shard_map/pallas_call | solution.py:368
Async XLA Ops:
  0.6 1.1 %copy-start = (f32[3,24,8,256]{3,2,1,0:T(8,128)S(1)}, f32[3,24,8,256]{3,2,1,0:T(8,128)}, u32[]{:S(2)}) copy-start(f32[3,24,8,256]{3,2,1,0:T(8,128)} %b_ref.5) | copy-start | bytes 1769476
  1.7 6.5 %copy-start.3 = (f32[128,128]{1,0:T(8,128)S(1)}, f32[128,128]{1,0:T(8,128)}, u32[]{:S(2)}) copy-start(f32[128,128]{1,0:T(8,128)} %zmix_ref.1) | copy-start | bytes 196612
  1.7 11.1 %copy-start.2 = (f32[24,8,256]{2,1,0:T(8,128)S(1)}, f32[24,8,256]{2,1,0:T(8,128)}, u32[]{:S(2)}) copy-start(f32[24,8,256]{2,1,0:T(8,128)} %r_ref.1) | copy-start | bytes 589828
  1.8 6.7 %collective-permute-start.1 = (f32[48,256]{1,0:T(8,128)S(1)}, f32[48,256]{1,0:T(8,128)S(1)}, u32[]{:S(2)}, u32[]{:S(2)}) collective-permute-start(f32[48,256]{1,0:T(8,128)S(1)} %get-tuple-element.10), channel_id=1, source_target_pairs={{0,2},{2,4},{4,6},{6,8},{8,10},{10,12},{12,14},{14,16},{16,18},{18... | collective-permute-start | bytes 147464 | tf_op jit(solution)/shard_map/ppermute | solution.py:322
  6.8 6.0 %collective-permute-start.2 = (f32[48,256]{1,0:T(8,128)S(1)}, f32[48,256]{1,0:T(8,128)S(1)}, u32[]{:S(2)}, u32[]{:S(2)}) collective-permute-start(f32[48,256]{1,0:T(8,128)S(1)} %get-tuple-element.12), channel_id=1, source_target_pairs={{2,0},{4,2},{6,4},{8,6},{10,8},{12,10},{14,12},{16,14},{18,16},{20... | collective-permute-start | bytes 147464 | tf_op jit(solution)/shard_map/ppermute | solution.py:323
  8.1 1.2 %collective-permute-start = (f32[2,8,256]{2,1,0:T(8,128)S(1)}, f32[2,8,256]{2,1,0:T(8,128)S(1)}, u32[]{:S(2)}, u32[]{:S(2)}) collective-permute-start(f32[2,8,256]{2,1,0:T(8,128)S(1)} %get-tuple-element.9), channel_id=1, source_target_pairs={{0,1},{1,0},{2,3},{3,2},{4,5},{5,4},{6,7},{7,6},{8,9},{9,8},{10,11... | collective-permute-start | bytes 49160 | tf_op jit(solution)/shard_map/ppermute | solution.py:313
  13.3 1.2 %collective-permute-start.3 = (f32[2,8,256]{2,1,0:T(8,128)S(1)}, f32[2,8,256]{2,1,0:T(8,128)S(1)}, u32[]{:S(2)}, u32[]{:S(2)}) collective-permute-start(f32[2,8,256]{2,1,0:T(8,128)S(1)} %get-tuple-element.14), channel_id=1, source_target_pairs={{0,1},{1,0},{2,3},{3,2},{4,5},{5,4},{6,7},{7,6},{8,9},{9,8},{10,11... | collective-permute-start | bytes 49160 | tf_op jit(solution)/shard_map/ppermute | solution.py:313
  13.4 1.2 %copy-start.1 = (f32[256,256]{1,0:T(8,128)S(1)}, f32[256,256]{1,0:T(8,128)}, u32[]{:S(2)}) copy-start(f32[256,256]{1,0:T(8,128)} %ymix_ref.1) | copy-start | bytes 786436

commit v8 on v7

--- a/solution.py
+++ b/solution.py
@@ -121,15 +121,18 @@
     lax.fori_loop(0, cells_x // BATCH, trip, 0)
 
 
-def pack_kernel(b_ref, gx_ref, up_ref, down_ref, side_ref):
+def pack_kernel(b_ref, place_ref, far_ref, near_ref, side_ref):
     cells_x, cells_z = b_ref.shape[1], b_ref.shape[2]
-    edge = jnp.where(gx_ref[0] == 0, cells_x - 1, 0)
+    edge = jnp.where((place_ref[0] & 1) == 0, cells_x - 1, 0)
+    odd = place_ref[0] >= 2
+    far_row = jnp.where(odd, cells_z - 1, 0)
+    near_row = jnp.where(odd, 0, cells_z - 1)
     for c in range(2):
         side_ref[c] = b_ref[c + 1, edge]
         for x in range(cells_x):
             at = pl.ds(c * cells_x + x, 1)
-            up_ref[at, :] = b_ref[c, x, cells_z - 1 :, :]
-            down_ref[at, :] = b_ref[c, x, :1, :]
+            far_ref[at, :] = b_ref[c, x, pl.ds(far_row, 1), :]
+            near_ref[at, :] = b_ref[c, x, pl.ds(near_row, 1), :]
 
 
 def x_neighbours(ref, side_ref, first, c, x):
@@ -148,30 +151,37 @@
     )
 
 
-def electric_kernel(b_ref, r_ref, side_ref, below_ref, above_ref, gx_ref, elec_ref, edge_ref):
+def electric_at(b_ref, r_ref, side_ref, far_ref, near_ref, place_ref, x):
     cells_x = b_ref.shape[1]
-    first = gx_ref[0] == 0
-
-    def at(x):
-        here = [b_ref[c, x] for c in range(3)]
-        rows = [pl.ds(c * cells_x + x, 1) for c in range(2)]
-        dz = [along_z(here[c], above_ref[rows[c], :], below_ref[rows[c], :]) for c in range(2)]
-        dx = [None] + [slope(*x_neighbours(b_ref, side_ref, first, c, x)) for c in (1, 2)]
-        current = (along_row(here[2]) - dz[1], dz[0] - dx[2], dx[1] - along_row(here[0]))
-        for c, value in enumerate(electric_parts(current, here, r_ref[x])):
-            elec_ref[c, x] = value
-
-    over_x(cells_x, at)
-    edge = jnp.where(first, cells_x - 1, 0)
+    odd = place_ref[0] >= 2
+    here = [b_ref[c, x] for c in range(3)]
+    dz = []
     for c in range(2):
-        edge_ref[c] = elec_ref[c + 1, edge]
-
-
-def step_kernel(b_ref, elec_ref, rows_ref):
+        at = pl.ds(c * cells_x + x, 1)
+        far, near = far_ref[at, :], near_ref[at, :]
+        dz.append(along_z(here[c], jnp.where(odd, far, near), jnp.where(odd, near, far)))
+    first = (place_ref[0] & 1) == 0
+    dx = [None] + [slope(*x_neighbours(b_ref, side_ref, first, c, x)) for c in (1, 2)]
+    current = (along_row(here[2]) - dz[1], dz[0] - dx[2], dx[1] - along_row(here[0]))
+    return electric_parts(current, here, r_ref[x])
+
+
+def edge_kernel(b_ref, r_ref, side_ref, far_ref, near_ref, place_ref, edge_ref):
+    edge = jnp.where((place_ref[0] & 1) == 0, b_ref.shape[1] - 1, 0)
+    made = electric_at(b_ref, r_ref, side_ref, far_ref, near_ref, place_ref, edge)
+    edge_ref[0], edge_ref[1] = made[1], made[2]
+
+
+def step_kernel(b_ref, r_ref, side_ref, far_ref, near_ref, place_ref, rows_ref, elec_ref):
     cells_x, cells_z = b_ref.shape[1], b_ref.shape[2]
     half = 0.5 * time_step
 
-    def at(x):
+    def make(x):
+        made = electric_at(b_ref, r_ref, side_ref, far_ref, near_ref, place_ref, x)
+        for c in range(3):
+            elec_ref[c, x] = made[c]
+
+    def step(x):
         here = [elec_ref[c, x] for c in range(3)]
         dz = [along_z(here[c], 0.0, 0.0) for c in range(2)]
         dx = [None] + [slope(*x_neighbours(elec_ref, None, None, c, x)) for c in (1, 2)]
@@ -185,7 +195,8 @@
         rows_ref[pl.ds(extra + 2, 1), :] = -half * here[0][:1]
         rows_ref[pl.ds(extra + 3, 1), :] = half * here[0][cells_z - 1 :]
 
-    over_x(cells_x, at)
+    over_x(cells_x, make)
+    over_x(cells_x, step)
 
 
 def split(value):
@@ -199,11 +210,11 @@
     return dot(lhs_high, rhs_high) + (dot(lhs_high, rhs_low) + dot(lhs_low, rhs_high))
 
 
-def mix_kernel(cells_x, cells_z, rows_ref, edge_ref, ymix_ref, gx_ref, out_ref, mixed):
+def mix_kernel(cells_x, cells_z, rows_ref, edge_ref, ymix_ref, place_ref, out_ref, mixed):
     cells_y = rows_ref.shape[1]
     halves = cells_y // LANES
     mixed[...] = full_dot(rows_ref[...], ymix_ref[...])
-    first = gx_ref[0] == 0
+    first = (place_ref[0] & 1) == 0
     factor = jnp.where(first, 0.5 * time_step, -0.5 * time_step)
     added = full_dot(edge_ref[...].reshape(2 * cells_z, cells_y), ymix_ref[...]) * factor
     edge = jnp.where(first, cells_x - 1, 0)
@@ -309,18 +320,22 @@
     total_z = cells_z * parts
     f32 = jnp.float32
     shape = lambda *sizes: jax.ShapeDtypeStruct(sizes, f32)
-    place = lax.axis_index("gx").astype(jnp.int32).reshape(1)
+    place = (lax.axis_index("gx") + 2 * (lax.axis_index("gz") & 1)).astype(jnp.int32).reshape(1)
     swap = lambda value: lax.ppermute(value, "gx", [(0, 1), (1, 0)])
 
-    up, down, side = pl.pallas_call(
+    far, near, side = pl.pallas_call(
         pack_kernel,
         out_shape=(shape(2 * cells_x, cells_y), shape(2 * cells_x, cells_y), shape(2, cells_z, cells_y)),
         in_specs=[VMEM, SMEM],
         out_specs=(VMEM, VMEM, VMEM),
         compiler_params=limit(6),
     )(b_field, place)
-    below = lax.ppermute(up, "gz", [(i, i + 1) for i in range(parts - 1)])
-    above = lax.ppermute(down, "gz", [(i + 1, i) for i in range(parts - 1)])
+    exchange = lambda value, low: lax.ppermute(
+        value,
+        "gz",
+        [pair for i in range(low, parts - 1, 2) for pair in ((i, i + 1), (i + 1, i))],
+    )
+    far, near = exchange(far, 1), exchange(near, 0)
     line = pl.pallas_call(
         line_matrix_kernel,
         out_shape=shape(total_z + parts, total_z),
@@ -328,23 +343,24 @@
         out_specs=VMEM,
         compiler_params=limit(4),
     )(zmix)
-    line, below = lax.optimization_barrier((line, below))
-    elec, edge = pl.pallas_call(
-        electric_kernel,
-        out_shape=(shape(*b_field.shape), shape(2, cells_z, cells_y)),
+    line, far = lax.optimization_barrier((line, far))
+    known = (b_field, resist, swap(side), far, near, place)
+    edge = pl.pallas_call(
+        edge_kernel,
+        out_shape=shape(2, cells_z, cells_y),
         in_specs=[VMEM] * 5 + [SMEM],
-        out_specs=(VMEM, VMEM),
-        compiler_params=limit(6),
-        cost_estimate=estimate(200.0 * b_field.size),
-    )(b_field, resist, swap(side), below, above, place)
+        out_specs=VMEM,
+        compiler_params=limit(6),
+    )(*known)
     rows = pl.pallas_call(
         step_kernel,
         out_shape=shape(3 * cells_x * cells_z + 4 * cells_x, cells_y),
-        in_specs=[VMEM] * 2,
+        in_specs=[VMEM] * 5 + [SMEM],
         out_specs=VMEM,
-        compiler_params=limit(6),
-        cost_estimate=estimate(200.0 * b_field.size),
-    )(b_field, elec)
+        scratch_shapes=[pltpu.VMEM(b_field.shape, f32)],
+        compiler_params=limit(6),
+        cost_estimate=estimate(400.0 * b_field.size),
+    )(*known)
     pairs = cells_x * (cells_y // LANES) // parts
     sent = pl.pallas_call(
         functools.partial(mix_kernel, cells_x, cells_z),

time: 66.1 us -> 62.5 us (0.946)
  waiting for transfers between devices: 4.97 us -> 2.32 us
  blocking collectives: 48.9 us -> 47.7 us
    ppermute x2, waiting for transfers between devices: 3.54 us -> 1.32 us  [kernel_form(): lax.ppermute(value, 'gz', [pair for i in range(low, parts - 1, 2) for pai...]
    all_to_all x1, blocking collectives: 27.3 us -> 26.1 us  [kernel_form(): lines = lax.all_to_all(sent, 'gz', split_axis=0, concat_axis=0, tiled=True)]
  transfers between devices with their start and end apart: 4 -> 4, of which waited for: 4 -> 3; matrix products, arithmetic and copies ran while one was open for 0% -> 0% of each run, Pallas kernels for 1% -> 2%
where the time goes in v8:
time: 62.5 us; the launch traced here: 62.2 us
  blocking collectives  47.7 us (76%)
  starting transfers between devices  6.64 us (11%)
  Pallas kernels  3.78 us (6%)
  waiting for transfers between devices  2.32 us (4%)
  local copies, waits for them, and re-layouts  1.07 us (2%)
  between operations  0.71 us (1%)
    all_to_all x1, blocking collectives, kernel_form(): lines = lax.all_to_all(sent, 'gz', split_axis=0, concat_axis=0, tiled=True)  26.1 us
    all_to_all x1, blocking collectives, kernel_form(): lax.all_to_all(product, 'gz', split_axis=0, concat_axis=0, tiled=True)  21.7 us
    ppermute x2, starting transfers between devices, kernel_form(): lax.ppermute(value, 'gz', [pair for i in range(low, parts - 1, 2) for pai...  6.56 us
    ppermute x2, waiting for transfers between devices, kernel_form(): lax.ppermute(value, 'gz', [pair for i in range(low, parts - 1, 2) for pai...  1.32 us
    pallas_call x1, Pallas kernels, kernel_form(): pl.pallas_call(functools.partial(finish_kernel, total_z ** (-0.5), cells_...  1.28 us
  transfers between devices with their start and end apart: 4, of which 3 were waited for; matrix products, arithmetic and copies ran while one was open for 0% of the time, Pallas kernels for 2%

profile of v8, /device:TPU:0, one launch (start us, length us, event | category | flops | bytes accessed | tf_op | source)
XLA Modules:
  0.0 62.2 jit_solution(18177099764991256900)
XLA Ops:
  0.6 0.0 copy-start
  0.6 1.1 %copy-done = f32[3,24,8,256]{3,2,1,0:T(8,128)S(1)} copy-done((f32[3,24,8,256]{3,2,1,0:T(8,128)S(1)}, f32[3,24,8,256]{3,2,1,0:T(8,128)}, u32[]{:S(2)}) %copy-start) | copy-done | bytes 589848
  1.7 0.0 copy-start.3
  1.7 0.0 copy-start.1
  1.7 0.1 shard_map.59
  1.8 0.8 %collective-permute-start.1 = (f32[48,256]{1,0:T(8,128)S(1)}, f32[48,256]{1,0:T(8,128)S(1)}, u32[]{:S(2)}, u32[]{:S(2)}) collective-permute-start(f32[48,256]{1,0:T(8,128)S(1)} %get-tuple-element.8), channel_id=1, source_target_pairs={{2,4},{4,2},{6,8},{8,6},{10,12},{12,10},{14,16},{16,14},{18,20},{2... | collective-permute-start | bytes 147464 | tf_op jit(solution)/shard_map/ppermute | solution.py:333
  2.6 5.8 %collective-permute-start.2 = (f32[48,256]{1,0:T(8,128)S(1)}, f32[48,256]{1,0:T(8,128)S(1)}, u32[]{:S(2)}, u32[]{:S(2)}) collective-permute-start(f32[48,256]{1,0:T(8,128)S(1)} %get-tuple-element.10), channel_id=1, source_target_pairs={{0,2},{2,0},{4,6},{6,4},{8,10},{10,8},{12,14},{14,12},{16,18},{18,... | collective-permute-start | bytes 147464 | tf_op jit(solution)/shard_map/ppermute | solution.py:333
  8.3 0.0 collective-permute-start
  8.3 0.0 copy-done.3
  8.3 0.2 shard_map.60.line_ref
  8.6 0.0 collective-permute-done.1.far_ref
  8.6 0.9 %collective-permute-done.side_ref = f32[2,8,256]{2,1,0:T(8,128)S(1)} collective-permute-done((f32[2,8,256]{2,1,0:T(8,128)S(1)}, f32[2,8,256]{2,1,0:T(8,128)S(1)}, u32[]{:S(2)}, u32[]{:S(2)}) %collective-permute-start) | collective-permute-done | bytes 16416 | tf_op jit(solution)/shard_map/ppermute | solution.py:324
  9.5 1.3 %collective-permute-done.2.near_ref = f32[48,256]{1,0:T(8,128)S(1)} collective-permute-done((f32[48,256]{1,0:T(8,128)S(1)}, f32[48,256]{1,0:T(8,128)S(1)}, u32[]{:S(2)}, u32[]{:S(2)}) %collective-permute-start.2) | collective-permute-done | bytes 49184 | tf_op jit(solution)/shard_map/ppermute | solution.py:333
  10.8 0.0 copy-done.1
  10.8 0.1 shard_map.62
  10.9 0.0 copy-start.2
  10.9 0.1 collective-permute-start.3
  11.0 1.1 %shard_map.61.rows_ref = f32[672,256]{1,0:T(8,128)S(1)} custom-call(f32[3,24,8,256]{3,2,1,0:T(8,128)S(1)} %copy-done, f32[24,8,256]{2,1,0:T(8,128)S(1)} %copy-done.1, f32[2,8,256]{2,1,0:T(8,128)S(1)} %collective-permute-done.side_ref, f32[48,256]{1,0:T(8,128)S(1)} %collective-permute-done.1.far_ref, f32[48,256]{1,0:T(8,128)S(1)} %collective-permute-done.2.near_ref, ...), custom_call_target="tpu_custom_call" | custom-call | flops 58982400 | tf_op jit(solution)/shard_map/pallas_call | solution.py:355
  12.1 0.1 collective-permute-done.3.edge_ref
  12.2 0.0 copy-done.2
  12.2 0.5 shard_map.63
  12.7 26.1 %all_to_all.10.in_ref = f32[16,21,4,128]{3,2,1,0:T(4,128)S(1)} all-to-all(f32[16,21,4,128]{3,2,1,0:T(4,128)S(1)} %shard_map.63), channel_id=1, replica_groups=mesh['gz'=16,'gx'=2] {'gz'}, dimensions={0} | all-to-all | bytes 1376256 | tf_op jit(solution)/shard_map/all_to_all | solution.py:373
  38.8 0.5 shard_map.64
  39.3 21.7 %all_to_all.11.in_ref = f32[16,21,4,128]{3,2,1,0:T(4,128)S(1)} all-to-all(f32[16,21,4,128]{3,2,1,0:T(4,128)S(1)} %shard_map.64), channel_id=1, replica_groups=mesh['gz'=16,'gx'=2] {'gz'}, dimensions={0} | all-to-all | bytes 1376256 | tf_op jit(solution)/shard_map/all_to_all | solution.py:381
  61.0 1.3 %shard_map.65 = (f32[3,24,8,256]{3,2,1,0:T(8,128)}, f32[3,24,8,256]{3,2,1,0:T(8,128)}) custom-call(f32[16,21,4,128]{3,2,1,0:T(4,128)S(1)} %all_to_all.11.in_ref), custom_call_target="tpu_custom_call" | custom-call | tf_op jit(solution)/shard_map/pallas_call | solution.py:384
Async XLA Ops:
  0.6 1.1 %copy-start = (f32[3,24,8,256]{3,2,1,0:T(8,128)S(1)}, f32[3,24,8,256]{3,2,1,0:T(8,128)}, u32[]{:S(2)}) copy-start(f32[3,24,8,256]{3,2,1,0:T(8,128)} %b_ref.5) | copy-start | bytes 1769476
  1.7 6.6 %copy-start.3 = (f32[128,128]{1,0:T(8,128)S(1)}, f32[128,128]{1,0:T(8,128)}, u32[]{:S(2)}) copy-start(f32[128,128]{1,0:T(8,128)} %zmix_ref.1) | copy-start | bytes 196612
  1.7 9.1 %copy-start.1 = (f32[24,8,256]{2,1,0:T(8,128)S(1)}, f32[24,8,256]{2,1,0:T(8,128)}, u32[]{:S(2)}) copy-start(f32[24,8,256]{2,1,0:T(8,128)} %r_ref.3) | copy-start | bytes 589828
  1.8 6.8 %collective-permute-start.1 = (f32[48,256]{1,0:T(8,128)S(1)}, f32[48,256]{1,0:T(8,128)S(1)}, u32[]{:S(2)}, u32[]{:S(2)}) collective-permute-start(f32[48,256]{1,0:T(8,128)S(1)} %get-tuple-element.8), channel_id=1, source_target_pairs={{2,4},{4,2},{6,8},{8,6},{10,12},{12,10},{14,16},{16,14},{18,20},{2... | collective-permute-start | bytes 147464 | tf_op jit(solution)/shard_map/ppermute | solution.py:333
  2.6 8.3 %collective-permute-start.2 = (f32[48,256]{1,0:T(8,128)S(1)}, f32[48,256]{1,0:T(8,128)S(1)}, u32[]{:S(2)}, u32[]{:S(2)}) collective-permute-start(f32[48,256]{1,0:T(8,128)S(1)} %get-tuple-element.10), channel_id=1, source_target_pairs={{0,2},{2,0},{4,6},{6,4},{8,10},{10,8},{12,14},{14,12},{16,18},{18,... | collective-permute-start | bytes 147464 | tf_op jit(solution)/shard_map/ppermute | solution.py:333
  8.3 1.2 %collective-permute-start = (f32[2,8,256]{2,1,0:T(8,128)S(1)}, f32[2,8,256]{2,1,0:T(8,128)S(1)}, u32[]{:S(2)}, u32[]{:S(2)}) collective-permute-start(f32[2,8,256]{2,1,0:T(8,128)S(1)} %get-tuple-element.7), channel_id=1, source_target_pairs={{0,1},{1,0},{2,3},{3,2},{4,5},{5,4},{6,7},{7,6},{8,9},{9,8},{10,11... | collective-permute-start | bytes 49160 | tf_op jit(solution)/shard_map/ppermute | solution.py:324
  10.9 1.3 %copy-start.2 = (f32[256,256]{1,0:T(8,128)S(1)}, f32[256,256]{1,0:T(8,128)}, u32[]{:S(2)}) copy-start(f32[256,256]{1,0:T(8,128)} %ymix_ref.1) | copy-start | bytes 786436
  10.9 1.2 %collective-permute-start.3 = (f32[2,8,256]{2,1,0:T(8,128)S(1)}, f32[2,8,256]{2,1,0:T(8,128)S(1)}, u32[]{:S(2)}, u32[]{:S(2)}) collective-permute-start(f32[2,8,256]{2,1,0:T(8,128)S(1)} %shard_map.62), channel_id=1, source_target_pairs={{0,1},{1,0},{2,3},{3,2},{4,5},{5,4},{6,7},{7,6},{8,9},{9,8},{10,11... | collective-permute-start | bytes 49160 | tf_op jit(solution)/shard_map/ppermute | solution.py:324

commit v9 on v8

--- a/solution.py
+++ b/solution.py
@@ -12,7 +12,7 @@
 SUBLANES = 8
 SHORT = 4
 PIECES = 3
-BATCH = 6
+BATCH = 11
 VMEM = pl.BlockSpec(memory_space=pltpu.VMEM)
 SMEM = pl.BlockSpec(memory_space=pltpu.SMEM)
 
@@ -113,42 +113,57 @@
 
 
 def over_x(cells_x, body):
+    batch = next(size for size in range(BATCH, 0, -1) if (cells_x - 2) % size == 0)
+
     def trip(i, carry):
-        for j in range(BATCH):
-            body(i * BATCH + j)
+        for j in range(batch):
+            body(1 + i * batch + j)
         return carry
 
-    lax.fori_loop(0, cells_x // BATCH, trip, 0)
-
-
-def pack_kernel(b_ref, place_ref, far_ref, near_ref, side_ref):
+    lax.fori_loop(0, (cells_x - 2) // batch, trip, 0)
+    body(0)
+    body(cells_x - 1)
+
+
+def pack_kernel(b_ref, place_ref, far_ref, near_ref, side_ref, held, sems):
     cells_x, cells_z = b_ref.shape[1], b_ref.shape[2]
     edge = jnp.where((place_ref[0] & 1) == 0, cells_x - 1, 0)
     odd = place_ref[0] >= 2
     far_row = jnp.where(odd, cells_z - 1, 0)
     near_row = jnp.where(odd, 0, cells_z - 1)
+    batch = cells_x // PIECES
+    copies = [
+        pltpu.make_async_copy(
+            b_ref.at[c, pl.ds(i * batch, batch)], held.at[c, pl.ds(i * batch, batch)], sems.at[c, i]
+        )
+        for c in range(2)
+        for i in range(PIECES)
+    ]
+    copies.append(pltpu.make_async_copy(b_ref.at[pl.ds(1, 2), edge], side_ref, sems.at[2, 0]))
+    for copy in copies:
+        copy.start()
+    for copy in copies:
+        copy.wait()
     for c in range(2):
-        side_ref[c] = b_ref[c + 1, edge]
         for x in range(cells_x):
             at = pl.ds(c * cells_x + x, 1)
-            far_ref[at, :] = b_ref[c, x, pl.ds(far_row, 1), :]
-            near_ref[at, :] = b_ref[c, x, pl.ds(near_row, 1), :]
-
-
-def x_neighbours(ref, side_ref, first, c, x):
-    cells_x = ref.shape[1]
-    after = ref[c, jnp.minimum(x + 1, cells_x - 1)]
-    before = ref[c, jnp.maximum(x - 1, 0)]
-    zero = jnp.zeros_like(after)
-    if side_ref is None:
-        past_end, past_start = zero, zero
-    else:
-        side = side_ref[c - 1]
-        past_end, past_start = jnp.where(first, side, zero), jnp.where(first, zero, side)
-    return (
-        jnp.where(x == cells_x - 1, past_end, after),
-        jnp.where(x == 0, past_start, before),
-    )
+            far_ref[at, :] = held[c, x, pl.ds(far_row, 1), :]
+            near_ref[at, :] = held[c, x, pl.ds(near_row, 1), :]
+
+
+def x_slope(ref, side_ref, first, c, x):
+    last = ref.shape[1] - 1
+
+    def beyond(mine):
+        if side_ref is None:
+            return 0.0
+        return jnp.where(mine, side_ref[c - 1], 0.0)
+
+    if isinstance(x, int) and x == 0:
+        return slope(ref[c, 1], beyond(jnp.logical_not(first) if side_ref is not None else None))
+    if isinstance(x, int) and x == last:
+        return slope(beyond(first), ref[c, last - 1])
+    return slope(ref[c, x + 1], ref[c, x - 1])
 
 
 def electric_at(b_ref, r_ref, side_ref, far_ref, near_ref, place_ref, x):
@@ -161,15 +176,17 @@
         far, near = far_ref[at, :], near_ref[at, :]
         dz.append(along_z(here[c], jnp.where(odd, far, near), jnp.where(odd, near, far)))
     first = (place_ref[0] & 1) == 0
-    dx = [None] + [slope(*x_neighbours(b_ref, side_ref, first, c, x)) for c in (1, 2)]
+    dx = [None] + [x_slope(b_ref, side_ref, first, c, x) for c in (1, 2)]
     current = (along_row(here[2]) - dz[1], dz[0] - dx[2], dx[1] - along_row(here[0]))
     return electric_parts(current, here, r_ref[x])
 
 
 def edge_kernel(b_ref, r_ref, side_ref, far_ref, near_ref, place_ref, edge_ref):
-    edge = jnp.where((place_ref[0] & 1) == 0, b_ref.shape[1] - 1, 0)
-    made = electric_at(b_ref, r_ref, side_ref, far_ref, near_ref, place_ref, edge)
-    edge_ref[0], edge_ref[1] = made[1], made[2]
+    known = (b_ref, r_ref, side_ref, far_ref, near_ref, place_ref)
+    low, high = electric_at(*known, 0), electric_at(*known, b_ref.shape[1] - 1)
+    first = (place_ref[0] & 1) == 0
+    for c in range(2):
+        edge_ref[c] = jnp.where(first, high[c + 1], low[c + 1])
 
 
 def step_kernel(b_ref, r_ref, side_ref, far_ref, near_ref, place_ref, rows_ref, elec_ref):
@@ -184,7 +201,7 @@
     def step(x):
         here = [elec_ref[c, x] for c in range(3)]
         dz = [along_z(here[c], 0.0, 0.0) for c in range(2)]
-        dx = [None] + [slope(*x_neighbours(elec_ref, None, None, c, x)) for c in (1, 2)]
+        dx = [None] + [x_slope(elec_ref, None, None, c, x) for c in (1, 2)]
         curl = (along_row(here[2]) - dz[1], dz[0] - dx[2], dx[1] - along_row(here[0]))
         for c in range(3):
             start = pl.multiple_of((c * cells_x + x) * cells_z, cells_z)
@@ -326,10 +343,14 @@
     far, near, side = pl.pallas_call(
         pack_kernel,
         out_shape=(shape(2 * cells_x, cells_y), shape(2 * cells_x, cells_y), shape(2, cells_z, cells_y)),
-        in_specs=[VMEM, SMEM],
+        in_specs=[pl.BlockSpec(memory_space=pltpu.HBM), SMEM],
         out_specs=(VMEM, VMEM, VMEM),
-        compiler_params=limit(6),
-    )(b_field, place)
+        scratch_shapes=[
+            pltpu.VMEM((2,) + b_field.shape[1:], f32),
+            pltpu.SemaphoreType.DMA((3, PIECES)),
+        ],
+        compiler_params=limit(6),
+    )(pltpu.with_memory_space_constraint(b_field, pltpu.HBM), place)
     exchange = lambda value, low: lax.ppermute(
         value,
         "gz",
@@ -407,7 +428,7 @@
         and cells_z == SUBLANES
         and cells_x % PIECES == 0
         and cells_y % LANES == 0
-        and cells_x % BATCH == 0
+        and cells_x >= 4
         and cells_x * (cells_y // LANES) % parts == 0
     )
     return (kernel_form if fits else plain_form)(b_field, resist, ymix, zmix)

time: 62.5 us -> 63.3 us (1.013)
  Pallas kernels: 3.78 us -> 4.81 us
  waiting for transfers between devices: 2.32 us -> 1.59 us
  local copies, waits for them, and re-layouts: 1.07 us -> 1.78 us
    pallas_call x1, Pallas kernels: 0.05 us -> 1.19 us  [kernel_form(): pl.pallas_call(pack_kernel, out_shape=(shape(2 * cells_x, cells_y), shape...]
    ppermute x2, waiting for transfers between devices: 1 us -> 0.27 us  [kernel_form(): swap = lambda value: lax.ppermute(value, 'gx', [(0, 1), (1, 0)])]
    unnamed x8, local copies, waits for them, and re-layouts: 1.07 us -> 1.78 us
where the time goes in v9:
time: 63.3 us; the launch traced here: 63 us
  blocking collectives  47.6 us (75%)
  starting transfers between devices  6.51 us (10%)
  Pallas kernels  4.81 us (8%)
  local copies, waits for them, and re-layouts  1.78 us (3%)
  waiting for transfers between devices  1.59 us (3%)
  between operations  0.71 us (1%)
    all_to_all x1, blocking collectives, kernel_form(): lines = lax.all_to_all(sent, 'gz', split_axis=0, concat_axis=0, tiled=True)  26 us
    all_to_all x1, blocking collectives, kernel_form(): lax.all_to_all(product, 'gz', split_axis=0, concat_axis=0, tiled=True)  21.7 us
    ppermute x2, starting transfers between devices, kernel_form(): lax.ppermute(value, 'gz', [pair for i in range(low, parts - 1, 2) for pai...  6.43 us
    unnamed x8, local copies, waits for them, and re-layouts  1.78 us
    ppermute x2, waiting for transfers between devices, kernel_form(): lax.ppermute(value, 'gz', [pair for i in range(low, parts - 1, 2) for pai...  1.32 us
    pallas_call x1, Pallas kernels, kernel_form(): pl.pallas_call(functools.partial(finish_kernel, total_z ** (-0.5), cells_...  1.28 us
  transfers between devices with their start and end apart: 4, of which 3 were waited for; matrix products, arithmetic and copies ran while one was open for 0% of the time, Pallas kernels for 2%

profile of v9, /device:TPU:0, one launch (start us, length us, event | category | flops | bytes accessed | tf_op | source)
XLA Modules:
  0.0 63.0 jit_solution(2546203955278463460)
XLA Ops:
  0.6 0.0 copy-start
  0.6 1.2 %shard_map.59 = (f32[48,256]{1,0:T(8,128)S(1)}, f32[48,256]{1,0:T(8,128)S(1)}, f32[2,8,256]{2,1,0:T(8,128)S(1)}) custom-call(f32[3,24,8,256]{3,2,1,0:T(8,128)} %b_ref.5, s32[1]{0:T(128)} %bitcast.place_ref), custom_call_target="tpu_custom_call" | custom-call | tf_op jit(solution)/shard_map/pallas_call | solution.py:343
  1.8 0.7 %collective-permute-start.1 = (f32[48,256]{1,0:T(8,128)S(1)}, f32[48,256]{1,0:T(8,128)S(1)}, u32[]{:S(2)}, u32[]{:S(2)}) collective-permute-start(f32[48,256]{1,0:T(8,128)S(1)} %get-tuple-element.8), channel_id=1, source_target_pairs={{2,4},{4,2},{6,8},{8,6},{10,12},{12,10},{14,16},{16,14},{18,20},{2... | collective-permute-start | bytes 147464 | tf_op jit(solution)/shard_map/ppermute | solution.py:354
  2.5 5.8 %collective-permute-start.2 = (f32[48,256]{1,0:T(8,128)S(1)}, f32[48,256]{1,0:T(8,128)S(1)}, u32[]{:S(2)}, u32[]{:S(2)}) collective-permute-start(f32[48,256]{1,0:T(8,128)S(1)} %get-tuple-element.10), channel_id=1, source_target_pairs={{0,2},{2,0},{4,6},{6,4},{8,10},{10,8},{12,14},{14,12},{16,18},{18,... | collective-permute-start | bytes 147464 | tf_op jit(solution)/shard_map/ppermute | solution.py:354
  8.3 0.0 collective-permute-start
  8.3 0.0 copy-start.3
  8.3 0.8 %copy-done.3 = f32[128,128]{1,0:T(8,128)S(1)} copy-done((f32[128,128]{1,0:T(8,128)S(1)}, f32[128,128]{1,0:T(8,128)}, u32[]{:S(2)}) %copy-start.3) | copy-done | bytes 65560
  9.1 0.2 shard_map.60.line_ref
  9.4 0.0 collective-permute-done.1.far_ref
  9.4 0.1 collective-permute-done.side_ref
  9.5 1.3 %collective-permute-done.2.near_ref = f32[48,256]{1,0:T(8,128)S(1)} collective-permute-done((f32[48,256]{1,0:T(8,128)S(1)}, f32[48,256]{1,0:T(8,128)S(1)}, u32[]{:S(2)}, u32[]{:S(2)}) %collective-permute-start.2) | collective-permute-done | bytes 49184 | tf_op jit(solution)/shard_map/ppermute | solution.py:354
  10.8 0.0 copy-done
  10.8 0.0 copy-start.1
  10.8 0.9 %copy-done.1 = f32[24,8,256]{2,1,0:T(8,128)S(1)} copy-done((f32[24,8,256]{2,1,0:T(8,128)S(1)}, f32[24,8,256]{2,1,0:T(8,128)}, u32[]{:S(2)}) %copy-start.1) | copy-done | bytes 196632
  11.7 0.1 shard_map.62
  11.8 0.0 copy-start.2
  11.8 0.1 collective-permute-start.3
  11.9 1.0 %shard_map.61.rows_ref = f32[672,256]{1,0:T(8,128)S(1)} custom-call(f32[3,24,8,256]{3,2,1,0:T(8,128)S(1)} %copy-done, f32[24,8,256]{2,1,0:T(8,128)S(1)} %copy-done.1, f32[2,8,256]{2,1,0:T(8,128)S(1)} %collective-permute-done.side_ref, f32[48,256]{1,0:T(8,128)S(1)} %collective-permute-done.1.far_ref, f32[48,256]{1,0:T(8,128)S(1)} %collective-permute-done.2.near_ref, ...), custom_call_target="tpu_custom_call" | custom-call | flops 58982400 | tf_op jit(solution)/shard_map/pallas_call | solution.py:376
  12.9 0.2 collective-permute-done.3.edge_ref
  13.1 0.0 copy-done.2
  13.1 0.5 shard_map.63
  13.6 26.0 %all_to_all.10.in_ref = f32[16,21,4,128]{3,2,1,0:T(4,128)S(1)} all-to-all(f32[16,21,4,128]{3,2,1,0:T(4,128)S(1)} %shard_map.63), channel_id=1, replica_groups=mesh['gz'=16,'gx'=2] {'gz'}, dimensions={0} | all-to-all | bytes 1376256 | tf_op jit(solution)/shard_map/all_to_all | solution.py:394
  39.6 0.5 shard_map.64
  40.1 21.7 %all_to_all.11.in_ref = f32[16,21,4,128]{3,2,1,0:T(4,128)S(1)} all-to-all(f32[16,21,4,128]{3,2,1,0:T(4,128)S(1)} %shard_map.64), channel_id=1, replica_groups=mesh['gz'=16,'gx'=2] {'gz'}, dimensions={0} | all-to-all | bytes 1376256 | tf_op jit(solution)/shard_map/all_to_all | solution.py:402
  61.7 1.3 %shard_map.65 = (f32[3,24,8,256]{3,2,1,0:T(8,128)}, f32[3,24,8,256]{3,2,1,0:T(8,128)}) custom-call(f32[16,21,4,128]{3,2,1,0:T(4,128)S(1)} %all_to_all.11.in_ref), custom_call_target="tpu_custom_call" | custom-call | tf_op jit(solution)/shard_map/pallas_call | solution.py:405
Async XLA Ops:
  0.6 10.2 %copy-start = (f32[3,24,8,256]{3,2,1,0:T(8,128)S(1)}, f32[3,24,8,256]{3,2,1,0:T(8,128)}, u32[]{:S(2)}) copy-start(f32[3,24,8,256]{3,2,1,0:T(8,128)} %b_ref.5) | copy-start | bytes 1769476
  1.8 7.5 %collective-permute-start.1 = (f32[48,256]{1,0:T(8,128)S(1)}, f32[48,256]{1,0:T(8,128)S(1)}, u32[]{:S(2)}, u32[]{:S(2)}) collective-permute-start(f32[48,256]{1,0:T(8,128)S(1)} %get-tuple-element.8), channel_id=1, source_target_pairs={{2,4},{4,2},{6,8},{8,6},{10,12},{12,10},{14,16},{16,14},{18,20},{2... | collective-permute-start | bytes 147464 | tf_op jit(solution)/shard_map/ppermute | solution.py:354
  2.5 8.3 %collective-permute-start.2 = (f32[48,256]{1,0:T(8,128)S(1)}, f32[48,256]{1,0:T(8,128)S(1)}, u32[]{:S(2)}, u32[]{:S(2)}) collective-permute-start(f32[48,256]{1,0:T(8,128)S(1)} %get-tuple-element.10), channel_id=1, source_target_pairs={{0,2},{2,0},{4,6},{6,4},{8,10},{10,8},{12,14},{14,12},{16,18},{18,... | collective-permute-start | bytes 147464 | tf_op jit(solution)/shard_map/ppermute | solution.py:354
  8.3 1.2 %collective-permute-start = (f32[2,8,256]{2,1,0:T(8,128)S(1)}, f32[2,8,256]{2,1,0:T(8,128)S(1)}, u32[]{:S(2)}, u32[]{:S(2)}) collective-permute-start(f32[2,8,256]{2,1,0:T(8,128)S(1)} %get-tuple-element.7), channel_id=1, source_target_pairs={{0,1},{1,0},{2,3},{3,2},{4,5},{5,4},{6,7},{7,6},{8,9},{9,8},{10,11... | collective-permute-start | bytes 49160 | tf_op jit(solution)/shard_map/ppermute | solution.py:341
  8.3 0.8 %copy-start.3 = (f32[128,128]{1,0:T(8,128)S(1)}, f32[128,128]{1,0:T(8,128)}, u32[]{:S(2)}) copy-start(f32[128,128]{1,0:T(8,128)} %zmix_ref.1) | copy-start | bytes 196612
  10.8 0.9 %copy-start.1 = (f32[24,8,256]{2,1,0:T(8,128)S(1)}, f32[24,8,256]{2,1,0:T(8,128)}, u32[]{:S(2)}) copy-start(f32[24,8,256]{2,1,0:T(8,128)} %r_ref.3) | copy-start | bytes 589828
  11.8 1.3 %copy-start.2 = (f32[256,256]{1,0:T(8,128)S(1)}, f32[256,256]{1,0:T(8,128)}, u32[]{:S(2)}) copy-start(f32[256,256]{1,0:T(8,128)} %ymix_ref.1) | copy-start | bytes 786436
  11.8 1.2 %collective-permute-start.3 = (f32[2,8,256]{2,1,0:T(8,128)S(1)}, f32[2,8,256]{2,1,0:T(8,128)S(1)}, u32[]{:S(2)}, u32[]{:S(2)}) collective-permute-start(f32[2,8,256]{2,1,0:T(8,128)S(1)} %shard_map.62), channel_id=1, source_target_pairs={{0,1},{1,0},{2,3},{3,2},{4,5},{5,4},{6,7},{7,6},{8,9},{9,8},{10,11... | collective-permute-start | bytes 49160 | tf_op jit(solution)/shard_map/ppermute | solution.py:341

commit v10 on v9

--- a/solution.py
+++ b/solution.py
@@ -11,7 +11,7 @@
 LANES = 128
 SUBLANES = 8
 SHORT = 4
-PIECES = 3
+PIECES = 6
 BATCH = 11
 VMEM = pl.BlockSpec(memory_space=pltpu.VMEM)
 SMEM = pl.BlockSpec(memory_space=pltpu.SMEM)
@@ -125,30 +125,18 @@
     body(cells_x - 1)
 
 
-def pack_kernel(b_ref, place_ref, far_ref, near_ref, side_ref, held, sems):
+def pack_kernel(b_ref, place_ref, far_ref, near_ref, side_ref):
     cells_x, cells_z = b_ref.shape[1], b_ref.shape[2]
     edge = jnp.where((place_ref[0] & 1) == 0, cells_x - 1, 0)
     odd = place_ref[0] >= 2
     far_row = jnp.where(odd, cells_z - 1, 0)
     near_row = jnp.where(odd, 0, cells_z - 1)
-    batch = cells_x // PIECES
-    copies = [
-        pltpu.make_async_copy(
-            b_ref.at[c, pl.ds(i * batch, batch)], held.at[c, pl.ds(i * batch, batch)], sems.at[c, i]
-        )
-        for c in range(2)
-        for i in range(PIECES)
-    ]
-    copies.append(pltpu.make_async_copy(b_ref.at[pl.ds(1, 2), edge], side_ref, sems.at[2, 0]))
-    for copy in copies:
-        copy.start()
-    for copy in copies:
-        copy.wait()
     for c in range(2):
+        side_ref[c] = b_ref[c + 1, edge]
         for x in range(cells_x):
             at = pl.ds(c * cells_x + x, 1)
-            far_ref[at, :] = held[c, x, pl.ds(far_row, 1), :]
-            near_ref[at, :] = held[c, x, pl.ds(near_row, 1), :]
+            far_ref[at, :] = b_ref[c, x, pl.ds(far_row, 1), :]
+            near_ref[at, :] = b_ref[c, x, pl.ds(near_row, 1), :]
 
 
 def x_slope(ref, side_ref, first, c, x):
@@ -343,14 +331,10 @@
     far, near, side = pl.pallas_call(
         pack_kernel,
         out_shape=(shape(2 * cells_x, cells_y), shape(2 * cells_x, cells_y), shape(2, cells_z, cells_y)),
-        in_specs=[pl.BlockSpec(memory_space=pltpu.HBM), SMEM],
+        in_specs=[VMEM, SMEM],
         out_specs=(VMEM, VMEM, VMEM),
-        scratch_shapes=[
-            pltpu.VMEM((2,) + b_field.shape[1:], f32),
-            pltpu.SemaphoreType.DMA((3, PIECES)),
-        ],
-        compiler_params=limit(6),
-    )(pltpu.with_memory_space_constraint(b_field, pltpu.HBM), place)
+        compiler_params=limit(6),
+    )(b_field, place)
     exchange = lambda value, low: lax.ppermute(
         value,
         "gz",

time: 63.3 us -> 62.5 us (0.987)
  Pallas kernels: 4.81 us -> 3.81 us
  waiting for transfers between devices: 1.59 us -> 2.43 us
  local copies, waits for them, and re-layouts: 1.78 us -> 1.07 us
    pallas_call x1, Pallas kernels: 1.19 us -> 0.05 us  [kernel_form(): pl.pallas_call(pack_kernel, out_shape=(shape(2 * cells_x, cells_y), shape...]
    ppermute x2, waiting for transfers between devices: 0.27 us -> 1.11 us  [kernel_form(): swap = lambda value: lax.ppermute(value, 'gx', [(0, 1), (1, 0)])]
    unnamed x8, local copies, waits for them, and re-layouts: 1.78 us -> 1.07 us
where the time goes in v10:
time: 62.5 us; the launch traced here: 62.3 us
  blocking collectives  47.6 us (76%)
  starting transfers between devices  6.64 us (11%)
  Pallas kernels  3.81 us (6%)
  waiting for transfers between devices  2.43 us (4%)
  local copies, waits for them, and re-layouts  1.07 us (2%)
  between operations  0.7 us (1%)
    all_to_all x1, blocking collectives, kernel_form(): lines = lax.all_to_all(sent, 'gz', split_axis=0, concat_axis=0, tiled=True)  26 us
    all_to_all x1, blocking collectives, kernel_form(): lax.all_to_all(product, 'gz', split_axis=0, concat_axis=0, tiled=True)  21.7 us
    ppermute x2, starting transfers between devices, kernel_form(): lax.ppermute(value, 'gz', [pair for i in range(low, parts - 1, 2) for pai...  6.56 us
    pallas_call x1, Pallas kernels, kernel_form(): pl.pallas_call(functools.partial(finish_kernel, total_z ** (-0.5), cells_...  1.41 us
    ppermute x2, waiting for transfers between devices, kernel_form(): lax.ppermute(value, 'gz', [pair for i in range(low, parts - 1, 2) for pai...  1.32 us
  transfers between devices with their start and end apart: 4, of which 3 were waited for; matrix products, arithmetic and copies ran while one was open for 0% of the time, Pallas kernels for 2%

profile of v10, /device:TPU:0, one launch (start us, length us, event | category | flops | bytes accessed | tf_op | source)
XLA Modules:
  0.0 62.3 jit_solution(14104133129489121463)
XLA Ops:
  0.6 0.0 copy-start
  0.6 1.1 %copy-done = f32[3,24,8,256]{3,2,1,0:T(8,128)S(1)} copy-done((f32[3,24,8,256]{3,2,1,0:T(8,128)S(1)}, f32[3,24,8,256]{3,2,1,0:T(8,128)}, u32[]{:S(2)}) %copy-start) | copy-done | bytes 589848
  1.7 0.0 copy-start.3
  1.7 0.0 copy-start.1
  1.7 0.1 shard_map.59
  1.8 0.8 %collective-permute-start.1 = (f32[48,256]{1,0:T(8,128)S(1)}, f32[48,256]{1,0:T(8,128)S(1)}, u32[]{:S(2)}, u32[]{:S(2)}) collective-permute-start(f32[48,256]{1,0:T(8,128)S(1)} %get-tuple-element.8), channel_id=1, source_target_pairs={{2,4},{4,2},{6,8},{8,6},{10,12},{12,10},{14,16},{16,14},{18,20},{2... | collective-permute-start | bytes 147464 | tf_op jit(solution)/shard_map/ppermute | solution.py:338
  2.6 5.8 %collective-permute-start.2 = (f32[48,256]{1,0:T(8,128)S(1)}, f32[48,256]{1,0:T(8,128)S(1)}, u32[]{:S(2)}, u32[]{:S(2)}) collective-permute-start(f32[48,256]{1,0:T(8,128)S(1)} %get-tuple-element.10), channel_id=1, source_target_pairs={{0,2},{2,0},{4,6},{6,4},{8,10},{10,8},{12,14},{14,12},{16,18},{18,... | collective-permute-start | bytes 147464 | tf_op jit(solution)/shard_map/ppermute | solution.py:338
  8.3 0.0 collective-permute-start
  8.3 0.0 copy-done.3
  8.3 0.2 shard_map.60.line_ref
  8.6 0.0 collective-permute-done.1.far_ref
  8.6 0.9 %collective-permute-done.side_ref = f32[2,8,256]{2,1,0:T(8,128)S(1)} collective-permute-done((f32[2,8,256]{2,1,0:T(8,128)S(1)}, f32[2,8,256]{2,1,0:T(8,128)S(1)}, u32[]{:S(2)}, u32[]{:S(2)}) %collective-permute-start) | collective-permute-done | bytes 16416 | tf_op jit(solution)/shard_map/ppermute | solution.py:329
  9.5 1.3 %collective-permute-done.2.near_ref = f32[48,256]{1,0:T(8,128)S(1)} collective-permute-done((f32[48,256]{1,0:T(8,128)S(1)}, f32[48,256]{1,0:T(8,128)S(1)}, u32[]{:S(2)}, u32[]{:S(2)}) %collective-permute-start.2) | collective-permute-done | bytes 49184 | tf_op jit(solution)/shard_map/ppermute | solution.py:338
  10.8 0.0 copy-done.1
  10.8 0.1 shard_map.62
  10.9 0.0 copy-start.2
  11.0 0.1 collective-permute-start.3
  11.0 1.0 %shard_map.61.rows_ref = f32[672,256]{1,0:T(8,128)S(1)} custom-call(f32[3,24,8,256]{3,2,1,0:T(8,128)S(1)} %copy-done, f32[24,8,256]{2,1,0:T(8,128)S(1)} %copy-done.1, f32[2,8,256]{2,1,0:T(8,128)S(1)} %collective-permute-done.side_ref, f32[48,256]{1,0:T(8,128)S(1)} %collective-permute-done.1.far_ref, f32[48,256]{1,0:T(8,128)S(1)} %collective-permute-done.2.near_ref, ...), custom_call_target="tpu_custom_call" | custom-call | flops 58982400 | tf_op jit(solution)/shard_map/pallas_call | solution.py:360
  12.0 0.2 collective-permute-done.3.edge_ref
  12.2 0.0 copy-done.2
  12.2 0.5 shard_map.63
  12.7 26.0 %all_to_all.10.in_ref = f32[16,21,4,128]{3,2,1,0:T(4,128)S(1)} all-to-all(f32[16,21,4,128]{3,2,1,0:T(4,128)S(1)} %shard_map.63), channel_id=1, replica_groups=mesh['gz'=16,'gx'=2] {'gz'}, dimensions={0} | all-to-all | bytes 1376256 | tf_op jit(solution)/shard_map/all_to_all | solution.py:378
  38.7 0.5 shard_map.64
  39.2 21.7 %all_to_all.11.in_ref = f32[16,21,4,128]{3,2,1,0:T(4,128)S(1)} all-to-all(f32[16,21,4,128]{3,2,1,0:T(4,128)S(1)} %shard_map.64), channel_id=1, replica_groups=mesh['gz'=16,'gx'=2] {'gz'}, dimensions={0} | all-to-all | bytes 1376256 | tf_op jit(solution)/shard_map/all_to_all | solution.py:386
  60.9 1.4 %shard_map.65 = (f32[3,24,8,256]{3,2,1,0:T(8,128)}, f32[3,24,8,256]{3,2,1,0:T(8,128)}) custom-call(f32[16,21,4,128]{3,2,1,0:T(4,128)S(1)} %all_to_all.11.in_ref), custom_call_target="tpu_custom_call" | custom-call | tf_op jit(solution)/shard_map/pallas_call | solution.py:389
Async XLA Ops:
  0.6 1.1 %copy-start = (f32[3,24,8,256]{3,2,1,0:T(8,128)S(1)}, f32[3,24,8,256]{3,2,1,0:T(8,128)}, u32[]{:S(2)}) copy-start(f32[3,24,8,256]{3,2,1,0:T(8,128)} %b_ref.5) | copy-start | bytes 1769476
  1.7 6.6 %copy-start.3 = (f32[128,128]{1,0:T(8,128)S(1)}, f32[128,128]{1,0:T(8,128)}, u32[]{:S(2)}) copy-start(f32[128,128]{1,0:T(8,128)} %zmix_ref.1) | copy-start | bytes 196612
  1.7 9.1 %copy-start.1 = (f32[24,8,256]{2,1,0:T(8,128)S(1)}, f32[24,8,256]{2,1,0:T(8,128)}, u32[]{:S(2)}) copy-start(f32[24,8,256]{2,1,0:T(8,128)} %r_ref.3) | copy-start | bytes 589828
  1.8 6.8 %collective-permute-start.1 = (f32[48,256]{1,0:T(8,128)S(1)}, f32[48,256]{1,0:T(8,128)S(1)}, u32[]{:S(2)}, u32[]{:S(2)}) collective-permute-start(f32[48,256]{1,0:T(8,128)S(1)} %get-tuple-element.8), channel_id=1, source_target_pairs={{2,4},{4,2},{6,8},{8,6},{10,12},{12,10},{14,16},{16,14},{18,20},{2... | collective-permute-start | bytes 147464 | tf_op jit(solution)/shard_map/ppermute | solution.py:338
  2.6 8.3 %collective-permute-start.2 = (f32[48,256]{1,0:T(8,128)S(1)}, f32[48,256]{1,0:T(8,128)S(1)}, u32[]{:S(2)}, u32[]{:S(2)}) collective-permute-start(f32[48,256]{1,0:T(8,128)S(1)} %get-tuple-element.10), channel_id=1, source_target_pairs={{0,2},{2,0},{4,6},{6,4},{8,10},{10,8},{12,14},{14,12},{16,18},{18,... | collective-permute-start | bytes 147464 | tf_op jit(solution)/shard_map/ppermute | solution.py:338
  8.3 1.2 %collective-permute-start = (f32[2,8,256]{2,1,0:T(8,128)S(1)}, f32[2,8,256]{2,1,0:T(8,128)S(1)}, u32[]{:S(2)}, u32[]{:S(2)}) collective-permute-start(f32[2,8,256]{2,1,0:T(8,128)S(1)} %get-tuple-element.7), channel_id=1, source_target_pairs={{0,1},{1,0},{2,3},{3,2},{4,5},{5,4},{6,7},{7,6},{8,9},{9,8},{10,11... | collective-permute-start | bytes 49160 | tf_op jit(solution)/shard_map/ppermute | solution.py:329
  10.9 1.3 %copy-start.2 = (f32[256,256]{1,0:T(8,128)S(1)}, f32[256,256]{1,0:T(8,128)}, u32[]{:S(2)}) copy-start(f32[256,256]{1,0:T(8,128)} %ymix_ref.1) | copy-start | bytes 786436
  11.0 1.2 %collective-permute-start.3 = (f32[2,8,256]{2,1,0:T(8,128)S(1)}, f32[2,8,256]{2,1,0:T(8,128)S(1)}, u32[]{:S(2)}, u32[]{:S(2)}) collective-permute-start(f32[2,8,256]{2,1,0:T(8,128)S(1)} %shard_map.62), channel_id=1, source_target_pairs={{0,1},{1,0},{2,3},{3,2},{4,5},{5,4},{6,7},{7,6},{8,9},{9,8},{10,11... | collective-permute-start | bytes 49160 | tf_op jit(solution)/shard_map/ppermute | solution.py:329

commit v11 on v10

--- a/solution.py
+++ b/solution.py
@@ -11,7 +11,7 @@
 LANES = 128
 SUBLANES = 8
 SHORT = 4
-PIECES = 6
+PIECES = 2
 BATCH = 11
 VMEM = pl.BlockSpec(memory_space=pltpu.VMEM)
 SMEM = pl.BlockSpec(memory_space=pltpu.SMEM)

time: 62.5 us -> 62.4 us (level)
  no operation moved by 1% of the time
where the time goes in v11:
time: 62.4 us; the launch traced here: 62.1 us
  blocking collectives  47.6 us (76%)
  starting transfers between devices  6.64 us (11%)
  Pallas kernels  3.64 us (6%)
  waiting for transfers between devices  2.43 us (4%)
  local copies, waits for them, and re-layouts  1.07 us (2%)
  between operations  0.7 us (1%)
    all_to_all x1, blocking collectives, kernel_form(): lines = lax.all_to_all(sent, 'gz', split_axis=0, concat_axis=0, tiled=True)  26 us
    all_to_all x1, blocking collectives, kernel_form(): lax.all_to_all(product, 'gz', split_axis=0, concat_axis=0, tiled=True)  21.7 us
    ppermute x2, starting transfers between devices, kernel_form(): lax.ppermute(value, 'gz', [pair for i in range(low, parts - 1, 2) for pai...  6.56 us
    ppermute x2, waiting for transfers between devices, kernel_form(): lax.ppermute(value, 'gz', [pair for i in range(low, parts - 1, 2) for pai...  1.32 us
  transfers between devices with their start and end apart: 4, of which 3 were waited for; matrix products, arithmetic and copies ran while one was open for 0% of the time, Pallas kernels for 2%

profile of v11, /device:TPU:0, one launch (start us, length us, event | category | flops | bytes accessed | tf_op | source)
XLA Modules:
  0.0 62.1 jit_solution(18342301420561633510)
XLA Ops:
  0.6 0.0 copy-start
  0.6 1.1 %copy-done = f32[3,24,8,256]{3,2,1,0:T(8,128)S(1)} copy-done((f32[3,24,8,256]{3,2,1,0:T(8,128)S(1)}, f32[3,24,8,256]{3,2,1,0:T(8,128)}, u32[]{:S(2)}) %copy-start) | copy-done | bytes 589848
  1.7 0.0 copy-start.3
  1.7 0.0 copy-start.1
  1.7 0.1 shard_map.59
  1.8 0.8 %collective-permute-start.1 = (f32[48,256]{1,0:T(8,128)S(1)}, f32[48,256]{1,0:T(8,128)S(1)}, u32[]{:S(2)}, u32[]{:S(2)}) collective-permute-start(f32[48,256]{1,0:T(8,128)S(1)} %get-tuple-element.8), channel_id=1, source_target_pairs={{2,4},{4,2},{6,8},{8,6},{10,12},{12,10},{14,16},{16,14},{18,20},{2... | collective-permute-start | bytes 147464 | tf_op jit(solution)/shard_map/ppermute | solution.py:338
  2.6 5.8 %collective-permute-start.2 = (f32[48,256]{1,0:T(8,128)S(1)}, f32[48,256]{1,0:T(8,128)S(1)}, u32[]{:S(2)}, u32[]{:S(2)}) collective-permute-start(f32[48,256]{1,0:T(8,128)S(1)} %get-tuple-element.10), channel_id=1, source_target_pairs={{0,2},{2,0},{4,6},{6,4},{8,10},{10,8},{12,14},{14,12},{16,18},{18,... | collective-permute-start | bytes 147464 | tf_op jit(solution)/shard_map/ppermute | solution.py:338
  8.3 0.0 collective-permute-start
  8.3 0.0 copy-done.3
  8.3 0.2 shard_map.60.line_ref
  8.6 0.0 collective-permute-done.1.far_ref
  8.6 0.9 %collective-permute-done.side_ref = f32[2,8,256]{2,1,0:T(8,128)S(1)} collective-permute-done((f32[2,8,256]{2,1,0:T(8,128)S(1)}, f32[2,8,256]{2,1,0:T(8,128)S(1)}, u32[]{:S(2)}, u32[]{:S(2)}) %collective-permute-start) | collective-permute-done | bytes 16416 | tf_op jit(solution)/shard_map/ppermute | solution.py:329
  9.5 1.3 %collective-permute-done.2.near_ref = f32[48,256]{1,0:T(8,128)S(1)} collective-permute-done((f32[48,256]{1,0:T(8,128)S(1)}, f32[48,256]{1,0:T(8,128)S(1)}, u32[]{:S(2)}, u32[]{:S(2)}) %collective-permute-start.2) | collective-permute-done | bytes 49184 | tf_op jit(solution)/shard_map/ppermute | solution.py:338
  10.8 0.0 copy-done.1
  10.8 0.1 shard_map.62
  10.9 0.0 copy-start.2
  11.0 0.1 collective-permute-start.3
  11.0 1.0 %shard_map.61.rows_ref = f32[672,256]{1,0:T(8,128)S(1)} custom-call(f32[3,24,8,256]{3,2,1,0:T(8,128)S(1)} %copy-done, f32[24,8,256]{2,1,0:T(8,128)S(1)} %copy-done.1, f32[2,8,256]{2,1,0:T(8,128)S(1)} %collective-permute-done.side_ref, f32[48,256]{1,0:T(8,128)S(1)} %collective-permute-done.1.far_ref, f32[48,256]{1,0:T(8,128)S(1)} %collective-permute-done.2.near_ref, ...), custom_call_target="tpu_custom_call" | custom-call | flops 58982400 | tf_op jit(solution)/shard_map/pallas_call | solution.py:360
  12.0 0.2 collective-permute-done.3.edge_ref
  12.2 0.0 copy-done.2
  12.2 0.5 shard_map.63
  12.7 26.0 %all_to_all.10.in_ref = f32[16,21,4,128]{3,2,1,0:T(4,128)S(1)} all-to-all(f32[16,21,4,128]{3,2,1,0:T(4,128)S(1)} %shard_map.63), channel_id=1, replica_groups=mesh['gz'=16,'gx'=2] {'gz'}, dimensions={0} | all-to-all | bytes 1376256 | tf_op jit(solution)/shard_map/all_to_all | solution.py:378
  38.7 0.5 shard_map.64
  39.2 21.7 %all_to_all.11.in_ref = f32[16,21,4,128]{3,2,1,0:T(4,128)S(1)} all-to-all(f32[16,21,4,128]{3,2,1,0:T(4,128)S(1)} %shard_map.64), channel_id=1, replica_groups=mesh['gz'=16,'gx'=2] {'gz'}, dimensions={0} | all-to-all | bytes 1376256 | tf_op jit(solution)/shard_map/all_to_all | solution.py:386
  60.9 1.2 %shard_map.65 = (f32[3,24,8,256]{3,2,1,0:T(8,128)}, f32[3,24,8,256]{3,2,1,0:T(8,128)}) custom-call(f32[16,21,4,128]{3,2,1,0:T(4,128)S(1)} %all_to_all.11.in_ref), custom_call_target="tpu_custom_call" | custom-call | tf_op jit(solution)/shard_map/pallas_call | solution.py:389
Async XLA Ops:
  0.6 1.1 %copy-start = (f32[3,24,8,256]{3,2,1,0:T(8,128)S(1)}, f32[3,24,8,256]{3,2,1,0:T(8,128)}, u32[]{:S(2)}) copy-start(f32[3,24,8,256]{3,2,1,0:T(8,128)} %b_ref.5) | copy-start | bytes 1769476
  1.7 6.6 %copy-start.3 = (f32[128,128]{1,0:T(8,128)S(1)}, f32[128,128]{1,0:T(8,128)}, u32[]{:S(2)}) copy-start(f32[128,128]{1,0:T(8,128)} %zmix_ref.1) | copy-start | bytes 196612
  1.7 9.1 %copy-start.1 = (f32[24,8,256]{2,1,0:T(8,128)S(1)}, f32[24,8,256]{2,1,0:T(8,128)}, u32[]{:S(2)}) copy-start(f32[24,8,256]{2,1,0:T(8,128)} %r_ref.3) | copy-start | bytes 589828
  1.8 6.8 %collective-permute-start.1 = (f32[48,256]{1,0:T(8,128)S(1)}, f32[48,256]{1,0:T(8,128)S(1)}, u32[]{:S(2)}, u32[]{:S(2)}) collective-permute-start(f32[48,256]{1,0:T(8,128)S(1)} %get-tuple-element.8), channel_id=1, source_target_pairs={{2,4},{4,2},{6,8},{8,6},{10,12},{12,10},{14,16},{16,14},{18,20},{2... | collective-permute-start | bytes 147464 | tf_op jit(solution)/shard_map/ppermute | solution.py:338
  2.6 8.3 %collective-permute-start.2 = (f32[48,256]{1,0:T(8,128)S(1)}, f32[48,256]{1,0:T(8,128)S(1)}, u32[]{:S(2)}, u32[]{:S(2)}) collective-permute-start(f32[48,256]{1,0:T(8,128)S(1)} %get-tuple-element.10), channel_id=1, source_target_pairs={{0,2},{2,0},{4,6},{6,4},{8,10},{10,8},{12,14},{14,12},{16,18},{18,... | collective-permute-start | bytes 147464 | tf_op jit(solution)/shard_map/ppermute | solution.py:338
  8.3 1.2 %collective-permute-start = (f32[2,8,256]{2,1,0:T(8,128)S(1)}, f32[2,8,256]{2,1,0:T(8,128)S(1)}, u32[]{:S(2)}, u32[]{:S(2)}) collective-permute-start(f32[2,8,256]{2,1,0:T(8,128)S(1)} %get-tuple-element.7), channel_id=1, source_target_pairs={{0,1},{1,0},{2,3},{3,2},{4,5},{5,4},{6,7},{7,6},{8,9},{9,8},{10,11... | collective-permute-start | bytes 49160 | tf_op jit(solution)/shard_map/ppermute | solution.py:329
  10.9 1.3 %copy-start.2 = (f32[256,256]{1,0:T(8,128)S(1)}, f32[256,256]{1,0:T(8,128)}, u32[]{:S(2)}) copy-start(f32[256,256]{1,0:T(8,128)} %ymix_ref.1) | copy-start | bytes 786436
  11.0 1.2 %collective-permute-start.3 = (f32[2,8,256]{2,1,0:T(8,128)S(1)}, f32[2,8,256]{2,1,0:T(8,128)S(1)}, u32[]{:S(2)}, u32[]{:S(2)}) collective-permute-start(f32[2,8,256]{2,1,0:T(8,128)S(1)} %shard_map.62), channel_id=1, source_target_pairs={{0,1},{1,0},{2,3},{3,2},{4,5},{5,4},{6,7},{7,6},{8,9},{9,8},{10,11... | collective-permute-start | bytes 49160 | tf_op jit(solution)/shard_map/ppermute | solution.py:329

commit v12 on v11

--- a/solution.py
+++ b/solution.py
@@ -11,8 +11,8 @@
 LANES = 128
 SUBLANES = 8
 SHORT = 4
-PIECES = 2
-BATCH = 11
+PIECES = 1
+BATCH = 22
 VMEM = pl.BlockSpec(memory_space=pltpu.VMEM)
 SMEM = pl.BlockSpec(memory_space=pltpu.SMEM)
 

time: 62.4 us -> 62.2 us (level)
  no operation moved by 1% of the time
where the time goes in v12:
time: 62.2 us; the launch traced here: 62 us
  blocking collectives  47.5 us (76%)
  starting transfers between devices  6.64 us (11%)
  Pallas kernels  3.46 us (6%)
  waiting for transfers between devices  2.63 us (4%)
  local copies, waits for them, and re-layouts  1.07 us (2%)
  between operations  0.71 us (1%)
    all_to_all x1, blocking collectives, kernel_form(): lines = lax.all_to_all(sent, 'gz', split_axis=0, concat_axis=0, tiled=True)  25.8 us
    all_to_all x1, blocking collectives, kernel_form(): lax.all_to_all(product, 'gz', split_axis=0, concat_axis=0, tiled=True)  21.7 us
    ppermute x2, starting transfers between devices, kernel_form(): lax.ppermute(value, 'gz', [pair for i in range(low, parts - 1, 2) for pai...  6.56 us
    ppermute x2, waiting for transfers between devices, kernel_form(): lax.ppermute(value, 'gz', [pair for i in range(low, parts - 1, 2) for pai...  1.32 us
    ppermute x2, waiting for transfers between devices, kernel_form(): swap = lambda value: lax.ppermute(value, 'gx', [(0, 1), (1, 0)])  1.31 us
    pallas_call x1, Pallas kernels, kernel_form(): pl.pallas_call(functools.partial(finish_kernel, total_z ** (-0.5), cells_...  1.26 us
  transfers between devices with their start and end apart: 4, of which 3 were waited for; matrix products, arithmetic and copies ran while one was open for 0% of the time, Pallas kernels for 2%

profile of v12, /device:TPU:0, one launch (start us, length us, event | category | flops | bytes accessed | tf_op | source)
XLA Modules:
  0.0 62.0 jit_solution(1882066362649414302)
XLA Ops:
  0.6 0.0 copy-start
  0.6 1.1 %copy-done = f32[3,24,8,256]{3,2,1,0:T(8,128)S(1)} copy-done((f32[3,24,8,256]{3,2,1,0:T(8,128)S(1)}, f32[3,24,8,256]{3,2,1,0:T(8,128)}, u32[]{:S(2)}) %copy-start) | copy-done | bytes 589848
  1.7 0.0 copy-start.3
  1.7 0.0 copy-start.1
  1.7 0.1 shard_map.59
  1.8 0.8 %collective-permute-start.1 = (f32[48,256]{1,0:T(8,128)S(1)}, f32[48,256]{1,0:T(8,128)S(1)}, u32[]{:S(2)}, u32[]{:S(2)}) collective-permute-start(f32[48,256]{1,0:T(8,128)S(1)} %get-tuple-element.8), channel_id=1, source_target_pairs={{2,4},{4,2},{6,8},{8,6},{10,12},{12,10},{14,16},{16,14},{18,20},{2... | collective-permute-start | bytes 147464 | tf_op jit(solution)/shard_map/ppermute | solution.py:338
  2.6 5.8 %collective-permute-start.2 = (f32[48,256]{1,0:T(8,128)S(1)}, f32[48,256]{1,0:T(8,128)S(1)}, u32[]{:S(2)}, u32[]{:S(2)}) collective-permute-start(f32[48,256]{1,0:T(8,128)S(1)} %get-tuple-element.10), channel_id=1, source_target_pairs={{0,2},{2,0},{4,6},{6,4},{8,10},{10,8},{12,14},{14,12},{16,18},{18,... | collective-permute-start | bytes 147464 | tf_op jit(solution)/shard_map/ppermute | solution.py:338
  8.3 0.0 collective-permute-start
  8.3 0.0 copy-done.3
  8.3 0.2 shard_map.60.line_ref
  8.6 0.0 collective-permute-done.1.far_ref
  8.6 0.9 %collective-permute-done.side_ref = f32[2,8,256]{2,1,0:T(8,128)S(1)} collective-permute-done((f32[2,8,256]{2,1,0:T(8,128)S(1)}, f32[2,8,256]{2,1,0:T(8,128)S(1)}, u32[]{:S(2)}, u32[]{:S(2)}) %collective-permute-start) | collective-permute-done | bytes 16416 | tf_op jit(solution)/shard_map/ppermute | solution.py:329
  9.5 1.3 %collective-permute-done.2.near_ref = f32[48,256]{1,0:T(8,128)S(1)} collective-permute-done((f32[48,256]{1,0:T(8,128)S(1)}, f32[48,256]{1,0:T(8,128)S(1)}, u32[]{:S(2)}, u32[]{:S(2)}) %collective-permute-start.2) | collective-permute-done | bytes 49184 | tf_op jit(solution)/shard_map/ppermute | solution.py:338
  10.8 0.0 copy-done.1
  10.8 0.1 shard_map.62
  10.9 0.0 copy-start.2
  11.0 0.1 collective-permute-start.3
  11.0 0.8 %shard_map.61.rows_ref = f32[672,256]{1,0:T(8,128)S(1)} custom-call(f32[3,24,8,256]{3,2,1,0:T(8,128)S(1)} %copy-done, f32[24,8,256]{2,1,0:T(8,128)S(1)} %copy-done.1, f32[2,8,256]{2,1,0:T(8,128)S(1)} %collective-permute-done.side_ref, f32[48,256]{1,0:T(8,128)S(1)} %collective-permute-done.1.far_ref, f32[48,256]{1,0:T(8,128)S(1)} %collective-permute-done.2.near_ref, ...), custom_call_target="tpu_custom_call" | custom-call | flops 58982400 | tf_op jit(solution)/shard_map/pallas_call | solution.py:360
  11.8 0.4 collective-permute-done.3.edge_ref
  12.2 0.0 copy-done.2
  12.2 0.5 shard_map.63
  12.7 25.8 %all_to_all.10.in_ref = f32[16,21,4,128]{3,2,1,0:T(4,128)S(1)} all-to-all(f32[16,21,4,128]{3,2,1,0:T(4,128)S(1)} %shard_map.63), channel_id=1, replica_groups=mesh['gz'=16,'gx'=2] {'gz'}, dimensions={0} | all-to-all | bytes 1376256 | tf_op jit(solution)/shard_map/all_to_all | solution.py:378
  38.5 0.5 shard_map.64
  39.0 21.7 %all_to_all.11.in_ref = f32[16,21,4,128]{3,2,1,0:T(4,128)S(1)} all-to-all(f32[16,21,4,128]{3,2,1,0:T(4,128)S(1)} %shard_map.64), channel_id=1, replica_groups=mesh['gz'=16,'gx'=2] {'gz'}, dimensions={0} | all-to-all | bytes 1376256 | tf_op jit(solution)/shard_map/all_to_all | solution.py:386
  60.7 1.3 %shard_map.65 = (f32[3,24,8,256]{3,2,1,0:T(8,128)}, f32[3,24,8,256]{3,2,1,0:T(8,128)}) custom-call(f32[16,21,4,128]{3,2,1,0:T(4,128)S(1)} %all_to_all.11.in_ref), custom_call_target="tpu_custom_call" | custom-call | tf_op jit(solution)/shard_map/pallas_call | solution.py:389
Async XLA Ops:
  0.6 1.1 %copy-start = (f32[3,24,8,256]{3,2,1,0:T(8,128)S(1)}, f32[3,24,8,256]{3,2,1,0:T(8,128)}, u32[]{:S(2)}) copy-start(f32[3,24,8,256]{3,2,1,0:T(8,128)} %b_ref.5) | copy-start | bytes 1769476
  1.7 6.6 %copy-start.3 = (f32[128,128]{1,0:T(8,128)S(1)}, f32[128,128]{1,0:T(8,128)}, u32[]{:S(2)}) copy-start(f32[128,128]{1,0:T(8,128)} %zmix_ref.1) | copy-start | bytes 196612
  1.7 9.1 %copy-start.1 = (f32[24,8,256]{2,1,0:T(8,128)S(1)}, f32[24,8,256]{2,1,0:T(8,128)}, u32[]{:S(2)}) copy-start(f32[24,8,256]{2,1,0:T(8,128)} %r_ref.3) | copy-start | bytes 589828
  1.8 6.8 %collective-permute-start.1 = (f32[48,256]{1,0:T(8,128)S(1)}, f32[48,256]{1,0:T(8,128)S(1)}, u32[]{:S(2)}, u32[]{:S(2)}) collective-permute-start(f32[48,256]{1,0:T(8,128)S(1)} %get-tuple-element.8), channel_id=1, source_target_pairs={{2,4},{4,2},{6,8},{8,6},{10,12},{12,10},{14,16},{16,14},{18,20},{2... | collective-permute-start | bytes 147464 | tf_op jit(solution)/shard_map/ppermute | solution.py:338
  2.6 8.3 %collective-permute-start.2 = (f32[48,256]{1,0:T(8,128)S(1)}, f32[48,256]{1,0:T(8,128)S(1)}, u32[]{:S(2)}, u32[]{:S(2)}) collective-permute-start(f32[48,256]{1,0:T(8,128)S(1)} %get-tuple-element.10), channel_id=1, source_target_pairs={{0,2},{2,0},{4,6},{6,4},{8,10},{10,8},{12,14},{14,12},{16,18},{18,... | collective-permute-start | bytes 147464 | tf_op jit(solution)/shard_map/ppermute | solution.py:338
  8.3 1.2 %collective-permute-start = (f32[2,8,256]{2,1,0:T(8,128)S(1)}, f32[2,8,256]{2,1,0:T(8,128)S(1)}, u32[]{:S(2)}, u32[]{:S(2)}) collective-permute-start(f32[2,8,256]{2,1,0:T(8,128)S(1)} %get-tuple-element.7), channel_id=1, source_target_pairs={{0,1},{1,0},{2,3},{3,2},{4,5},{5,4},{6,7},{7,6},{8,9},{9,8},{10,11... | collective-permute-start | bytes 49160 | tf_op jit(solution)/shard_map/ppermute | solution.py:329
  10.9 1.3 %copy-start.2 = (f32[256,256]{1,0:T(8,128)S(1)}, f32[256,256]{1,0:T(8,128)}, u32[]{:S(2)}) copy-start(f32[256,256]{1,0:T(8,128)} %ymix_ref.1) | copy-start | bytes 786436
  11.0 1.2 %collective-permute-start.3 = (f32[2,8,256]{2,1,0:T(8,128)S(1)}, f32[2,8,256]{2,1,0:T(8,128)S(1)}, u32[]{:S(2)}, u32[]{:S(2)}) collective-permute-start(f32[2,8,256]{2,1,0:T(8,128)S(1)} %shard_map.62), channel_id=1, source_target_pairs={{0,1},{1,0},{2,3},{3,2},{4,5},{5,4},{6,7},{7,6},{8,9},{9,8},{10,11... | collective-permute-start | bytes 49160 | tf_op jit(solution)/shard_map/ppermute | solution.py:329

commit v13 on v12

--- a/solution.py
+++ b/solution.py
@@ -215,17 +215,13 @@
     return dot(lhs_high, rhs_high) + (dot(lhs_high, rhs_low) + dot(lhs_low, rhs_high))
 
 
-def mix_kernel(cells_x, cells_z, rows_ref, edge_ref, ymix_ref, place_ref, out_ref, mixed):
+def mix_kernel(cells_x, cells_z, rows_ref, edge_ref, ymix_ref, place_ref, out_ref):
     cells_y = rows_ref.shape[1]
     halves = cells_y // LANES
-    mixed[...] = full_dot(rows_ref[...], ymix_ref[...])
+    mixed = full_dot(rows_ref[...], ymix_ref[...])
     first = (place_ref[0] & 1) == 0
-    factor = jnp.where(first, 0.5 * time_step, -0.5 * time_step)
-    added = full_dot(edge_ref[...].reshape(2 * cells_z, cells_y), ymix_ref[...]) * factor
-    edge = jnp.where(first, cells_x - 1, 0)
-    for c, term in ((1, added[cells_z:]), (2, -added[:cells_z])):
-        at = pl.ds(pl.multiple_of((c * cells_x + edge) * cells_z, cells_z), cells_z)
-        mixed[at, :] = mixed[at, :] + term
+    added = full_dot(edge_ref[...].reshape(2 * cells_z, cells_y), ymix_ref[...]) * (0.5 * time_step)
+    terms = {1: added[cells_z:], 2: -added[:cells_z]}
     pairs = cells_x * halves // out_ref.shape[0]
     extra = 3 * cells_x * cells_z
     for x in range(cells_x):
@@ -235,7 +231,12 @@
             for c in range(3):
                 at = (q * 3 + c) * cells_z
                 line = (c * cells_x + x) * cells_z
-                store_tile(out_ref, part, at, mixed[line : line + cells_z, lanes])
+                tile = mixed[line : line + cells_z, lanes]
+                if c and x == 0:
+                    tile = tile - jnp.where(first, 0.0, terms[c][:, lanes])
+                if c and x == cells_x - 1:
+                    tile = tile + jnp.where(first, terms[c][:, lanes], 0.0)
+                store_tile(out_ref, part, at, tile)
             at = pairs * 3 * cells_z + q * 4
             store_tile(out_ref, part, at, mixed[extra + 4 * x : extra + 4 * x + 4, lanes])
 
@@ -372,7 +373,6 @@
         out_shape=shape(parts, pairs * (3 * cells_z + 4) // SHORT, SHORT, LANES),
         in_specs=[VMEM] * 3 + [SMEM],
         out_specs=VMEM,
-        scratch_shapes=[pltpu.VMEM(rows.shape, f32)],
         compiler_params=limit(6),
     )(rows, swap(edge), ymix, place)
     lines = lax.all_to_all(sent, "gz", split_axis=0, concat_axis=0, tiled=True)

time: 62.2 us -> 62.2 us (level)
  no operation moved by 1% of the time
where the time goes in v13:
time: 62.2 us; the launch traced here: 61.9 us
  blocking collectives  47.4 us (76%)
  starting transfers between devices  6.64 us (11%)
  Pallas kernels  3.44 us (6%)
  waiting for transfers between devices  2.63 us (4%)
  local copies, waits for them, and re-layouts  1.07 us (2%)
  between operations  0.71 us (1%)
    all_to_all x1, blocking collectives, kernel_form(): lines = lax.all_to_all(sent, 'gz', split_axis=0, concat_axis=0, tiled=True)  25.8 us
    all_to_all x1, blocking collectives, kernel_form(): lax.all_to_all(product, 'gz', split_axis=0, concat_axis=0, tiled=True)  21.7 us
    ppermute x2, starting transfers between devices, kernel_form(): lax.ppermute(value, 'gz', [pair for i in range(low, parts - 1, 2) for pai...  6.56 us
    ppermute x2, waiting for transfers between devices, kernel_form(): lax.ppermute(value, 'gz', [pair for i in range(low, parts - 1, 2) for pai...  1.32 us
    ppermute x2, waiting for transfers between devices, kernel_form(): swap = lambda value: lax.ppermute(value, 'gx', [(0, 1), (1, 0)])  1.31 us
    pallas_call x1, Pallas kernels, kernel_form(): pl.pallas_call(functools.partial(finish_kernel, total_z ** (-0.5), cells_...  1.26 us
  transfers between devices with their start and end apart: 4, of which 3 were waited for; matrix products, arithmetic and copies ran while one was open for 0% of the time, Pallas kernels for 2%

profile of v13, /device:TPU:0, one launch (start us, length us, event | category | flops | bytes accessed | tf_op | source)
XLA Modules:
  0.0 61.9 jit_solution(13297991025500747677)
XLA Ops:
  0.6 0.0 copy-start
  0.6 1.1 %copy-done = f32[3,24,8,256]{3,2,1,0:T(8,128)S(1)} copy-done((f32[3,24,8,256]{3,2,1,0:T(8,128)S(1)}, f32[3,24,8,256]{3,2,1,0:T(8,128)}, u32[]{:S(2)}) %copy-start) | copy-done | bytes 589848
  1.7 0.0 copy-start.3
  1.7 0.0 copy-start.1
  1.7 0.1 shard_map.59
  1.8 0.8 %collective-permute-start.1 = (f32[48,256]{1,0:T(8,128)S(1)}, f32[48,256]{1,0:T(8,128)S(1)}, u32[]{:S(2)}, u32[]{:S(2)}) collective-permute-start(f32[48,256]{1,0:T(8,128)S(1)} %get-tuple-element.8), channel_id=1, source_target_pairs={{2,4},{4,2},{6,8},{8,6},{10,12},{12,10},{14,16},{16,14},{18,20},{2... | collective-permute-start | bytes 147464 | tf_op jit(solution)/shard_map/ppermute | solution.py:339
  2.6 5.8 %collective-permute-start.2 = (f32[48,256]{1,0:T(8,128)S(1)}, f32[48,256]{1,0:T(8,128)S(1)}, u32[]{:S(2)}, u32[]{:S(2)}) collective-permute-start(f32[48,256]{1,0:T(8,128)S(1)} %get-tuple-element.10), channel_id=1, source_target_pairs={{0,2},{2,0},{4,6},{6,4},{8,10},{10,8},{12,14},{14,12},{16,18},{18,... | collective-permute-start | bytes 147464 | tf_op jit(solution)/shard_map/ppermute | solution.py:339
  8.3 0.0 collective-permute-start
  8.3 0.0 copy-done.3
  8.3 0.2 shard_map.60.line_ref
  8.6 0.0 collective-permute-done.1.far_ref
  8.6 0.9 %collective-permute-done.side_ref = f32[2,8,256]{2,1,0:T(8,128)S(1)} collective-permute-done((f32[2,8,256]{2,1,0:T(8,128)S(1)}, f32[2,8,256]{2,1,0:T(8,128)S(1)}, u32[]{:S(2)}, u32[]{:S(2)}) %collective-permute-start) | collective-permute-done | bytes 16416 | tf_op jit(solution)/shard_map/ppermute | solution.py:330
  9.5 1.3 %collective-permute-done.2.near_ref = f32[48,256]{1,0:T(8,128)S(1)} collective-permute-done((f32[48,256]{1,0:T(8,128)S(1)}, f32[48,256]{1,0:T(8,128)S(1)}, u32[]{:S(2)}, u32[]{:S(2)}) %collective-permute-start.2) | collective-permute-done | bytes 49184 | tf_op jit(solution)/shard_map/ppermute | solution.py:339
  10.8 0.0 copy-done.1
  10.8 0.1 shard_map.62
  10.9 0.0 copy-start.2
  11.0 0.1 collective-permute-start.3
  11.0 0.8 %shard_map.61.rows_ref = f32[672,256]{1,0:T(8,128)S(1)} custom-call(f32[3,24,8,256]{3,2,1,0:T(8,128)S(1)} %copy-done, f32[24,8,256]{2,1,0:T(8,128)S(1)} %copy-done.1, f32[2,8,256]{2,1,0:T(8,128)S(1)} %collective-permute-done.side_ref, f32[48,256]{1,0:T(8,128)S(1)} %collective-permute-done.1.far_ref, f32[48,256]{1,0:T(8,128)S(1)} %collective-permute-done.2.near_ref, ...), custom_call_target="tpu_custom_call" | custom-call | flops 58982400 | tf_op jit(solution)/shard_map/pallas_call | solution.py:361
  11.8 0.4 collective-permute-done.3.edge_ref
  12.2 0.0 copy-done.2
  12.2 0.5 shard_map.63
  12.7 25.8 %all_to_all.10.in_ref = f32[16,21,4,128]{3,2,1,0:T(4,128)S(1)} all-to-all(f32[16,21,4,128]{3,2,1,0:T(4,128)S(1)} %shard_map.63), channel_id=1, replica_groups=mesh['gz'=16,'gx'=2] {'gz'}, dimensions={0} | all-to-all | bytes 1376256 | tf_op jit(solution)/shard_map/all_to_all | solution.py:378
  38.5 0.5 shard_map.64
  39.0 21.7 %all_to_all.11.in_ref = f32[16,21,4,128]{3,2,1,0:T(4,128)S(1)} all-to-all(f32[16,21,4,128]{3,2,1,0:T(4,128)S(1)} %shard_map.64), channel_id=1, replica_groups=mesh['gz'=16,'gx'=2] {'gz'}, dimensions={0} | all-to-all | bytes 1376256 | tf_op jit(solution)/shard_map/all_to_all | solution.py:386
  60.7 1.3 %shard_map.65 = (f32[3,24,8,256]{3,2,1,0:T(8,128)}, f32[3,24,8,256]{3,2,1,0:T(8,128)}) custom-call(f32[16,21,4,128]{3,2,1,0:T(4,128)S(1)} %all_to_all.11.in_ref), custom_call_target="tpu_custom_call" | custom-call | tf_op jit(solution)/shard_map/pallas_call | solution.py:389
Async XLA Ops:
  0.6 1.1 %copy-start = (f32[3,24,8,256]{3,2,1,0:T(8,128)S(1)}, f32[3,24,8,256]{3,2,1,0:T(8,128)}, u32[]{:S(2)}) copy-start(f32[3,24,8,256]{3,2,1,0:T(8,128)} %b_ref.5) | copy-start | bytes 1769476
  1.7 6.6 %copy-start.3 = (f32[128,128]{1,0:T(8,128)S(1)}, f32[128,128]{1,0:T(8,128)}, u32[]{:S(2)}) copy-start(f32[128,128]{1,0:T(8,128)} %zmix_ref.1) | copy-start | bytes 196612
  1.7 9.1 %copy-start.1 = (f32[24,8,256]{2,1,0:T(8,128)S(1)}, f32[24,8,256]{2,1,0:T(8,128)}, u32[]{:S(2)}) copy-start(f32[24,8,256]{2,1,0:T(8,128)} %r_ref.3) | copy-start | bytes 589828
  1.8 6.8 %collective-permute-start.1 = (f32[48,256]{1,0:T(8,128)S(1)}, f32[48,256]{1,0:T(8,128)S(1)}, u32[]{:S(2)}, u32[]{:S(2)}) collective-permute-start(f32[48,256]{1,0:T(8,128)S(1)} %get-tuple-element.8), channel_id=1, source_target_pairs={{2,4},{4,2},{6,8},{8,6},{10,12},{12,10},{14,16},{16,14},{18,20},{2... | collective-permute-start | bytes 147464 | tf_op jit(solution)/shard_map/ppermute | solution.py:339
  2.6 8.3 %collective-permute-start.2 = (f32[48,256]{1,0:T(8,128)S(1)}, f32[48,256]{1,0:T(8,128)S(1)}, u32[]{:S(2)}, u32[]{:S(2)}) collective-permute-start(f32[48,256]{1,0:T(8,128)S(1)} %get-tuple-element.10), channel_id=1, source_target_pairs={{0,2},{2,0},{4,6},{6,4},{8,10},{10,8},{12,14},{14,12},{16,18},{18,... | collective-permute-start | bytes 147464 | tf_op jit(solution)/shard_map/ppermute | solution.py:339
  8.3 1.2 %collective-permute-start = (f32[2,8,256]{2,1,0:T(8,128)S(1)}, f32[2,8,256]{2,1,0:T(8,128)S(1)}, u32[]{:S(2)}, u32[]{:S(2)}) collective-permute-start(f32[2,8,256]{2,1,0:T(8,128)S(1)} %get-tuple-element.7), channel_id=1, source_target_pairs={{0,1},{1,0},{2,3},{3,2},{4,5},{5,4},{6,7},{7,6},{8,9},{9,8},{10,11... | collective-permute-start | bytes 49160 | tf_op jit(solution)/shard_map/ppermute | solution.py:330
  10.9 1.3 %copy-start.2 = (f32[256,256]{1,0:T(8,128)S(1)}, f32[256,256]{1,0:T(8,128)}, u32[]{:S(2)}) copy-start(f32[256,256]{1,0:T(8,128)} %ymix_ref.1) | copy-start | bytes 786436
  11.0 1.2 %collective-permute-start.3 = (f32[2,8,256]{2,1,0:T(8,128)S(1)}, f32[2,8,256]{2,1,0:T(8,128)S(1)}, u32[]{:S(2)}, u32[]{:S(2)}) collective-permute-start(f32[2,8,256]{2,1,0:T(8,128)S(1)} %shard_map.62), channel_id=1, source_target_pairs={{0,1},{1,0},{2,3},{3,2},{4,5},{5,4},{6,7},{7,6},{8,9},{9,8},{10,11... | collective-permute-start | bytes 49160 | tf_op jit(solution)/shard_map/ppermute | solution.py:330
